TPU v7x, 512 devices: a whole 4x8x8 slice. The times are simulated.
512 devices in a mesh: row: 16 (over y, core), col: 32 (over z, x).
Axes of the slice: x: 4, y: 8, z: 8, core: 2. Of those that a mesh axis runs over, the one named last changes fastest.
Arguments:
- couplings: float32 [24576, 24576], P('row', 'col'), may hold values from -0.0390625 to 0.0390625
- diag_terms: float32 [24576], P('col'), may hold values from 1 to 4
- start_block: float32 [3, 24576], P(None, 'col'), may hold values from -6 to 6
Outputs:
- basis_scaled: float32 [2, 3, 24576], P(None, None, 'col')
- coeffs: float32 [2, 2, 3, 3], replicated
All inputs are finite; a program needn't handle non-finite values.
Results may differ from a plain program's by a relative error of at most 0.0003.
Values sent between devices are 32-bit elements; how exact they have to be, the bound alone decides.
No kernel may reach another device: no remote copies, remote signals or barrier semaphores. Data moves between devices by JAX's collectives and lax.ppermute only.
A program may use at most 64 MiB of HBM per device.

v0:
```python
import jax
import jax.numpy as jnp
from jax import lax
from jax.sharding import PartitionSpec as P

ITERS = 2
M = 24576


def turned_gather(arrays, axis, dims):
    turned = [jnp.moveaxis(a, dim, 0) for a, dim in zip(arrays, dims)]
    both = jnp.concatenate([t.reshape(len(t), -1) for t in turned], axis=1)
    result, at, done = (lax.all_gather(both, axis, axis=0, tiled=True), 0, [])
    for t, dim in zip(turned, dims):
        piece = result[:, at : at + t[0].size].reshape(-1, *t.shape[1:])
        done.append(jnp.moveaxis(piece, 0, dim))
        at += t[0].size
    return tuple(done)


def from_everyone(shard, axis):
    copies = jnp.broadcast_to(shard, (lax.axis_size(axis), *shard.shape))
    return lax.all_to_all(copies, axis, split_axis=0, concat_axis=0, tiled=True)


def over_copies(shard, axis):
    everything = from_everyone(shard, axis)
    return jnp.sum(everything, axis=0)


def in_order(tiles, dim):
    shape = list(tiles.shape[1:])
    shape[dim] *= tiles.shape[0]
    return jnp.moveaxis(tiles, 0, dim).reshape(shape)


def gathered_copies(shard, axis, dim):
    return in_order(from_everyone(shard, axis), dim)


def product(a, b):
    return jnp.dot(a, b, precision=lax.Precision.HIGHEST, preferred_element_type=jnp.float32)


def product_rows(a, matrix):
    return lax.dot_general(
        a,
        matrix,
        (((1,), (1,)), ((), ())),
        precision=lax.Precision.HIGHEST,
        preferred_element_type=jnp.float32,
    )


def shards(couplings, diag_terms, start_block):
    row_index = lax.axis_index("row")
    col_index = lax.axis_index("col")
    width_row = couplings.shape[0]
    width_col = couplings.shape[1]
    root = jnp.sqrt(jnp.float32(M))
    scaled = []
    blocks = []
    start_full, diag_full = turned_gather((start_block, diag_terms), "col", (1, 0))
    first_factor = jnp.linalg.cholesky(product(start_full, start_full.T))
    current = jax.scipy.linalg.solve_triangular(first_factor, start_full, lower=True)
    basis = [current]
    for step in range(ITERS):
        col_piece = lax.dynamic_slice_in_dim(current, col_index * width_col, width_col, 1)
        row_piece = lax.dynamic_slice_in_dim(current, row_index * width_row, width_row, 1)
        forward_rows = over_copies(product_rows(col_piece, couplings), "col")
        backward_cols = over_copies(product(row_piece, couplings), "row")
        forward = lax.all_gather(forward_rows, "row", axis=1, tiled=True)
        backward = gathered_copies(backward_cols, "col", 1)
        image = diag_full[None, :] * current + 0.5 * (forward + backward)
        prior = jnp.concatenate(basis, 0)
        correlation = product(image, prior.T)
        image = image - product(correlation, prior)
        factor = jnp.linalg.cholesky(product(image, image.T))
        current = jax.scipy.linalg.solve_triangular(factor, image, lower=True)
        basis.append(current)
        own_cols = lax.dynamic_slice_in_dim(current, col_index * width_col, width_col, 1)
        scaled.append(own_cols * root)
        blocks.append(jnp.stack([correlation[:, 3 * step : 3 * step + 3], factor]))
    return (jnp.stack(scaled), jnp.stack(blocks))


def solution(mesh):
    placed = (P("row", "col"), P("col"), P(None, "col"))
    return jax.shard_map(
        shards, mesh=mesh, in_specs=placed, out_specs=(P(None, None, "col"), P()), check_vma=False
    )
```

profile of v0, /device:TPU:1, one launch (start us, length us, event | category | flops | bytes accessed | tf_op | source)
XLA Modules:
  0.0 230.9 jit_solution(8561767828042711058)
XLA Ops:
  0.6 0.7 reshape.22
  1.3 0.7 pad_maximum_fusion.4
  2.0 44.4 %all_gather.9 = f32[24576,4]{0,1:T(4,128)S(1)} all-gather(f32[768,4]{0,1:T(4,128)S(1)} %pad_maximum_fusion.4), channel_id=1, replica_groups=mesh['row'=16,'col'=32] {'col'}, dimensions={0}, use_global_device_ids=true | all-gather | bytes 405504 | tf_op jit(solution)/shard_map/all_gather | solution.py:13
  46.5 1.8 fusion.4
  48.3 0.1 copy.32
  48.4 0.3 cholesky.59
  48.7 0.6 compare_reduce_fusion.2
  49.4 0.6 fusion.19
  50.0 0.3 custom-call.7
  50.3 1.0 fusion.1
  51.2 4.6 %fusion.13 = f32[3,768]{1,0:T(4,128)S(1)} fusion(f32[1536,768]{1,0:T(8,128)} %param.6, f32[3,24576]{1,0:T(4,128)S(1)} %fusion.1, s32[]{:T(128)S(6)} %select_n.14), kind=kOutput, calls=%fused_computation.19 | convolution fusion | flops 42467328 | bytes 4752388 | tf_op jit(solution)/shard_map/dot_general | solution.py:42
  55.9 0.7 broadcast_in_dim.19
  56.6 19.9 %all-to-all-start.1 = ((f32[16,3,768]{2,1,0:T(4,128)}), f32[16,3,768]{2,1,0:T(4,128)S(1)}, u32[]{:S(2)}, u32[]{:S(2)}) async-start(f32[16,3,768]{2,1,0:T(4,128)} %broadcast_in_dim.19), calls=%async_computation.1 | async-start | bytes 393216 | tf_op jit(solution)/shard_map/all_to_all | solution.py:23
  76.5 6.2 %fusion.15 = f32[3,1536]{1,0:T(4,128)S(1)} fusion(f32[1536,768]{1,0:T(8,128)} %param.6, f32[3,24576]{1,0:T(4,128)S(1)} %fusion.1, s32[]{:T(128)S(6)} %select_n.7), kind=kOutput, calls=%fused_computation.24 | convolution fusion | flops 42467328 | bytes 4749316 | tf_op jit(solution)/shard_map/dot_general | solution.py:46
  82.7 4.0 %all-to-all-done.1 = f32[16,3,768]{2,1,0:T(4,128)S(1)} async-done(((f32[16,3,768]{2,1,0:T(4,128)}), f32[16,3,768]{2,1,0:T(4,128)S(1)}, u32[]{:S(2)}, u32[]{:S(2)}) %all-to-all-start.1) | async-done | bytes 147488 | tf_op jit(solution)/shard_map/all_to_all | solution.py:23
  86.7 1.0 broadcast_in_dim.18
  87.7 4.9 %all-to-all-start = ((f32[32,3,1536]{2,1,0:T(4,128)}), f32[32,3,1536]{2,1,0:T(4,128)S(1)}, u32[]{:S(2)}, u32[]{:S(2)}) async-start(f32[32,3,1536]{2,1,0:T(4,128)} %broadcast_in_dim.18), calls=%async_computation | async-start | bytes 1572864 | tf_op jit(solution)/shard_map/all_to_all | solution.py:23
  92.7 22.3 %all-to-all-done = f32[32,3,1536]{2,1,0:T(4,128)S(1)} async-done(((f32[32,3,1536]{2,1,0:T(4,128)}), f32[32,3,1536]{2,1,0:T(4,128)S(1)}, u32[]{:S(2)}, u32[]{:S(2)}) %all-to-all-start) | async-done | bytes 589856 | tf_op jit(solution)/shard_map/all_to_all | solution.py:23
  115.0 0.8 broadcast_in_dim.20
  115.8 5.1 %all-to-all-start.2 = ((f32[32,3,768]{2,1,0:T(4,128)}), f32[32,3,768]{2,1,0:T(4,128)S(1)}, u32[]{:S(2)}, u32[]{:S(2)}) async-start(f32[32,3,768]{2,1,0:T(4,128)} %broadcast_in_dim.20), calls=%async_computation.2 | async-start | bytes 786432 | tf_op jit(solution)/shard_map/all_to_all | solution.py:23
  120.9 0.1 slice.20
  121.0 0.1 reduce_sum.36
  121.2 16.9 %all_gather.10 = f32[3,24576]{1,0:T(4,128)S(1)} all-gather(f32[3,1536]{1,0:T(4,128)S(1)} %reduce_sum.36), channel_id=1, replica_groups=mesh['row'=16,'col'=32] {'row'}, dimensions={1}, use_global_device_ids=true | all-gather | bytes 313344 | tf_op jit(solution)/shard_map/all_gather | solution.py:72
  138.1 0.0 all-to-all-done.2
  138.1 1.8 fusion.6
  139.8 0.9 convolution_subtract_fusion
  140.8 1.8 fusion.41
  142.6 0.1 copy.36
  142.7 0.3 cholesky.70
  143.0 0.6 compare_reduce_fusion.1
  143.6 0.6 fusion.31
  144.3 0.3 custom-call.8
  144.6 1.0 fusion.22
  145.5 4.6 %fusion.11 = f32[3,768]{1,0:T(4,128)S(1)} fusion(f32[1536,768]{1,0:T(8,128)} %param.6, f32[3,24576]{1,0:T(4,128)S(1)} %fusion.22, s32[]{:T(128)S(6)} %select_n.14), kind=kOutput, calls=%fused_computation.17 | convolution fusion | flops 42467328 | bytes 4752388 | tf_op jit(solution)/shard_map/dot_general | solution.py:42
  150.2 0.7 broadcast_in_dim.22
  150.9 5.1 %all-to-all-start.4 = ((f32[16,3,768]{2,1,0:T(4,128)}), f32[16,3,768]{2,1,0:T(4,128)S(1)}, u32[]{:S(2)}, u32[]{:S(2)}) async-start(f32[16,3,768]{2,1,0:T(4,128)} %broadcast_in_dim.22), calls=%async_computation.4 | async-start | bytes 393216 | tf_op jit(solution)/shard_map/all_to_all | solution.py:23
  155.9 6.2 %fusion.17 = f32[3,1536]{1,0:T(4,128)S(1)} fusion(f32[1536,768]{1,0:T(8,128)} %param.6, f32[3,24576]{1,0:T(4,128)S(1)} %fusion.22, s32[]{:T(128)S(6)} %select_n.7), kind=kOutput, calls=%fused_computation.26 | convolution fusion | flops 42467328 | bytes 4749316 | tf_op jit(solution)/shard_map/dot_general | solution.py:46
  162.1 4.0 %all-to-all-done.4 = f32[16,3,768]{2,1,0:T(4,128)S(1)} async-done(((f32[16,3,768]{2,1,0:T(4,128)}), f32[16,3,768]{2,1,0:T(4,128)S(1)}, u32[]{:S(2)}, u32[]{:S(2)}) %all-to-all-start.4) | async-done | bytes 147488 | tf_op jit(solution)/shard_map/all_to_all | solution.py:23
  166.1 1.0 broadcast_in_dim.21
  167.1 9.5 %all-to-all-start.3 = ((f32[32,3,1536]{2,1,0:T(4,128)}), f32[32,3,1536]{2,1,0:T(4,128)S(1)}, u32[]{:S(2)}, u32[]{:S(2)}) async-start(f32[32,3,1536]{2,1,0:T(4,128)} %broadcast_in_dim.21), calls=%async_computation.3 | async-start | bytes 1572864 | tf_op jit(solution)/shard_map/all_to_all | solution.py:23
  176.7 22.3 %all-to-all-done.3 = f32[32,3,1536]{2,1,0:T(4,128)S(1)} async-done(((f32[32,3,1536]{2,1,0:T(4,128)}), f32[32,3,1536]{2,1,0:T(4,128)S(1)}, u32[]{:S(2)}, u32[]{:S(2)}) %all-to-all-start.3) | async-done | bytes 589856 | tf_op jit(solution)/shard_map/all_to_all | solution.py:23
  199.0 0.8 broadcast_in_dim.23
  199.8 5.1 %all-to-all-start.5 = ((f32[32,3,768]{2,1,0:T(4,128)}), f32[32,3,768]{2,1,0:T(4,128)S(1)}, u32[]{:S(2)}, u32[]{:S(2)}) async-start(f32[32,3,768]{2,1,0:T(4,128)} %broadcast_in_dim.23), calls=%async_computation.5 | async-start | bytes 786432 | tf_op jit(solution)/shard_map/all_to_all | solution.py:23
  205.0 0.1 reduce_sum.38
  205.1 16.9 %all_gather.11 = f32[3,24576]{1,0:T(4,128)S(1)} all-gather(f32[3,1536]{1,0:T(4,128)S(1)} %reduce_sum.38), channel_id=1, replica_groups=mesh['row'=16,'col'=32] {'row'}, dimensions={1}, use_global_device_ids=true | all-gather | bytes 313344 | tf_op jit(solution)/shard_map/all_gather | solution.py:72
  222.0 0.0 all-to-all-done.5
  222.0 1.8 fusion
  223.8 1.0 convolution_subtract_fusion.1
  224.8 1.8 fusion.42
  226.6 0.1 copy.40
  226.7 0.3 cholesky.81
  227.0 0.6 compare_reduce_fusion
  227.7 0.7 fusion.32
  228.4 0.3 custom-call.9
  228.7 1.0 fusion.20
  229.7 0.6 copy.44
  230.3 0.6 pad_maximum_fusion.5
  (15 shorter events, 0.3 us)
Async XLA Ops:
  56.6 30.1 %all-to-all-start.1 = ((f32[16,3,768]{2,1,0:T(4,128)}), f32[16,3,768]{2,1,0:T(4,128)S(1)}, u32[]{:S(2)}, u32[]{:S(2)}) async-start(f32[16,3,768]{2,1,0:T(4,128)} %broadcast_in_dim.19), calls=%async_computation.1 | async-start | bytes 393216 | tf_op jit(solution)/shard_map/all_to_all | solution.py:23
  87.7 27.3 %all-to-all-start = ((f32[32,3,1536]{2,1,0:T(4,128)}), f32[32,3,1536]{2,1,0:T(4,128)S(1)}, u32[]{:S(2)}, u32[]{:S(2)}) async-start(f32[32,3,1536]{2,1,0:T(4,128)} %broadcast_in_dim.18), calls=%async_computation | async-start | bytes 1572864 | tf_op jit(solution)/shard_map/all_to_all | solution.py:23
  115.8 22.3 %all-to-all-start.2 = ((f32[32,3,768]{2,1,0:T(4,128)}), f32[32,3,768]{2,1,0:T(4,128)S(1)}, u32[]{:S(2)}, u32[]{:S(2)}) async-start(f32[32,3,768]{2,1,0:T(4,128)} %broadcast_in_dim.20), calls=%async_computation.2 | async-start | bytes 786432 | tf_op jit(solution)/shard_map/all_to_all | solution.py:23
  150.9 15.3 %all-to-all-start.4 = ((f32[16,3,768]{2,1,0:T(4,128)}), f32[16,3,768]{2,1,0:T(4,128)S(1)}, u32[]{:S(2)}, u32[]{:S(2)}) async-start(f32[16,3,768]{2,1,0:T(4,128)} %broadcast_in_dim.22), calls=%async_computation.4 | async-start | bytes 393216 | tf_op jit(solution)/shard_map/all_to_all | solution.py:23
  167.1 31.9 %all-to-all-start.3 = ((f32[32,3,1536]{2,1,0:T(4,128)}), f32[32,3,1536]{2,1,0:T(4,128)S(1)}, u32[]{:S(2)}, u32[]{:S(2)}) async-start(f32[32,3,1536]{2,1,0:T(4,128)} %broadcast_in_dim.21), calls=%async_computation.3 | async-start | bytes 1572864 | tf_op jit(solution)/shard_map/all_to_all | solution.py:23
  199.8 22.2 %all-to-all-start.5 = ((f32[32,3,768]{2,1,0:T(4,128)}), f32[32,3,768]{2,1,0:T(4,128)S(1)}, u32[]{:S(2)}, u32[]{:S(2)}) async-start(f32[32,3,768]{2,1,0:T(4,128)} %broadcast_in_dim.23), calls=%async_computation.5 | async-start | bytes 786432 | tf_op jit(solution)/shard_map/all_to_all | solution.py:23
where the time goes:
time: 232 us; the launch traced here: 231 us
  blocking collectives  78.2 us (34%)
  waiting for transfers between devices  52.7 us (23%)
  starting transfers between devices  49.7 us (21%)
  matrix products  35.4 us (15%)
  other arithmetic  7.44 us (3%)
  local copies, waits for them, and re-layouts  6.66 us (3%)
    all_to_all x6, waiting for transfers between devices, from_everyone(): return lax.all_to_all(copies, axis, split_axis=0, concat_axis=0, tiled=True)  52.7 us
    all_to_all x6, starting transfers between devices, from_everyone(): return lax.all_to_all(copies, axis, split_axis=0, concat_axis=0, tiled=True)  49.7 us
    all_gather x1, blocking collectives, turned_gather(): result, at, done = (lax.all_gather(both, axis, axis=0, tiled=True), 0, [])  44.4 us
    all_gather x2, blocking collectives, shards(): forward = lax.all_gather(forward_rows, 'row', axis=1, tiled=True)  33.8 us
    dot_general x9, matrix products, product(): jnp.dot(a, b, precision=lax.Precision.HIGHEST, preferred_element_type=jnp...  20.2 us
    dot_general x2, matrix products, product_rows(): lax.dot_general(a, matrix, (((1,), (1,)), ((), ())), precision=lax.Precis...  12.4 us
    broadcast_in_dim x6, local copies, waits for them, and re-layouts, from_everyone(): copies = jnp.broadcast_to(shard, (lax.axis_size(axis), *shard.shape))  4.95 us
  transfers between devices with their start and end apart: 6, of which 4 were waited for; matrix products, arithmetic and copies ran while one was open for 6% of the time, Pallas kernels for 0%

commit v1 on v0

v1 whole, which is shorter than its diff:
```python
import jax
import jax.numpy as jnp
from jax import lax
from jax.sharding import PartitionSpec as P

M = 24576
SHIFT = 2.0


def product(a, b):
    return jnp.dot(a, b, precision=lax.Precision.HIGHEST, preferred_element_type=jnp.float32)


def product_rows(a, matrix):
    return lax.dot_general(
        a,
        matrix,
        (((1,), (1,)), ((), ())),
        precision=lax.Precision.HIGHEST,
        preferred_element_type=jnp.float32,
    )


def shards(couplings, diag_terms, start_block):
    row_index = lax.axis_index("row")
    width = couplings.shape[1]
    flat = 3 * width
    cols = lax.axis_size("col")
    rows = lax.axis_size("row")
    shifted = diag_terms - SHIFT

    def exchange(block, extra):
        halves = jnp.moveaxis(product_rows(block, couplings).reshape(3, 2, width), 1, 0).reshape(2, flat)
        slot = lax.broadcasted_iota(jnp.int32, (cols, 1), 0)
        aimed = jnp.where(slot // 2 == row_index, jnp.tile(halves, (cols // 2, 1)), 0.0)
        parts = [jnp.broadcast_to(block.reshape(1, flat), (cols, flat)), aimed]
        if extra is not None:
            padded = jnp.pad(extra, (0, 128 - extra.shape[0]))
            parts.append(jnp.broadcast_to(padded[None], (cols, 128)))
        sent = jnp.concatenate(parts, 1)[:, None, :]
        got = lax.all_to_all(sent, "col", 0, 0, tiled=True)[:, 0, :]
        mine = lax.dynamic_slice(got, (2 * row_index, 0), (2, flat)).reshape(2, 3, width)
        tail = jnp.sum(got[:, flat:], axis=0)
        return jnp.moveaxis(mine, 0, 1).reshape(3, 2 * width), tail

    def collect(block, own_rows, forward):
        part = 0.5 * (product(own_rows, couplings) + forward)
        sent = jnp.broadcast_to(part.reshape(1, 1, flat), (rows, 1, flat))
        got = lax.all_to_all(sent, "row", 0, 0, tiled=True)
        return jnp.sum(got, axis=0).reshape(3, width) + shifted[None] * block

    def inverse(lower):
        return jax.scipy.linalg.solve_triangular(lower, jnp.eye(3, dtype=jnp.float32), lower=True)

    own_rows, tail = exchange(start_block, None)
    z1 = collect(start_block, own_rows, tail.reshape(3, width))
    both = jnp.concatenate([start_block, z1], 0)
    gram = product(both, both.T)
    own_rows, tail = exchange(z1, gram.reshape(-1))
    gram = tail[flat : flat + 36].reshape(6, 6)
    n0 = inverse(jnp.linalg.cholesky(gram[:3, :3]))
    c0 = product(product(n0, gram[:3, 3:]), n0.T)
    c0 = product(n0, product(n0, gram[3:, :3]).T).T
    h1 = product(product(n0, gram[3:, 3:]), n0.T) - product(c0, c0.T)
    l1 = jnp.linalg.cholesky(0.5 * (h1 + h1.T))
    n1 = inverse(l1)
    y2 = collect(z1, own_rows, tail[:flat].reshape(3, width))
    q0 = product(n0, start_block)
    u = product(n0, z1)
    q1 = product(n1, u - product(c0, q0))
    w = product(n1, product(n0, y2) - product(c0, u))
    w = w - product(l1.T, q0) - product(c0, q1)
    three = jnp.concatenate([q0, q1, w], 0)
    last = product(w, three.T)
    sent = jnp.broadcast_to(jnp.pad(last.reshape(-1), (0, 101))[None, None], (cols, 1, 128))
    last = jnp.sum(lax.all_to_all(sent, "col", 0, 0, tiled=True), axis=(0, 1))[:27].reshape(3, 9)
    d0, d1, h2 = last[:, :3], last[:, 3:6], last[:, 6:]
    h2 = h2 - product(d0, d0.T) - product(d1, d1.T)
    l2 = jnp.linalg.cholesky(0.5 * (h2 + h2.T))
    q2 = product(inverse(l2), w - product(d0, q0) - product(d1, q1))
    root = jnp.sqrt(jnp.float32(M))
    shift = SHIFT * jnp.eye(3, dtype=jnp.float32)
    coeffs = jnp.stack([jnp.stack([c0 + shift, l1]), jnp.stack([c0 + d1 + shift, l2])])
    return jnp.stack([q1, q2]) * root, coeffs


def solution(mesh):
    placed = (P("row", "col"), P("col"), P(None, "col"))
    return jax.shard_map(
        shards, mesh=mesh, in_specs=placed, out_specs=(P(None, None, "col"), P()), check_vma=False
    )
```

time: 232 us -> 142 us (0.61)
  blocking collectives: 78.2 us -> 36.6 us
  starting transfers between devices: 49.7 us -> 27.6 us
  waiting for transfers between devices: 52.7 us -> 35.7 us
  matrix products: 35.4 us -> 26.7 us
    all_gather x3 -> x0, blocking collectives: 78.2 us -> none  [the longest x1 44.4 us: turned_gather(): result, at, done = (lax.all_gather(both, axis, axis=0, tiled=True), 0, [])]
    all_to_all x0 -> x2, blocking collectives: none -> 36.6 us  [the longest x1 23.2 us: exchange(): got = lax.all_to_all(sent, 'col', 0, 0, tiled=True)[:, 0, :]]
    all_to_all x6 -> x3, starting transfers between devices: 49.7 us -> 27.6 us  [the longest x2 13.9 us: collect(): got = lax.all_to_all(sent, 'row', 0, 0, tiled=True)]
    all_to_all x6 -> x3, waiting for transfers between devices: 52.7 us -> 35.7 us  [the longest x2 18.1 us: collect(): got = lax.all_to_all(sent, 'row', 0, 0, tiled=True)]
    dot_general x9 -> x23, matrix products: 20.2 us -> 13.7 us  [product(): jnp.dot(a, b, precision=lax.Precision.HIGHEST, preferred_element_type=jnp...]
    broadcast_in_dim x6 -> x9, local copies, waits for them, and re-layouts: 4.95 us -> 4.11 us  [the longest x2 1.84 us: exchange(): sent = jnp.concatenate(parts, 1)[:, None, :]]
    another operation x21 -> x18, other arithmetic: 6.34 us -> 6.2 us  [the longest x4 1.44 us: inverse(): jax.scipy.linalg.solve_triangular(lower, jnp.eye(3, dtype=jnp.float32), l...]
  transfers between devices with their start and end apart: 6 -> 3, of which waited for: 4 -> 3; matrix products, arithmetic and copies ran while one was open for 6% -> 0% of each run, Pallas kernels for 0% -> 0%
where the time goes in v1:
time: 142 us; the launch traced here: 141 us
  blocking collectives  36.6 us (26%)
  waiting for transfers between devices  35.7 us (25%)
  starting transfers between devices  27.6 us (19%)
  matrix products  26.7 us (19%)
  local copies, waits for them, and re-layouts  6.89 us (5%)
  other arithmetic  6.83 us (5%)
    all_to_all x1, blocking collectives, exchange(): got = lax.all_to_all(sent, 'col', 0, 0, tiled=True)[:, 0, :]  23.2 us
    all_to_all x2, waiting for transfers between devices, collect(): got = lax.all_to_all(sent, 'row', 0, 0, tiled=True)  18.1 us
    all_to_all x1, waiting for transfers between devices, exchange(): got = lax.all_to_all(sent, 'col', 0, 0, tiled=True)[:, 0, :]  17.6 us
    all_to_all x2, starting transfers between devices, collect(): got = lax.all_to_all(sent, 'row', 0, 0, tiled=True)  13.9 us
    all_to_all x1, starting transfers between devices, exchange(): got = lax.all_to_all(sent, 'col', 0, 0, tiled=True)[:, 0, :]  13.7 us
    dot_general x23, matrix products, product(): jnp.dot(a, b, precision=lax.Precision.HIGHEST, preferred_element_type=jnp...  13.7 us
    all_to_all x1, blocking collectives, shards(): lax.all_to_all(sent, 'col', 0, 0, tiled=True)  13.4 us
    dot_general x2, matrix products, product_rows(): lax.dot_general(a, matrix, (((1,), (1,)), ((), ())), precision=lax.Precis...  12.4 us
  transfers between devices with their start and end apart: 3, of which 3 were waited for; matrix products, arithmetic and copies ran while one was open for 0% of the time, Pallas kernels for 0%

profile of v1, /device:TPU:1, one launch (start us, length us, event | category | flops | bytes accessed | tf_op | source)
XLA Modules:
  0.0 141.4 jit_solution(4378207847548916984)
XLA Ops:
  0.6 0.7 reshape.142
  1.4 6.2 %fusion.50 = f32[3,1536]{1,0:T(4,128)S(1)} fusion(f32[3,768]{1,0:T(4,128)} %param.8, f32[1536,768]{1,0:T(8,128)} %param.6), kind=kOutput, calls=%fused_computation.105 | convolution fusion | flops 42467328 | bytes 4746240 | tf_op jit(solution)/shard_map/dot_general | solution.py:15
  7.7 0.2 tile.22
  8.1 1.2 broadcast_in_dim.68
  9.3 13.7 %all-to-all-start = ((f32[32,1,4608]{2,1,0:T(1,128)}), f32[32,1,4608]{2,1,0:T(1,128)S(1)}, u32[]{:S(2)}, u32[]{:S(2)}) async-start(f32[32,1,4608]{2,1,0:T(1,128)} %broadcast_in_dim.68), calls=%async_computation | async-start | bytes 1179648 | tf_op jit(solution)/shard_map/all_to_all | solution.py:41
  23.0 17.6 %all-to-all-done = f32[32,1,4608]{2,1,0:T(1,128)S(1)} async-done(((f32[32,1,4608]{2,1,0:T(1,128)}), f32[32,1,4608]{2,1,0:T(1,128)S(1)}, u32[]{:S(2)}, u32[]{:S(2)}) %all-to-all-start) | async-done | bytes 589856 | tf_op jit(solution)/shard_map/all_to_all | solution.py:41
  40.8 4.6 %fusion.1 = f32[3,768]{1,0:T(4,128)S(1)} fusion(f32[3,768]{1,0:T(4,128)S(1)} %reshape.129, f32[3,1536]{1,0:T(4,128)S(1)} %bitcast.119, f32[1536,768]{1,0:T(8,128)} %param.6), kind=kOutput, calls=%fused_computation.10 | convolution fusion | flops 42471936 | bytes 4755456 | tf_op jit(solution)/shard_map/dot_general | solution.py:11
  45.5 0.7 broadcast_in_dim.70
  46.2 9.5 %all-to-all-start.1 = ((f32[16,1,2304]{2,1,0:T(1,128)}), f32[16,1,2304]{2,1,0:T(1,128)S(1)}, u32[]{:S(2)}, u32[]{:S(2)}) async-start(f32[16,1,2304]{2,1,0:T(1,128)} %broadcast_in_dim.70), calls=%async_computation.1 | async-start | bytes 294912 | tf_op jit(solution)/shard_map/all_to_all | solution.py:49
  55.7 9.2 %all-to-all-done.1 = f32[16,1,2304]{2,1,0:T(1,128)S(1)} async-done(((f32[16,1,2304]{2,1,0:T(1,128)}), f32[16,1,2304]{2,1,0:T(1,128)S(1)}, u32[]{:S(2)}, u32[]{:S(2)}) %all-to-all-start.1) | async-done | bytes 147488 | tf_op jit(solution)/shard_map/all_to_all | solution.py:49
  64.9 0.1 reduce_sum.46
  65.0 6.2 %fusion.51 = f32[3,1536]{1,0:T(4,128)S(1)} fusion(f32[3,768]{1,0:T(4,128)S(1)} %multiply_add_fusion, f32[1536,768]{1,0:T(8,128)} %param.6), kind=kOutput, calls=%fused_computation.106 | convolution fusion | flops 42467328 | bytes 4746240 | tf_op jit(solution)/shard_map/dot_general | solution.py:15
  71.3 0.1 fusion.8
  71.6 0.2 tile.25
  72.0 0.6 copy.68
  72.6 23.2 %all_to_all.25 = f32[32,1,4736]{2,1,0:T(1,128)S(1)} all-to-all(f32[32,1,4736]{2,1,0:T(1,128)S(1)} %copy.68), channel_id=1, replica_groups=mesh['row'=16,'col'=32] {'col'}, dimensions={0} | all-to-all | bytes 1212416 | tf_op jit(solution)/shard_map/all_to_all | solution.py:41
  96.0 0.1 copy.90
  96.2 0.3 cholesky.59
  96.5 0.6 compare_reduce_fusion.2
  97.1 0.6 fusion.22
  97.8 0.3 custom-call.7
  98.0 0.2 fusion.20
  98.2 0.2 fusion.54
  98.4 0.2 fusion.55
  98.6 0.1 fusion.34
  98.7 0.2 fusion.36
  98.9 0.1 fusion.53
  99.0 0.1 fusion.52
  99.2 0.2 convolution_subtract_fusion.8
  99.4 0.1 copy.72
  99.5 0.1 copy.73
  99.6 0.3 cholesky.70
  99.9 0.6 compare_reduce_fusion.1
  100.5 0.6 fusion.42
  101.2 0.3 custom-call.8
  101.6 4.6 %fusion = f32[3,768]{1,0:T(4,128)S(1)} fusion(f32[3,768]{1,0:T(4,128)S(1)} %reshape.136, f32[3,1536]{1,0:T(4,128)S(1)} %bitcast.120, f32[1536,768]{1,0:T(8,128)} %param.6), kind=kOutput, calls=%fused_computation.7 | convolution fusion | flops 42471936 | bytes 4755456 | tf_op jit(solution)/shard_map/dot_general | solution.py:11
  106.2 0.7 broadcast_in_dim.76
  107.0 4.4 %all-to-all-start.3 = ((f32[16,1,2304]{2,1,0:T(1,128)}), f32[16,1,2304]{2,1,0:T(1,128)S(1)}, u32[]{:S(2)}, u32[]{:S(2)}) async-start(f32[16,1,2304]{2,1,0:T(1,128)} %broadcast_in_dim.76), calls=%async_computation.3 | async-start | bytes 294912 | tf_op jit(solution)/shard_map/all_to_all | solution.py:49
  111.4 0.2 convolution_subtract_fusion.5
  111.6 0.2 fusion.18
  111.8 0.2 fusion.56
  112.0 8.9 %all-to-all-done.3 = f32[16,1,2304]{2,1,0:T(1,128)S(1)} async-done(((f32[16,1,2304]{2,1,0:T(1,128)}), f32[16,1,2304]{2,1,0:T(1,128)S(1)}, u32[]{:S(2)}, u32[]{:S(2)}) %all-to-all-start.3) | async-done | bytes 147488 | tf_op jit(solution)/shard_map/all_to_all | solution.py:49
  120.9 0.1 reduce_sum.48
  121.0 0.2 fusion.12
  121.2 0.2 convolution_subtract_fusion.4
  121.5 0.2 fusion.57
  121.6 0.9 convolution_subtract_fusion.3
  122.5 0.2 convolution_subtract_fusion.2
  122.7 0.1 fusion.2
  123.0 13.4 %all_to_all.26 = f32[32,1,128]{2,1,0:T(1,128)S(1)} all-to-all(f32[32,1,128]{2,1,0:T(1,128)S(1)} %broadcast_in_dim.77), channel_id=1, replica_groups=mesh['row'=16,'col'=32] {'col'}, dimensions={0} | all-to-all | bytes 32768 | tf_op jit(solution)/shard_map/all_to_all | solution.py:76
  136.7 0.2 convolution_subtract_fusion.1
  137.0 0.1 copy.81
  137.2 0.2 convolution_subtract_fusion.6
  137.4 0.1 copy.78
  137.5 0.1 copy.79
  137.6 0.3 cholesky.81
  137.9 0.6 compare_reduce_fusion
  138.6 0.6 fusion.40
  139.2 0.2 convolution_subtract_fusion
  139.5 0.3 custom-call.9
  139.7 0.2 fusion.16
  139.9 0.2 convolution_bitcast_fusion
  140.1 0.6 copy.85
  140.8 0.6 pad_maximum_fusion.1
  (59 shorter events, 1.9 us)
Async XLA Ops:
  8.1 47.6 %copy-start.1 = (f32[768]{0:T(1024)S(1)}, f32[768]{0:T(1024)}, u32[]{:S(2)}) copy-start(f32[768]{0:T(1024)} %param.7) | copy-start | bytes 9220
  8.1 56.9 %copy-start = (f32[3,768]{1,0:T(4,128)S(1)}, f32[3,768]{1,0:T(4,128)}, u32[]{:S(2)}) copy-start(f32[3,768]{1,0:T(4,128)} %param.8) | copy-start | bytes 27652
  9.3 31.3 %all-to-all-start = ((f32[32,1,4608]{2,1,0:T(1,128)}), f32[32,1,4608]{2,1,0:T(1,128)S(1)}, u32[]{:S(2)}, u32[]{:S(2)}) async-start(f32[32,1,4608]{2,1,0:T(1,128)} %broadcast_in_dim.68), calls=%async_computation | async-start | bytes 1179648 | tf_op jit(solution)/shard_map/all_to_all | solution.py:41
  46.2 18.7 %all-to-all-start.1 = ((f32[16,1,2304]{2,1,0:T(1,128)}), f32[16,1,2304]{2,1,0:T(1,128)S(1)}, u32[]{:S(2)}, u32[]{:S(2)}) async-start(f32[16,1,2304]{2,1,0:T(1,128)} %broadcast_in_dim.70), calls=%async_computation.1 | async-start | bytes 294912 | tf_op jit(solution)/shard_map/all_to_all | solution.py:49
  107.0 14.0 %all-to-all-start.3 = ((f32[16,1,2304]{2,1,0:T(1,128)}), f32[16,1,2304]{2,1,0:T(1,128)S(1)}, u32[]{:S(2)}, u32[]{:S(2)}) async-start(f32[16,1,2304]{2,1,0:T(1,128)} %broadcast_in_dim.76), calls=%async_computation.3 | async-start | bytes 294912 | tf_op jit(solution)/shard_map/all_to_all | solution.py:49

commit v2 on v0

v2 whole, which is shorter than its diff:
```python
import jax
import jax.numpy as jnp
from jax import lax
from jax.experimental import pallas as pl
from jax.experimental.pallas import tpu as pltpu
from jax.sharding import PartitionSpec as P

M = 24576
SHIFT = 2.5
W = 768
FLAT = 3 * W
CHUNK = 256
F32 = jnp.float32
BF16 = jnp.bfloat16
VMEM = pl.BlockSpec(memory_space=pltpu.VMEM)


def in_vmem(shape, dtype=F32):
    return pltpu.VMEM(shape, dtype)


def three_parts(x):
    first = x.astype(BF16).astype(F32)
    rest = x - first
    second = rest.astype(BF16).astype(F32)
    return jnp.concatenate([first, second, rest - second], 0).astype(BF16)


def folded(wide):
    return wide[0:8] + wide[8:16] + wide[16:24]


def over_rows(parts, matrix):
    return lax.dot_general(parts, matrix, (((1,), (1,)), ((), ())), preferred_element_type=F32)


def over_cols(parts, matrix):
    return lax.dot_general(parts, matrix, (((1,), (0,)), ((), ())), preferred_element_type=F32)


def rows_of(flat):
    return [flat[:, k * W : (k + 1) * W] for k in range(3)]


def inner(a, b):
    return jnp.sum(a * b, axis=1, keepdims=True)


def packed(values):
    lane = lax.broadcasted_iota(jnp.int32, (1, 128), 1)
    tile = jnp.zeros((1, 128), F32)
    for at, value in enumerate(values):
        tile = jnp.where(lane == at, value, tile)
    return tile


def unpacked(tile, count):
    lane = lax.broadcasted_iota(jnp.int32, (1, 128), 1)
    return [jnp.sum(jnp.where(lane == at, tile, 0.0), axis=1, keepdims=True) for at in range(count)]


def symmetric(six):
    a, b, c, d, e, f = six
    return [[a, b, c], [b, d, e], [c, e, f]]


def times(a, b):
    return [[sum(a[i][k] * b[k][j] for k in range(3)) for j in range(3)] for i in range(3)]


def turned(a):
    return [[a[j][i] for j in range(3)] for i in range(3)]


def minus(a, b):
    return [[a[i][j] - b[i][j] for j in range(3)] for i in range(3)]


def cholesky(h):
    zero = jnp.zeros_like(h[0][0])
    a = jnp.sqrt(h[0][0])
    b = h[1][0] / a
    c = h[2][0] / a
    d = jnp.sqrt(h[1][1] - b * b)
    e = (h[2][1] - c * b) / d
    f = jnp.sqrt(h[2][2] - c * c - e * e)
    return [[a, zero, zero], [b, d, zero], [c, e, f]]


def inverse(low):
    zero = jnp.zeros_like(low[0][0])
    a, d, f = 1.0 / low[0][0], 1.0 / low[1][1], 1.0 / low[2][2]
    b = -low[1][0] * a * d
    e = -low[2][1] * d * f
    c = -(low[2][0] * a + low[2][1] * b) * f
    return [[a, zero, zero], [b, d, zero], [c, e, f]]


def combine(matrix, vectors):
    return [sum(matrix[i][k] * vectors[k] for k in range(3)) for i in range(3)]


def place(row_index, forward_ref, sent_ref):
    for half in range(2):
        for k in range(3):
            sent_ref[2 * row_index + half, :, k * W : (k + 1) * W] = forward_ref[k : k + 1, half * W : (half + 1) * W]


def first_kernel(x_ref, a_ref, sent_ref, high_ref, low_ref, whole, x_rows, forward, sems):
    row_index = lax.axis_index("row")
    pieces = [pl.ds(i * CHUNK, CHUNK) for i in range(2 * W // CHUNK)]
    copies = [pltpu.make_async_copy(a_ref.at[piece], whole.at[piece], sems.at[i]) for i, piece in enumerate(pieces)]
    for copy in copies:
        copy.start()
    x = x_ref[...]
    x_rows[...] = jnp.zeros_like(x_rows)
    for k, row in enumerate(rows_of(x)):
        x_rows[k : k + 1, :] = row
    for p in range(sent_ref.shape[0]):
        sent_ref[p] = x
    parts = three_parts(x_rows[...])
    for copy, piece in zip(copies, pieces):
        copy.wait()
        block = whole[piece, :]
        high = block.astype(BF16)
        low = (block - high.astype(F32)).astype(BF16)
        high_ref[piece, :] = high
        low_ref[piece, :] = low
        forward[:, piece] = 0.5 * folded(over_rows(parts, high) + over_rows(parts, low))
    place(row_index, forward, sent_ref)


def forward_kernel(z_ref, x_ref, high_ref, low_ref, sent_ref, z_rows, forward):
    row_index = lax.axis_index("row")
    z = z_ref[...]
    z_rows[...] = jnp.zeros_like(z_rows)
    for k, row in enumerate(rows_of(z)):
        z_rows[k : k + 1, :] = row
    parts = three_parts(z_rows[...])
    six = rows_of(x_ref[...]) + rows_of(z)
    tile = packed([inner(six[i], six[j]) for i in range(6) for j in range(i, 6)])
    for p in range(sent_ref.shape[0]):
        sent_ref[p, :, 0:FLAT] = z
        sent_ref[p, :, FLAT:] = tile
    forward[...] = 0.5 * folded(over_rows(parts, high_ref[...]) + over_rows(parts, low_ref[...]))
    place(row_index, forward, sent_ref)


def backward_kernel(got_ref, own_ref, cross_ref, high_ref, low_ref, sent_ref, v_rows):
    row_index = lax.axis_index("row")
    col_index = lax.axis_index("col")
    home = col_index // 2 == row_index
    v_rows[...] = jnp.zeros_like(v_rows)
    for half in range(2):
        mine = jnp.where(col_index % 2 == half, own_ref[...], cross_ref[...])
        block = jnp.where(home, mine, got_ref[2 * row_index + half, :, 0:FLAT])
        for k, row in enumerate(rows_of(block)):
            v_rows[k : k + 1, half * W : (half + 1) * W] = row
    parts = three_parts(v_rows[...])
    total = got_ref[0, :, 0:FLAT]
    for p in range(1, got_ref.shape[0]):
        total = total + got_ref[p, :, 0:FLAT]
    total = rows_of(jnp.where(home, total, 0.0))
    back = 0.5 * folded(over_cols(parts, high_ref[...]) + over_cols(parts, low_ref[...]))
    for k in range(3):
        part = back[k : k + 1] + total[k]
        for p in range(sent_ref.shape[0]):
            sent_ref[p, :, k * W : (k + 1) * W] = part


def algebra_kernel(got_ref, coef_ref):
    tile = got_ref[0, :, FLAT:]
    for p in range(1, got_ref.shape[0]):
        tile = tile + got_ref[p, :, FLAT:]
    flat = iter(unpacked(tile, 21))
    gram = {(i, j): next(flat) for i in range(6) for j in range(i, 6)}
    g00 = symmetric([gram[i, j] for i in range(3) for j in range(i, 3)])
    g01 = [[gram[i, j + 3] for j in range(3)] for i in range(3)]
    g11 = symmetric([gram[i + 3, j + 3] for i in range(3) for j in range(i, 3)])
    n0 = inverse(cholesky(g00))
    n0t = turned(n0)
    c0 = times(times(n0, turned(g01)), n0t)
    l1 = cholesky(minus(times(times(n0, g11), n0t), times(c0, turned(c0))))
    n1 = inverse(l1)
    at = 0
    for matrix in (n0, n1, c0, l1):
        for i in range(3):
            for j in range(3):
                coef_ref[at : at + 1, :] = jnp.broadcast_to(matrix[i][j], (1, 128))
                at += 1


def loaded(coef_ref, which, width):
    row = lambda at: coef_ref[at : at + 1, :]
    wide = lambda v: v if width == 128 else jnp.concatenate([v] * (width // 128), 1)
    return [[wide(row(9 * which + 3 * i + j)) for j in range(3)] for i in range(3)]


def residual_kernel(got_ref, z_ref, x_ref, d_ref, coef_ref, sent_ref, basis_ref):
    total = got_ref[0]
    for p in range(1, got_ref.shape[0]):
        total = total + got_ref[p]
    z = z_ref[...]
    y = rows_of(total + d_ref[...] * z)
    n0, n1, c0, l1 = (loaded(coef_ref, i, W) for i in range(4))
    q0 = combine(n0, rows_of(x_ref[...]))
    u = combine(n0, rows_of(z))
    q1 = combine(n1, [a - b for a, b in zip(u, combine(c0, q0))])
    w = combine(n1, [a - b for a, b in zip(combine(n0, y), combine(c0, u))])
    known = [a + b for a, b in zip(combine(turned(l1), q0), combine(c0, q1))]
    w = [a - b for a, b in zip(w, known)]
    values = [inner(a, b) for a in w for b in q0 + q1]
    values += [inner(w[i], w[j]) for i in range(3) for j in range(i, 3)]
    tile = packed(values)
    for p in range(sent_ref.shape[0]):
        sent_ref[p] = tile
    for at, row in enumerate(q0 + q1 + w):
        basis_ref[at : at + 1, :] = row


def last_kernel(got_ref, basis_ref, coef_ref, out_ref, coeffs_ref):
    tile = got_ref[0]
    for p in range(1, got_ref.shape[0]):
        tile = tile + got_ref[p]
    values = unpacked(tile, 24)
    d0 = [values[6 * i : 6 * i + 3] for i in range(3)]
    d1 = [values[6 * i + 3 : 6 * i + 6] for i in range(3)]
    h2 = minus(minus(symmetric(values[18:]), times(d0, turned(d0))), times(d1, turned(d1)))
    l2 = cholesky(h2)
    n2 = inverse(l2)
    rows = [basis_ref[at : at + 1, :] for at in range(9)]
    q0, q1, w = rows[:3], rows[3:6], rows[6:]
    known = [a + b for a, b in zip(combine(d0, q0), combine(d1, q1))]
    q2 = combine(n2, [a - b for a, b in zip(w, known)])
    root = float(M) ** 0.5
    for k in range(3):
        out_ref[0, k : k + 1, :] = q1[k] * root
        out_ref[1, k : k + 1, :] = q2[k] * root
    c0, l1 = ([[v[:, 0:1] for v in line] for line in loaded(coef_ref, i, 128)] for i in (2, 3))
    down = lax.broadcasted_iota(jnp.int32, (3, 3), 0)
    across = lax.broadcasted_iota(jnp.int32, (3, 3), 1)

    def square(matrix, shift):
        tile = jnp.where(down == across, shift, 0.0)
        for i in range(3):
            for j in range(3):
                tile = jnp.where((down == i) & (across == j), tile + matrix[i][j], tile)
        return tile

    second = [[c0[i][j] + d1[i][j] for j in range(3)] for i in range(3)]
    coeffs_ref[0, 0] = square(c0, SHIFT)
    coeffs_ref[0, 1] = square(l1, 0.0)
    coeffs_ref[1, 0] = square(second, SHIFT)
    coeffs_ref[1, 1] = square(l2, 0.0)


def call(kernel, out, inputs, scratch=(), specs=None, flops=2_000_000):
    return pl.pallas_call(
        kernel,
        out_shape=out,
        in_specs=specs or [VMEM] * len(inputs),
        out_specs=jax.tree.map(lambda _: VMEM, out),
        scratch_shapes=list(scratch),
        cost_estimate=pl.CostEstimate(flops=flops, bytes_accessed=100_000, transcendentals=0),
        name=kernel.__name__,
        compiler_params=pltpu.CompilerParams(vmem_limit_bytes=24 << 20),
    )(*inputs)


def shards(couplings, diag_terms, start_block):
    cols = lax.axis_size("col")
    rows = lax.axis_size("row")
    x = start_block.reshape(1, FLAT)
    d = jnp.tile(diag_terms - SHIFT, 3).reshape(1, FLAT)
    swap = [(i, i ^ 1) for i in range(cols)]
    whole = (2 * W, W)
    f32 = lambda *shape: jax.ShapeDtypeStruct(shape, F32)

    def swapped(block):
        return lax.ppermute(block, "col", swap)

    def collect(got, own, cross):
        sent = call(
            backward_kernel,
            f32(rows, 1, FLAT),
            (got, own, cross, high, low),
            [pltpu.VMEM((8, 2 * W), F32)],
        )
        return lax.all_to_all(sent, "row", 0, 0, tiled=True)

    cross = swapped(x)
    sent, high, low = call(
        first_kernel,
        (f32(cols, 1, FLAT), in_vmem(whole, BF16), in_vmem(whole, BF16)),
        (x, couplings),
        [
            pltpu.VMEM(whole, F32),
            pltpu.VMEM((8, W), F32),
            pltpu.VMEM((8, 2 * W), F32),
            pltpu.SemaphoreType.DMA((2 * W // CHUNK,)),
        ],
        [VMEM, pl.BlockSpec(memory_space=pl.ANY)],
    )
    got = lax.all_to_all(sent, "col", 0, 0, tiled=True)
    got = collect(got, x, cross)
    z = jnp.sum(got, axis=0) + d * x
    cross = swapped(z)
    sent = call(
        forward_kernel,
        f32(cols, 1, FLAT + 128),
        (z, x, high, low),
        [pltpu.VMEM((8, W), F32), pltpu.VMEM((8, 2 * W), F32)],
    )
    got = lax.all_to_all(sent, "col", 0, 0, tiled=True)
    coef = call(algebra_kernel, f32(40, 128), (got,))
    got = collect(got, z, cross)
    sent, basis = call(residual_kernel, (f32(cols, 1, 128), f32(16, W)), (got, z, x, d, coef))
    got = lax.all_to_all(sent, "col", 0, 0, tiled=True)
    return call(last_kernel, (f32(2, 3, W), f32(2, 2, 3, 3)), (got, basis, coef))


def solution(mesh):
    placed = (P("row", "col"), P("col"), P(None, "col"))
    return jax.shard_map(
        shards, mesh=mesh, in_specs=placed, out_specs=(P(None, None, "col"), P()), check_vma=False
    )
```

time: 232 us -> 110 us (0.47)
  blocking collectives: 78.2 us -> 12.2 us
  matrix products: 35.4 us -> 0 us
  waiting for transfers between devices: 52.7 us -> 37.2 us
  starting transfers between devices: 49.7 us -> 38.3 us
  Pallas kernels: 0 us -> 10.5 us
  other arithmetic: 7.44 us -> 0.12 us
  local copies, waits for them, and re-layouts: 6.66 us -> 10.7 us
    all_gather x3 -> x0, blocking collectives: 78.2 us -> none  [the longest x1 44.4 us: turned_gather(): result, at, done = (lax.all_gather(both, axis, axis=0, tiled=True), 0, [])]
    dot_general x11 -> x0, matrix products: 32.6 us -> none  [the longest x9 20.2 us: product(): jnp.dot(a, b, precision=lax.Precision.HIGHEST, preferred_element_type=jnp...]
    all_to_all x6 -> x4, waiting for transfers between devices: 52.7 us -> 34.1 us  [the longest x2 18.5 us: collect(): return lax.all_to_all(sent, 'row', 0, 0, tiled=True)]
    all_to_all x6 -> x4, starting transfers between devices: 49.7 us -> 32 us  [the longest x2 17.6 us: shards(): got = lax.all_to_all(sent, 'col', 0, 0, tiled=True)]
    all_to_all x0 -> x1, blocking collectives: none -> 12.2 us  [shards(): got = lax.all_to_all(sent, 'col', 0, 0, tiled=True)]
    pallas_call x0 -> x7, Pallas kernels: none -> 10.5 us  [call(): pl.pallas_call(kernel, out_shape=out, in_specs=specs or [VMEM] * len(inpu...]
    unnamed x1 -> x15, local copies, waits for them, and re-layouts: 0.62 us -> 9.49 us
    another operation x21 -> x0, other arithmetic: 6.34 us -> none  [the longest x6 1.93 us: shards(): factor = jnp.linalg.cholesky(product(image, image.T))]
  transfers between devices with their start and end apart: 6 -> 6, of which waited for: 4 -> 6; matrix products, arithmetic and copies ran while one was open for 6% -> 0% of each run, Pallas kernels for 0% -> 0%
where the time goes in v2:
time: 110 us
  starting transfers between devices  38.3 us (35%)
  waiting for transfers between devices  37.2 us (34%)
  blocking collectives  12.2 us (11%)
  local copies, waits for them, and re-layouts  10.7 us (10%)
  Pallas kernels  10.5 us (10%)
    all_to_all x2, waiting for transfers between devices, collect(): return lax.all_to_all(sent, 'row', 0, 0, tiled=True)  18.5 us
    all_to_all x2, starting transfers between devices, shards(): got = lax.all_to_all(sent, 'col', 0, 0, tiled=True)  17.6 us
    all_to_all x2, waiting for transfers between devices, shards(): got = lax.all_to_all(sent, 'col', 0, 0, tiled=True)  15.6 us
    all_to_all x2, starting transfers between devices, collect(): return lax.all_to_all(sent, 'row', 0, 0, tiled=True)  14.4 us
    all_to_all x1, blocking collectives, shards(): got = lax.all_to_all(sent, 'col', 0, 0, tiled=True)  12.2 us
    pallas_call x7, Pallas kernels, call(): pl.pallas_call(kernel, out_shape=out, in_specs=specs or [VMEM] * len(inpu...  10.5 us
    unnamed x15, local copies, waits for them, and re-layouts  9.49 us
    ppermute x2, starting transfers between devices, swapped(): return lax.ppermute(block, 'col', swap)  6.28 us
  transfers between devices with their start and end apart: 6, of which 6 were waited for; matrix products, arithmetic and copies ran while one was open for 0% of the time, Pallas kernels for 0%

profile of v2, /device:TPU:1, one launch (start us, length us, event | category | flops | bytes accessed | tf_op | source)
XLA Modules:
  0.0 109.7 jit_solution(9278101723717686400)
XLA Ops:
  0.6 0.7 copy.7
  1.4 0.0 copy-start.4
  1.4 2.3 %copy-done.4 = f32[1536,768]{1,0:T(8,128)S(1)} copy-done((f32[1536,768]{1,0:T(8,128)S(1)}, f32[1536,768]{1,0:T(8,128)}, u32[]{:S(2)}) %copy-start.4) | copy-done | bytes 4718616
  3.7 4.4 %first_kernel.1 = (f32[32,1,2304]{2,1,0:T(1,128)}, bf16[1536,768]{1,0:T(8,128)(2,1)S(1)}, bf16[1536,768]{1,0:T(8,128)(2,1)S(1)}) custom-call(f32[1,2304]{1,0:T(1,128)S(1)} %bitcast.7, f32[1536,768]{1,0:T(8,128)S(1)} %copy-done.4), custom_call_target="tpu_custom_call" | custom-call | flops 2000000 | bytes 100000 | tf_op jit(solution)/shard_map/first_kernel/pallas_call | solution.py:258
  8.1 0.0 copy-start
  8.1 1.4 %copy-done = bf16[1536,768]{1,0:T(8,128)(2,1)} copy-done((bf16[1536,768]{1,0:T(8,128)(2,1)}, bf16[1536,768]{1,0:T(8,128)(2,1)S(1)}, u32[]{:S(2)}) %copy-start) | copy-done | bytes 2359320
  9.5 13.7 %all-to-all-start = ((f32[32,1,2304]{2,1,0:T(1,128)}), f32[32,1,2304]{2,1,0:T(1,128)S(1)}, u32[]{:S(2)}, u32[]{:S(2)}) async-start(f32[32,1,2304]{2,1,0:T(1,128)} %get-tuple-element.7), calls=%async_computation | async-start | bytes 589824 | tf_op jit(solution)/shard_map/all_to_all | solution.py:304
  23.2 3.1 %collective-permute-start = (f32[1,2304]{1,0:T(1,128)S(1)}, f32[1,2304]{1,0:T(1,128)S(1)}, u32[]{:S(2)}, u32[]{:S(2)}) collective-permute-start(f32[1,2304]{1,0:T(1,128)S(1)} %bitcast.8), channel_id=1, source_target_pairs={{0,1},{1,0},{2,3},{3,2},{4,5},{5,4},{6,7},{7,6},{8,9},{9,8},{10,11... | collective-permute-start | bytes 27656 | tf_op jit(solution)/shard_map/ppermute | solution.py:280
  26.4 1.6 %collective-permute-done.cross_ref = f32[1,2304]{1,0:T(1,128)S(1)} collective-permute-done((f32[1,2304]{1,0:T(1,128)S(1)}, f32[1,2304]{1,0:T(1,128)S(1)}, u32[]{:S(2)}, u32[]{:S(2)}) %collective-permute-start) | collective-permute-done | bytes 9248 | tf_op jit(solution)/shard_map/ppermute | solution.py:280
  27.9 7.3 %all-to-all-done.got_ref = f32[32,1,2304]{2,1,0:T(1,128)S(1)} async-done(((f32[32,1,2304]{2,1,0:T(1,128)}), f32[32,1,2304]{2,1,0:T(1,128)S(1)}, u32[]{:S(2)}, u32[]{:S(2)}) %all-to-all-start) | async-done | bytes 294944 | tf_op jit(solution)/shard_map/all_to_all | solution.py:304
  35.2 0.0 copy-start.1
  35.2 1.7 %copy-done.1 = bf16[1536,768]{1,0:T(8,128)(2,1)S(1)} copy-done((bf16[1536,768]{1,0:T(8,128)(2,1)S(1)}, bf16[1536,768]{1,0:T(8,128)(2,1)}, u32[]{:S(2)}) %copy-start.1) | copy-done | bytes 2359320
  36.9 0.0 copy-start.5
  36.9 1.6 %backward_kernel.2 = f32[16,1,2304]{2,1,0:T(1,128)} custom-call(f32[32,1,2304]{2,1,0:T(1,128)S(1)} %all-to-all-done.got_ref, f32[1,2304]{1,0:T(1,128)S(1)} %bitcast.9, f32[1,2304]{1,0:T(1,128)S(1)} %collective-permute-done.cross_ref, bf16[1536,768]{1,0:T(8,128)(2,1)S(1)} %get-tuple-element.8.high_ref, bf16[1536,768]{1,0:T(8,128)(2,1)S(1)} %copy-done.1), custom_call_target="tpu_custom_call" | custom-call | flops 2000000 | bytes 100000 | tf_op jit(solution)/shard_map/backward_kernel/pallas_call | solution.py:258
  38.5 9.3 %all-to-all-start.1 = ((f32[16,1,2304]{2,1,0:T(1,128)}), f32[16,1,2304]{2,1,0:T(1,128)S(1)}, u32[]{:S(2)}, u32[]{:S(2)}) async-start(f32[16,1,2304]{2,1,0:T(1,128)} %backward_kernel.2), calls=%async_computation.1 | async-start | bytes 294912 | tf_op jit(solution)/shard_map/all_to_all | solution.py:289
  47.8 0.0 copy-done.5
  47.9 9.2 %all-to-all-done.1 = f32[16,1,2304]{2,1,0:T(1,128)S(1)} async-done(((f32[16,1,2304]{2,1,0:T(1,128)}), f32[16,1,2304]{2,1,0:T(1,128)S(1)}, u32[]{:S(2)}, u32[]{:S(2)}) %all-to-all-start.1) | async-done | bytes 147488 | tf_op jit(solution)/shard_map/all_to_all | solution.py:289
  57.0 0.1 reduce_sum.11
  57.2 0.0 copy-start.2
  57.2 1.7 %copy-done.2 = bf16[1536,768]{1,0:T(8,128)(2,1)S(1)} copy-done((bf16[1536,768]{1,0:T(8,128)(2,1)S(1)}, bf16[1536,768]{1,0:T(8,128)(2,1)}, u32[]{:S(2)}) %copy-start.2) | copy-done | bytes 2359320
  58.8 2.2 %forward_kernel.1 = f32[32,1,2432]{2,1,0:T(1,128)} custom-call(f32[1,2304]{1,0:T(1,128)S(1)} %multiply_add_fusion.z_ref.own_ref, f32[1,2304]{1,0:T(1,128)S(1)} %bitcast.11, bf16[1536,768]{1,0:T(8,128)(2,1)S(1)} %get-tuple-element.8.high_ref, bf16[1536,768]{1,0:T(8,128)(2,1)S(1)} %copy-done.2), custom_call_target="tpu_custom_call" | custom-call | flops 2000000 | bytes 100000 | tf_op jit(solution)/shard_map/forward_kernel/pallas_call | solution.py:258
  61.0 3.9 %all-to-all-start.2 = ((f32[32,1,2432]{2,1,0:T(1,128)}), f32[32,1,2432]{2,1,0:T(1,128)S(1)}, u32[]{:S(2)}, u32[]{:S(2)}) async-start(f32[32,1,2432]{2,1,0:T(1,128)} %forward_kernel.1), calls=%async_computation.2 | async-start | bytes 622592 | tf_op jit(solution)/shard_map/all_to_all | solution.py:314
  65.0 3.1 %collective-permute-start.1 = (f32[1,2304]{1,0:T(1,128)S(1)}, f32[1,2304]{1,0:T(1,128)S(1)}, u32[]{:S(2)}, u32[]{:S(2)}) collective-permute-start(f32[1,2304]{1,0:T(1,128)S(1)} %multiply_add_fusion.z_ref.own_ref), channel_id=1, source_target_pairs={{0,1},{1,0},{2,3},{3,2},{4,5},{5,4},{6,7},{7,6},{8,9},{9,8},{10,11... | collective-permute-start | bytes 27656 | tf_op jit(solution)/shard_map/ppermute | solution.py:280
  68.1 1.6 %collective-permute-done.1.cross_ref = f32[1,2304]{1,0:T(1,128)S(1)} collective-permute-done((f32[1,2304]{1,0:T(1,128)S(1)}, f32[1,2304]{1,0:T(1,128)S(1)}, u32[]{:S(2)}, u32[]{:S(2)}) %collective-permute-start.1) | collective-permute-done | bytes 9248 | tf_op jit(solution)/shard_map/ppermute | solution.py:280
  69.7 8.3 %all-to-all-done.2.got_ref = f32[32,1,2432]{2,1,0:T(1,128)S(1)} async-done(((f32[32,1,2432]{2,1,0:T(1,128)}), f32[32,1,2432]{2,1,0:T(1,128)S(1)}, u32[]{:S(2)}, u32[]{:S(2)}) %all-to-all-start.2) | async-done | bytes 311328 | tf_op jit(solution)/shard_map/all_to_all | solution.py:314
  77.9 0.0 copy-start.3
  77.9 1.7 %copy-done.3 = bf16[1536,768]{1,0:T(8,128)(2,1)S(1)} copy-done((bf16[1536,768]{1,0:T(8,128)(2,1)S(1)}, bf16[1536,768]{1,0:T(8,128)(2,1)}, u32[]{:S(2)}) %copy-start.3) | copy-done | bytes 2359320
  79.6 1.6 %backward_kernel.3 = f32[16,1,2304]{2,1,0:T(1,128)} custom-call(f32[32,1,2432]{2,1,0:T(1,128)S(1)} %all-to-all-done.2.got_ref, f32[1,2304]{1,0:T(1,128)S(1)} %multiply_add_fusion.z_ref.own_ref, f32[1,2304]{1,0:T(1,128)S(1)} %collective-permute-done.1.cross_ref, bf16[1536,768]{1,0:T(8,128)(2,1)S(1)} %get-tuple-element.8.high_ref, bf16[1536,768]{1,0:T(8,128)(2,1)S(1)} %copy-done.3), custom_call_target="tpu_custom_call" | custom-call | flops 2000000 | bytes 100000 | tf_op jit(solution)/shard_map/backward_kernel/pallas_call | solution.py:258
  81.2 5.1 %all-to-all-start.3 = ((f32[16,1,2304]{2,1,0:T(1,128)}), f32[16,1,2304]{2,1,0:T(1,128)S(1)}, u32[]{:S(2)}, u32[]{:S(2)}) async-start(f32[16,1,2304]{2,1,0:T(1,128)} %backward_kernel.3), calls=%async_computation.3 | async-start | bytes 294912 | tf_op jit(solution)/shard_map/all_to_all | solution.py:289
  86.3 0.2 algebra_kernel.1.coef_ref
  86.5 9.3 %all-to-all-done.3.got_ref = f32[16,1,2304]{2,1,0:T(1,128)S(1)} async-done(((f32[16,1,2304]{2,1,0:T(1,128)}), f32[16,1,2304]{2,1,0:T(1,128)S(1)}, u32[]{:S(2)}, u32[]{:S(2)}) %all-to-all-start.3) | async-done | bytes 147488 | tf_op jit(solution)/shard_map/all_to_all | solution.py:289
  95.8 0.3 residual_kernel.1
  96.1 12.2 %all_to_all.25.got_ref = f32[32,1,128]{2,1,0:T(1,128)S(1)} all-to-all(f32[32,1,128]{2,1,0:T(1,128)S(1)} %get-tuple-element.10), channel_id=1, replica_groups=mesh['row'=16,'col'=32] {'col'}, dimensions={0} | all-to-all | bytes 32768 | tf_op jit(solution)/shard_map/all_to_all | solution.py:318
  108.3 0.2 last_kernel.1
  108.5 0.6 copy.5
  109.1 0.6 copy.6
  (4 shorter events, 0.0 us)
Async XLA Ops:
  1.4 2.3 %copy-start.4 = (f32[1536,768]{1,0:T(8,128)S(1)}, f32[1536,768]{1,0:T(8,128)}, u32[]{:S(2)}) copy-start(f32[1536,768]{1,0:T(8,128)} %a_ref.1) | copy-start | bytes 14155780
  8.1 1.4 %copy-start = (bf16[1536,768]{1,0:T(8,128)(2,1)}, bf16[1536,768]{1,0:T(8,128)(2,1)S(1)}, u32[]{:S(2)}) copy-start(bf16[1536,768]{1,0:T(8,128)(2,1)S(1)} %get-tuple-element.9.low_ref) | copy-start | bytes 7077892
  9.5 25.7 %all-to-all-start = ((f32[32,1,2304]{2,1,0:T(1,128)}), f32[32,1,2304]{2,1,0:T(1,128)S(1)}, u32[]{:S(2)}, u32[]{:S(2)}) async-start(f32[32,1,2304]{2,1,0:T(1,128)} %get-tuple-element.7), calls=%async_computation | async-start | bytes 589824 | tf_op jit(solution)/shard_map/all_to_all | solution.py:304
  23.2 4.7 %collective-permute-start = (f32[1,2304]{1,0:T(1,128)S(1)}, f32[1,2304]{1,0:T(1,128)S(1)}, u32[]{:S(2)}, u32[]{:S(2)}) collective-permute-start(f32[1,2304]{1,0:T(1,128)S(1)} %bitcast.8), channel_id=1, source_target_pairs={{0,1},{1,0},{2,3},{3,2},{4,5},{5,4},{6,7},{7,6},{8,9},{9,8},{10,11... | collective-permute-start | bytes 27656 | tf_op jit(solution)/shard_map/ppermute | solution.py:280
  35.2 1.7 %copy-start.1 = (bf16[1536,768]{1,0:T(8,128)(2,1)S(1)}, bf16[1536,768]{1,0:T(8,128)(2,1)}, u32[]{:S(2)}) copy-start(bf16[1536,768]{1,0:T(8,128)(2,1)} %copy-done) | copy-start | bytes 7077892
  36.9 10.9 %copy-start.5 = (f32[768]{0:T(1024)S(1)}, f32[768]{0:T(1024)}, u32[]{:S(2)}) copy-start(f32[768]{0:T(1024)} %param.4) | copy-start | bytes 9220
  38.5 18.6 %all-to-all-start.1 = ((f32[16,1,2304]{2,1,0:T(1,128)}), f32[16,1,2304]{2,1,0:T(1,128)S(1)}, u32[]{:S(2)}, u32[]{:S(2)}) async-start(f32[16,1,2304]{2,1,0:T(1,128)} %backward_kernel.2), calls=%async_computation.1 | async-start | bytes 294912 | tf_op jit(solution)/shard_map/all_to_all | solution.py:289
  57.2 1.7 %copy-start.2 = (bf16[1536,768]{1,0:T(8,128)(2,1)S(1)}, bf16[1536,768]{1,0:T(8,128)(2,1)}, u32[]{:S(2)}) copy-start(bf16[1536,768]{1,0:T(8,128)(2,1)} %copy-done) | copy-start | bytes 7077892
  61.0 16.9 %all-to-all-start.2 = ((f32[32,1,2432]{2,1,0:T(1,128)}), f32[32,1,2432]{2,1,0:T(1,128)S(1)}, u32[]{:S(2)}, u32[]{:S(2)}) async-start(f32[32,1,2432]{2,1,0:T(1,128)} %forward_kernel.1), calls=%async_computation.2 | async-start | bytes 622592 | tf_op jit(solution)/shard_map/all_to_all | solution.py:314
  65.0 4.7 %collective-permute-start.1 = (f32[1,2304]{1,0:T(1,128)S(1)}, f32[1,2304]{1,0:T(1,128)S(1)}, u32[]{:S(2)}, u32[]{:S(2)}) collective-permute-start(f32[1,2304]{1,0:T(1,128)S(1)} %multiply_add_fusion.z_ref.own_ref), channel_id=1, source_target_pairs={{0,1},{1,0},{2,3},{3,2},{4,5},{5,4},{6,7},{7,6},{8,9},{9,8},{10,11... | collective-permute-start | bytes 27656 | tf_op jit(solution)/shard_map/ppermute | solution.py:280
  77.9 1.7 %copy-start.3 = (bf16[1536,768]{1,0:T(8,128)(2,1)S(1)}, bf16[1536,768]{1,0:T(8,128)(2,1)}, u32[]{:S(2)}) copy-start(bf16[1536,768]{1,0:T(8,128)(2,1)} %copy-done) | copy-start | bytes 7077892
  81.2 14.6 %all-to-all-start.3 = ((f32[16,1,2304]{2,1,0:T(1,128)}), f32[16,1,2304]{2,1,0:T(1,128)S(1)}, u32[]{:S(2)}, u32[]{:S(2)}) async-start(f32[16,1,2304]{2,1,0:T(1,128)} %backward_kernel.3), calls=%async_computation.3 | async-start | bytes 294912 | tf_op jit(solution)/shard_map/all_to_all | solution.py:289

commit v3 on v2

--- a/solution.py
+++ b/solution.py
@@ -13,6 +13,7 @@
 F32 = jnp.float32
 BF16 = jnp.bfloat16
 VMEM = pl.BlockSpec(memory_space=pltpu.VMEM)
+HBM = pl.BlockSpec(memory_space=pltpu.HBM)
 
 
 def in_vmem(shape, dtype=F32):
@@ -106,32 +107,47 @@
             sent_ref[2 * row_index + half, :, k * W : (k + 1) * W] = forward_ref[k : k + 1, half * W : (half + 1) * W]
 
 
-def first_kernel(x_ref, a_ref, sent_ref, high_ref, low_ref, whole, x_rows, forward, sems):
+def first_kernel(x_ref, a_ref, sent_ref, flat_ref, high_ref, low_ref, whole, low, x_rows, forward, sems, out_sems):
     row_index = lax.axis_index("row")
     pieces = [pl.ds(i * CHUNK, CHUNK) for i in range(2 * W // CHUNK)]
     copies = [pltpu.make_async_copy(a_ref.at[piece], whole.at[piece], sems.at[i]) for i, piece in enumerate(pieces)]
+    leaving = [pltpu.make_async_copy(low.at[piece], low_ref.at[piece], out_sems.at[i]) for i, piece in enumerate(pieces)]
     for copy in copies:
         copy.start()
-    x = x_ref[...]
     x_rows[...] = jnp.zeros_like(x_rows)
-    for k, row in enumerate(rows_of(x)):
-        x_rows[k : k + 1, :] = row
+    x_rows[0:3, :] = x_ref[...]
+    for k in range(3):
+        flat_ref[:, k * W : (k + 1) * W] = x_ref[k : k + 1, :]
+    x = flat_ref[...]
     for p in range(sent_ref.shape[0]):
         sent_ref[p] = x
     parts = three_parts(x_rows[...])
-    for copy, piece in zip(copies, pieces):
-        copy.wait()
+    for i, piece in enumerate(pieces):
+        copies[i].wait()
         block = whole[piece, :]
         high = block.astype(BF16)
-        low = (block - high.astype(F32)).astype(BF16)
+        rest = (block - high.astype(F32)).astype(BF16)
         high_ref[piece, :] = high
-        low_ref[piece, :] = low
-        forward[:, piece] = 0.5 * folded(over_rows(parts, high) + over_rows(parts, low))
+        low[piece, :] = rest
+        leaving[i].start()
+        forward[:, piece] = 0.5 * folded(over_rows(parts, high) + over_rows(parts, rest))
     place(row_index, forward, sent_ref)
-
-
-def forward_kernel(z_ref, x_ref, high_ref, low_ref, sent_ref, z_rows, forward):
+    for copy in leaving:
+        copy.wait()
+
+
+def fetch(low_ref, low, sems):
+    step = low.shape[0] // sems.shape[0]
+    pieces = [pl.ds(i * step, step) for i in range(sems.shape[0])]
+    copies = [pltpu.make_async_copy(low_ref.at[piece], low.at[piece], sems.at[i]) for i, piece in enumerate(pieces)]
+    for copy in copies:
+        copy.start()
+    return list(zip(copies, pieces))
+
+
+def forward_kernel(z_ref, x_ref, high_ref, low_ref, sent_ref, low, z_rows, forward, sems):
     row_index = lax.axis_index("row")
+    copies = fetch(low_ref, low, sems)
     z = z_ref[...]
     z_rows[...] = jnp.zeros_like(z_rows)
     for k, row in enumerate(rows_of(z)):
@@ -142,11 +158,15 @@
     for p in range(sent_ref.shape[0]):
         sent_ref[p, :, 0:FLAT] = z
         sent_ref[p, :, FLAT:] = tile
-    forward[...] = 0.5 * folded(over_rows(parts, high_ref[...]) + over_rows(parts, low_ref[...]))
+    forward[...] = folded(over_rows(parts, high_ref[...]))
+    for copy, piece in copies:
+        copy.wait()
+        forward[:, piece] = 0.5 * (forward[:, piece] + folded(over_rows(parts, low[piece, :])))
     place(row_index, forward, sent_ref)
 
 
-def backward_kernel(got_ref, own_ref, cross_ref, high_ref, low_ref, sent_ref, v_rows):
+def backward_kernel(got_ref, own_ref, cross_ref, high_ref, low_ref, sent_ref, low, v_rows, sems):
+    copies = fetch(low_ref, low, sems)
     row_index = lax.axis_index("row")
     col_index = lax.axis_index("col")
     home = col_index // 2 == row_index
@@ -161,7 +181,12 @@
     for p in range(1, got_ref.shape[0]):
         total = total + got_ref[p, :, 0:FLAT]
     total = rows_of(jnp.where(home, total, 0.0))
-    back = 0.5 * folded(over_cols(parts, high_ref[...]) + over_cols(parts, low_ref[...]))
+    wide = over_cols(parts, high_ref[...])
+    for i, (copy, piece) in enumerate(copies):
+        copy.wait()
+        step = low.shape[0] // len(copies)
+        wide = wide + over_cols(parts[:, i * step : (i + 1) * step], low[piece, :])
+    back = 0.5 * folded(wide)
     for k in range(3):
         part = back[k : k + 1] + total[k]
         for p in range(sent_ref.shape[0]):
@@ -234,8 +259,8 @@
     q2 = combine(n2, [a - b for a, b in zip(w, known)])
     root = float(M) ** 0.5
     for k in range(3):
-        out_ref[0, k : k + 1, :] = q1[k] * root
-        out_ref[1, k : k + 1, :] = q2[k] * root
+        out_ref[k, 0:1, :] = q1[k] * root
+        out_ref[k, 1:2, :] = q2[k] * root
     c0, l1 = ([[v[:, 0:1] for v in line] for line in loaded(coef_ref, i, 128)] for i in (2, 3))
     down = lax.broadcasted_iota(jnp.int32, (3, 3), 0)
     across = lax.broadcasted_iota(jnp.int32, (3, 3), 1)
@@ -248,18 +273,19 @@
         return tile
 
     second = [[c0[i][j] + d1[i][j] for j in range(3)] for i in range(3)]
-    coeffs_ref[0, 0] = square(c0, SHIFT)
-    coeffs_ref[0, 1] = square(l1, 0.0)
-    coeffs_ref[1, 0] = square(second, SHIFT)
-    coeffs_ref[1, 1] = square(l2, 0.0)
-
-
-def call(kernel, out, inputs, scratch=(), specs=None, flops=2_000_000):
+    blocks = [[square(c0, SHIFT), square(l1, 0.0)], [square(second, SHIFT), square(l2, 0.0)]]
+    for j in range(2):
+        for i in range(3):
+            for which in range(2):
+                coeffs_ref[j, i, which : which + 1, :] = blocks[j][which][i : i + 1, :]
+
+
+def call(kernel, out, inputs, scratch=(), specs=None, out_specs=None, flops=2_000_000):
     return pl.pallas_call(
         kernel,
         out_shape=out,
         in_specs=specs or [VMEM] * len(inputs),
-        out_specs=jax.tree.map(lambda _: VMEM, out),
+        out_specs=out_specs or jax.tree.map(lambda _: VMEM, out),
         scratch_shapes=list(scratch),
         cost_estimate=pl.CostEstimate(flops=flops, bytes_accessed=100_000, transcendentals=0),
         name=kernel.__name__,
@@ -270,11 +296,16 @@
 def shards(couplings, diag_terms, start_block):
     cols = lax.axis_size("col")
     rows = lax.axis_size("row")
-    x = start_block.reshape(1, FLAT)
     d = jnp.tile(diag_terms - SHIFT, 3).reshape(1, FLAT)
     swap = [(i, i ^ 1) for i in range(cols)]
     whole = (2 * W, W)
+    steps = 2 * W // CHUNK
     f32 = lambda *shape: jax.ShapeDtypeStruct(shape, F32)
+    low_scratch = pltpu.VMEM(whole, BF16)
+    low_sems = pltpu.SemaphoreType.DMA((3,))
+
+    def stay(array):
+        return pltpu.with_memory_space_constraint(array, pltpu.HBM)
 
     def swapped(block):
         return lax.ppermute(block, "col", swap)
@@ -283,24 +314,28 @@
         sent = call(
             backward_kernel,
             f32(rows, 1, FLAT),
-            (got, own, cross, high, low),
-            [pltpu.VMEM((8, 2 * W), F32)],
+            (got, own, cross, high, stay(low)),
+            [low_scratch, pltpu.VMEM((8, 2 * W), F32), low_sems],
+            [VMEM] * 4 + [HBM],
         )
         return lax.all_to_all(sent, "row", 0, 0, tiled=True)
 
-    cross = swapped(x)
-    sent, high, low = call(
+    sent, x, high, low = call(
         first_kernel,
-        (f32(cols, 1, FLAT), in_vmem(whole, BF16), in_vmem(whole, BF16)),
-        (x, couplings),
+        (f32(cols, 1, FLAT), f32(1, FLAT), in_vmem(whole, BF16), pltpu.HBM(whole, BF16)),
+        (start_block, stay(couplings)),
         [
             pltpu.VMEM(whole, F32),
+            low_scratch,
             pltpu.VMEM((8, W), F32),
             pltpu.VMEM((8, 2 * W), F32),
-            pltpu.SemaphoreType.DMA((2 * W // CHUNK,)),
+            pltpu.SemaphoreType.DMA((steps,)),
+            pltpu.SemaphoreType.DMA((steps,)),
         ],
-        [VMEM, pl.BlockSpec(memory_space=pl.ANY)],
+        [VMEM, HBM],
+        (VMEM, VMEM, VMEM, HBM),
     )
+    cross = swapped(x)
     got = lax.all_to_all(sent, "col", 0, 0, tiled=True)
     got = collect(got, x, cross)
     z = jnp.sum(got, axis=0) + d * x
@@ -308,15 +343,17 @@
     sent = call(
         forward_kernel,
         f32(cols, 1, FLAT + 128),
-        (z, x, high, low),
-        [pltpu.VMEM((8, W), F32), pltpu.VMEM((8, 2 * W), F32)],
+        (z, x, high, stay(low)),
+        [low_scratch, pltpu.VMEM((8, W), F32), pltpu.VMEM((8, 2 * W), F32), low_sems],
+        [VMEM] * 3 + [HBM],
     )
     got = lax.all_to_all(sent, "col", 0, 0, tiled=True)
     coef = call(algebra_kernel, f32(40, 128), (got,))
     got = collect(got, z, cross)
     sent, basis = call(residual_kernel, (f32(cols, 1, 128), f32(16, W)), (got, z, x, d, coef))
     got = lax.all_to_all(sent, "col", 0, 0, tiled=True)
-    return call(last_kernel, (f32(2, 3, W), f32(2, 2, 3, 3)), (got, basis, coef))
+    blocks, coeffs = call(last_kernel, (f32(3, 2, W), f32(2, 3, 2, 3)), (got, basis, coef))
+    return jnp.swapaxes(blocks, 0, 1), jnp.swapaxes(coeffs, 1, 2)
 
 
 def solution(mesh):

time: 110 us -> 106 us (0.964)
  local copies, waits for them, and re-layouts: 10.7 us -> 0.72 us
  Pallas kernels: 10.5 us -> 16 us
    unnamed x15 -> x6, local copies, waits for them, and re-layouts: 9.49 us -> 0.72 us
    pallas_call x7, Pallas kernels: 10.5 us -> 16 us  [call(): pl.pallas_call(kernel, out_shape=out, in_specs=specs or [VMEM] * len(inpu...]
    pallas_call x2 -> x0, local copies, waits for them, and re-layouts: 1.21 us -> none  [call(): pl.pallas_call(kernel, out_shape=out, in_specs=specs or [VMEM] * len(inpu...]
where the time goes in v3:
time: 106 us; the launch traced here: 105 us
  starting transfers between devices  38.4 us (36%)
  waiting for transfers between devices  37.2 us (35%)
  Pallas kernels  16 us (15%)
  blocking collectives  12.2 us (12%)
    all_to_all x2, waiting for transfers between devices, collect(): return lax.all_to_all(sent, 'row', 0, 0, tiled=True)  18.5 us
    all_to_all x2, starting transfers between devices, shards(): got = lax.all_to_all(sent, 'col', 0, 0, tiled=True)  17.6 us
    pallas_call x7, Pallas kernels, call(): pl.pallas_call(kernel, out_shape=out, in_specs=specs or [VMEM] * len(inpu...  16 us
    all_to_all x2, waiting for transfers between devices, shards(): got = lax.all_to_all(sent, 'col', 0, 0, tiled=True)  15.6 us
    all_to_all x2, starting transfers between devices, collect(): return lax.all_to_all(sent, 'row', 0, 0, tiled=True)  14.5 us
    all_to_all x1, blocking collectives, shards(): got = lax.all_to_all(sent, 'col', 0, 0, tiled=True)  12.2 us
    ppermute x2, starting transfers between devices, swapped(): return lax.ppermute(block, 'col', swap)  6.28 us
    ppermute x2, waiting for transfers between devices, swapped(): return lax.ppermute(block, 'col', swap)  3.11 us
  transfers between devices with their start and end apart: 6, of which 6 were waited for; matrix products, arithmetic and copies ran while one was open for 0% of the time, Pallas kernels for 0%

profile of v3, /device:TPU:1, one launch (start us, length us, event | category | flops | bytes accessed | tf_op | source)
XLA Modules:
  0.0 105.4 jit_solution(14114903357012246148)
XLA Ops:
  0.6 0.0 copy-start
  0.6 0.7 copy-done
  1.3 5.5 %first_kernel.1 = (f32[32,1,2304]{2,1,0:T(1,128)}, f32[1,2304]{1,0:T(1,128)S(1)}, bf16[1536,768]{1,0:T(8,128)(2,1)S(1)}, bf16[1536,768]{1,0:T(8,128)(2,1)}) custom-call(f32[3,768]{1,0:T(4,128)S(1)} %copy-done, f32[1536,768]{1,0:T(8,128)} %a_ref.1), custom_call_target="tpu_custom_call" | custom-call | flops 2000000 | bytes 100000 | tf_op jit(solution)/shard_map/first_kernel/pallas_call | solution.py:284
  6.8 13.7 %all-to-all-start = ((f32[32,1,2304]{2,1,0:T(1,128)}), f32[32,1,2304]{2,1,0:T(1,128)S(1)}, u32[]{:S(2)}, u32[]{:S(2)}) async-start(f32[32,1,2304]{2,1,0:T(1,128)} %get-tuple-element.10), calls=%async_computation | async-start | bytes 589824 | tf_op jit(solution)/shard_map/all_to_all | solution.py:339
  20.6 3.1 %collective-permute-start = (f32[1,2304]{1,0:T(1,128)S(1)}, f32[1,2304]{1,0:T(1,128)S(1)}, u32[]{:S(2)}, u32[]{:S(2)}) collective-permute-start(f32[1,2304]{1,0:T(1,128)S(1)} %get-tuple-element.11.own_ref.x_ref), channel_id=1, source_target_pairs={{0,1},{1,0},{2,3},{3,2},{4,5},{5,4},{6,7},{7,6},{8,9},{9,8},{10,11... | collective-permute-start | bytes 27656 | tf_op jit(solution)/shard_map/ppermute | solution.py:311
  23.7 1.6 %collective-permute-done.cross_ref = f32[1,2304]{1,0:T(1,128)S(1)} collective-permute-done((f32[1,2304]{1,0:T(1,128)S(1)}, f32[1,2304]{1,0:T(1,128)S(1)}, u32[]{:S(2)}, u32[]{:S(2)}) %collective-permute-start) | collective-permute-done | bytes 9248 | tf_op jit(solution)/shard_map/ppermute | solution.py:311
  25.3 7.3 %all-to-all-done.got_ref = f32[32,1,2304]{2,1,0:T(1,128)S(1)} async-done(((f32[32,1,2304]{2,1,0:T(1,128)}), f32[32,1,2304]{2,1,0:T(1,128)S(1)}, u32[]{:S(2)}, u32[]{:S(2)}) %all-to-all-start) | async-done | bytes 294944 | tf_op jit(solution)/shard_map/all_to_all | solution.py:339
  32.6 0.0 copy-start.1
  32.6 3.1 %backward_kernel.2 = f32[16,1,2304]{2,1,0:T(1,128)} custom-call(f32[32,1,2304]{2,1,0:T(1,128)S(1)} %all-to-all-done.got_ref, f32[1,2304]{1,0:T(1,128)S(1)} %get-tuple-element.11.own_ref.x_ref, f32[1,2304]{1,0:T(1,128)S(1)} %collective-permute-done.cross_ref, bf16[1536,768]{1,0:T(8,128)(2,1)S(1)} %get-tuple-element.12.high_ref, ...), custom_call_target="tpu_custom_call" | custom-call | flops 2000000 | bytes 100000 | tf_op jit(solution)/shard_map/backward_kernel/pallas_call | solution.py:284
  35.7 9.4 %all-to-all-start.1 = ((f32[16,1,2304]{2,1,0:T(1,128)}), f32[16,1,2304]{2,1,0:T(1,128)S(1)}, u32[]{:S(2)}, u32[]{:S(2)}) async-start(f32[16,1,2304]{2,1,0:T(1,128)} %backward_kernel.2), calls=%async_computation.1 | async-start | bytes 294912 | tf_op jit(solution)/shard_map/all_to_all | solution.py:321
  45.0 0.0 copy-done.1
  45.1 9.2 %all-to-all-done.1 = f32[16,1,2304]{2,1,0:T(1,128)S(1)} async-done(((f32[16,1,2304]{2,1,0:T(1,128)}), f32[16,1,2304]{2,1,0:T(1,128)S(1)}, u32[]{:S(2)}, u32[]{:S(2)}) %all-to-all-start.1) | async-done | bytes 147488 | tf_op jit(solution)/shard_map/all_to_all | solution.py:321
  54.3 0.1 reduce_sum.11
  54.4 3.1 %forward_kernel.1 = f32[32,1,2432]{2,1,0:T(1,128)} custom-call(f32[1,2304]{1,0:T(1,128)S(1)} %multiply_add_fusion.z_ref.own_ref, f32[1,2304]{1,0:T(1,128)S(1)} %get-tuple-element.11.own_ref.x_ref, bf16[1536,768]{1,0:T(8,128)(2,1)S(1)} %get-tuple-element.12.high_ref, bf16[1536,768]{1,0:T(8,128)(2,1)} %get-tuple-element.13.low_ref), custom_call_target="tpu_custom_call" | custom-call | flops 2000000 | bytes 100000 | tf_op jit(solution)/shard_map/forward_kernel/pallas_call | solution.py:284
  57.5 3.9 %all-to-all-start.2 = ((f32[32,1,2432]{2,1,0:T(1,128)}), f32[32,1,2432]{2,1,0:T(1,128)S(1)}, u32[]{:S(2)}, u32[]{:S(2)}) async-start(f32[32,1,2432]{2,1,0:T(1,128)} %forward_kernel.1), calls=%async_computation.2 | async-start | bytes 622592 | tf_op jit(solution)/shard_map/all_to_all | solution.py:350
  61.4 3.1 %collective-permute-start.1 = (f32[1,2304]{1,0:T(1,128)S(1)}, f32[1,2304]{1,0:T(1,128)S(1)}, u32[]{:S(2)}, u32[]{:S(2)}) collective-permute-start(f32[1,2304]{1,0:T(1,128)S(1)} %multiply_add_fusion.z_ref.own_ref), channel_id=1, source_target_pairs={{0,1},{1,0},{2,3},{3,2},{4,5},{5,4},{6,7},{7,6},{8,9},{9,8},{10,11... | collective-permute-start | bytes 27656 | tf_op jit(solution)/shard_map/ppermute | solution.py:311
  64.6 1.6 %collective-permute-done.1.cross_ref = f32[1,2304]{1,0:T(1,128)S(1)} collective-permute-done((f32[1,2304]{1,0:T(1,128)S(1)}, f32[1,2304]{1,0:T(1,128)S(1)}, u32[]{:S(2)}, u32[]{:S(2)}) %collective-permute-start.1) | collective-permute-done | bytes 9248 | tf_op jit(solution)/shard_map/ppermute | solution.py:311
  66.1 8.2 %all-to-all-done.2.got_ref = f32[32,1,2432]{2,1,0:T(1,128)S(1)} async-done(((f32[32,1,2432]{2,1,0:T(1,128)}), f32[32,1,2432]{2,1,0:T(1,128)S(1)}, u32[]{:S(2)}, u32[]{:S(2)}) %all-to-all-start.2) | async-done | bytes 311328 | tf_op jit(solution)/shard_map/all_to_all | solution.py:350
  74.4 3.1 %backward_kernel.3 = f32[16,1,2304]{2,1,0:T(1,128)} custom-call(f32[32,1,2432]{2,1,0:T(1,128)S(1)} %all-to-all-done.2.got_ref, f32[1,2304]{1,0:T(1,128)S(1)} %multiply_add_fusion.z_ref.own_ref, f32[1,2304]{1,0:T(1,128)S(1)} %collective-permute-done.1.cross_ref, bf16[1536,768]{1,0:T(8,128)(2,1)S(1)} %get-tuple-element.12.high_ref, ...), custom_call_target="tpu_custom_call" | custom-call | flops 2000000 | bytes 100000 | tf_op jit(solution)/shard_map/backward_kernel/pallas_call | solution.py:284
  77.4 5.1 %all-to-all-start.3 = ((f32[16,1,2304]{2,1,0:T(1,128)}), f32[16,1,2304]{2,1,0:T(1,128)S(1)}, u32[]{:S(2)}, u32[]{:S(2)}) async-start(f32[16,1,2304]{2,1,0:T(1,128)} %backward_kernel.3), calls=%async_computation.3 | async-start | bytes 294912 | tf_op jit(solution)/shard_map/all_to_all | solution.py:321
  82.5 0.2 algebra_kernel.1.coef_ref
  82.8 9.3 %all-to-all-done.3.got_ref = f32[16,1,2304]{2,1,0:T(1,128)S(1)} async-done(((f32[16,1,2304]{2,1,0:T(1,128)}), f32[16,1,2304]{2,1,0:T(1,128)S(1)}, u32[]{:S(2)}, u32[]{:S(2)}) %all-to-all-start.3) | async-done | bytes 147488 | tf_op jit(solution)/shard_map/all_to_all | solution.py:321
  92.1 0.3 residual_kernel.1
  92.4 12.2 %all_to_all.25.got_ref = f32[32,1,128]{2,1,0:T(1,128)S(1)} all-to-all(f32[32,1,128]{2,1,0:T(1,128)S(1)} %get-tuple-element.14), channel_id=1, replica_groups=mesh['row'=16,'col'=32] {'col'}, dimensions={0} | all-to-all | bytes 32768 | tf_op jit(solution)/shard_map/all_to_all | solution.py:354
  104.5 0.8 last_kernel.1
  (4 shorter events, 0.0 us)
Async XLA Ops:
  0.6 0.7 copy-start
  6.8 25.7 %all-to-all-start = ((f32[32,1,2304]{2,1,0:T(1,128)}), f32[32,1,2304]{2,1,0:T(1,128)S(1)}, u32[]{:S(2)}, u32[]{:S(2)}) async-start(f32[32,1,2304]{2,1,0:T(1,128)} %get-tuple-element.10), calls=%async_computation | async-start | bytes 589824 | tf_op jit(solution)/shard_map/all_to_all | solution.py:339
  20.6 4.7 %collective-permute-start = (f32[1,2304]{1,0:T(1,128)S(1)}, f32[1,2304]{1,0:T(1,128)S(1)}, u32[]{:S(2)}, u32[]{:S(2)}) collective-permute-start(f32[1,2304]{1,0:T(1,128)S(1)} %get-tuple-element.11.own_ref.x_ref), channel_id=1, source_target_pairs={{0,1},{1,0},{2,3},{3,2},{4,5},{5,4},{6,7},{7,6},{8,9},{9,8},{10,11... | collective-permute-start | bytes 27656 | tf_op jit(solution)/shard_map/ppermute | solution.py:311
  32.6 12.4 %copy-start.1 = (f32[768]{0:T(1024)S(1)}, f32[768]{0:T(1024)}, u32[]{:S(2)}) copy-start(f32[768]{0:T(1024)} %param.4) | copy-start | bytes 9220
  35.7 18.6 %all-to-all-start.1 = ((f32[16,1,2304]{2,1,0:T(1,128)}), f32[16,1,2304]{2,1,0:T(1,128)S(1)}, u32[]{:S(2)}, u32[]{:S(2)}) async-start(f32[16,1,2304]{2,1,0:T(1,128)} %backward_kernel.2), calls=%async_computation.1 | async-start | bytes 294912 | tf_op jit(solution)/shard_map/all_to_all | solution.py:321
  57.5 16.9 %all-to-all-start.2 = ((f32[32,1,2432]{2,1,0:T(1,128)}), f32[32,1,2432]{2,1,0:T(1,128)S(1)}, u32[]{:S(2)}, u32[]{:S(2)}) async-start(f32[32,1,2432]{2,1,0:T(1,128)} %forward_kernel.1), calls=%async_computation.2 | async-start | bytes 622592 | tf_op jit(solution)/shard_map/all_to_all | solution.py:350
  61.4 4.7 %collective-permute-start.1 = (f32[1,2304]{1,0:T(1,128)S(1)}, f32[1,2304]{1,0:T(1,128)S(1)}, u32[]{:S(2)}, u32[]{:S(2)}) collective-permute-start(f32[1,2304]{1,0:T(1,128)S(1)} %multiply_add_fusion.z_ref.own_ref), channel_id=1, source_target_pairs={{0,1},{1,0},{2,3},{3,2},{4,5},{5,4},{6,7},{7,6},{8,9},{9,8},{10,11... | collective-permute-start | bytes 27656 | tf_op jit(solution)/shard_map/ppermute | solution.py:311
  77.4 14.6 %all-to-all-start.3 = ((f32[16,1,2304]{2,1,0:T(1,128)}), f32[16,1,2304]{2,1,0:T(1,128)S(1)}, u32[]{:S(2)}, u32[]{:S(2)}) async-start(f32[16,1,2304]{2,1,0:T(1,128)} %backward_kernel.3), calls=%async_computation.3 | async-start | bytes 294912 | tf_op jit(solution)/shard_map/all_to_all | solution.py:321

commit v4 on v2

--- a/solution.py
+++ b/solution.py
@@ -13,6 +13,7 @@
 F32 = jnp.float32
 BF16 = jnp.bfloat16
 VMEM = pl.BlockSpec(memory_space=pltpu.VMEM)
+HBM = pl.BlockSpec(memory_space=pltpu.HBM)
 
 
 def in_vmem(shape, dtype=F32):
@@ -106,16 +107,22 @@
             sent_ref[2 * row_index + half, :, k * W : (k + 1) * W] = forward_ref[k : k + 1, half * W : (half + 1) * W]
 
 
-def first_kernel(x_ref, a_ref, sent_ref, high_ref, low_ref, whole, x_rows, forward, sems):
+def first_kernel(x_hbm, d_ref, a_ref, sent_ref, flat_ref, diag_ref, high_ref, low_ref, whole, x_ref, x_rows, forward, sems, x_sem):
     row_index = lax.axis_index("row")
-    pieces = [pl.ds(i * CHUNK, CHUNK) for i in range(2 * W // CHUNK)]
+    pieces = [slice(i * CHUNK, (i + 1) * CHUNK) for i in range(2 * W // CHUNK)]
     copies = [pltpu.make_async_copy(a_ref.at[piece], whole.at[piece], sems.at[i]) for i, piece in enumerate(pieces)]
+    first = pltpu.make_async_copy(x_hbm, x_ref, x_sem)
+    first.start()
     for copy in copies:
         copy.start()
-    x = x_ref[...]
     x_rows[...] = jnp.zeros_like(x_rows)
-    for k, row in enumerate(rows_of(x)):
-        x_rows[k : k + 1, :] = row
+    first.wait()
+    x_rows[0:3, :] = x_ref[...]
+    for k in range(3):
+        lanes = slice(k * W, (k + 1) * W)
+        flat_ref[:, lanes] = x_ref[k : k + 1, :]
+        diag_ref[:, lanes] = d_ref[...] - SHIFT
+    x = flat_ref[...]
     for p in range(sent_ref.shape[0]):
         sent_ref[p] = x
     parts = three_parts(x_rows[...])
@@ -151,24 +158,32 @@
     col_index = lax.axis_index("col")
     home = col_index // 2 == row_index
     v_rows[...] = jnp.zeros_like(v_rows)
+    own = rows_of(own_ref[...])
+    cross = rows_of(cross_ref[...]) if cross_ref.shape[0] == 1 else [cross_ref[k : k + 1, :] for k in range(3)]
     for half in range(2):
-        mine = jnp.where(col_index % 2 == half, own_ref[...], cross_ref[...])
-        block = jnp.where(home, mine, got_ref[2 * row_index + half, :, 0:FLAT])
-        for k, row in enumerate(rows_of(block)):
-            v_rows[k : k + 1, half * W : (half + 1) * W] = row
+        sent_here = rows_of(got_ref[2 * row_index + half, :, 0:FLAT])
+        for k in range(3):
+            mine = jnp.where(col_index % 2 == half, own[k], cross[k])
+            v_rows[k : k + 1, half * W : (half + 1) * W] = jnp.where(home, mine, sent_here[k])
     parts = three_parts(v_rows[...])
     total = got_ref[0, :, 0:FLAT]
     for p in range(1, got_ref.shape[0]):
         total = total + got_ref[p, :, 0:FLAT]
     total = rows_of(jnp.where(home, total, 0.0))
-    back = 0.5 * folded(over_cols(parts, high_ref[...]) + over_cols(parts, low_ref[...]))
+    wide = over_cols(parts, high_ref[...]) + over_cols(parts, low_ref[...])
+    back = 0.5 * folded(wide)
     for k in range(3):
         part = back[k : k + 1] + total[k]
         for p in range(sent_ref.shape[0]):
             sent_ref[p, :, k * W : (k + 1) * W] = part
 
 
-def algebra_kernel(got_ref, coef_ref):
+def second_backward_kernel(got_ref, own_ref, cross_ref, high_ref, low_ref, sent_ref, coef_ref, v_rows):
+    algebra(got_ref, coef_ref)
+    backward_kernel(got_ref, own_ref, cross_ref, high_ref, low_ref, sent_ref, v_rows)
+
+
+def algebra(got_ref, coef_ref):
     tile = got_ref[0, :, FLAT:]
     for p in range(1, got_ref.shape[0]):
         tile = tile + got_ref[p, :, FLAT:]
@@ -234,8 +249,8 @@
     q2 = combine(n2, [a - b for a, b in zip(w, known)])
     root = float(M) ** 0.5
     for k in range(3):
-        out_ref[0, k : k + 1, :] = q1[k] * root
-        out_ref[1, k : k + 1, :] = q2[k] * root
+        out_ref[k, 0:1, :] = q1[k] * root
+        out_ref[k, 1:2, :] = q2[k] * root
     c0, l1 = ([[v[:, 0:1] for v in line] for line in loaded(coef_ref, i, 128)] for i in (2, 3))
     down = lax.broadcasted_iota(jnp.int32, (3, 3), 0)
     across = lax.broadcasted_iota(jnp.int32, (3, 3), 1)
@@ -248,18 +263,26 @@
         return tile
 
     second = [[c0[i][j] + d1[i][j] for j in range(3)] for i in range(3)]
-    coeffs_ref[0, 0] = square(c0, SHIFT)
-    coeffs_ref[0, 1] = square(l1, 0.0)
-    coeffs_ref[1, 0] = square(second, SHIFT)
-    coeffs_ref[1, 1] = square(l2, 0.0)
-
-
-def call(kernel, out, inputs, scratch=(), specs=None, flops=2_000_000):
+    blocks = [[square(c0, SHIFT), square(l1, 0.0)], [square(second, SHIFT), square(l2, 0.0)]]
+    for j in range(2):
+        for i in range(3):
+            for which in range(2):
+                coeffs_ref[j, i, which : which + 1, :] = blocks[j][which][i : i + 1, :]
+
+
+def collect_kernel(got_ref, d_ref, x_ref, z_ref):
+    total = got_ref[0]
+    for p in range(1, got_ref.shape[0]):
+        total = total + got_ref[p]
+    z_ref[...] = total + d_ref[...] * x_ref[...]
+
+
+def call(kernel, out, inputs, scratch=(), specs=None, out_specs=None, flops=2_000_000):
     return pl.pallas_call(
         kernel,
         out_shape=out,
         in_specs=specs or [VMEM] * len(inputs),
-        out_specs=jax.tree.map(lambda _: VMEM, out),
+        out_specs=out_specs or jax.tree.map(lambda _: VMEM, out),
         scratch_shapes=list(scratch),
         cost_estimate=pl.CostEstimate(flops=flops, bytes_accessed=100_000, transcendentals=0),
         name=kernel.__name__,
@@ -270,53 +293,54 @@
 def shards(couplings, diag_terms, start_block):
     cols = lax.axis_size("col")
     rows = lax.axis_size("row")
-    x = start_block.reshape(1, FLAT)
-    d = jnp.tile(diag_terms - SHIFT, 3).reshape(1, FLAT)
     swap = [(i, i ^ 1) for i in range(cols)]
     whole = (2 * W, W)
-    f32 = lambda *shape: jax.ShapeDtypeStruct(shape, F32)
-
-    def swapped(block):
-        return lax.ppermute(block, "col", swap)
-
-    def collect(got, own, cross):
-        sent = call(
-            backward_kernel,
-            f32(rows, 1, FLAT),
-            (got, own, cross, high, low),
-            [pltpu.VMEM((8, 2 * W), F32)],
-        )
-        return lax.all_to_all(sent, "row", 0, 0, tiled=True)
-
-    cross = swapped(x)
-    sent, high, low = call(
+    tall = pltpu.VMEM((8, 2 * W), F32)
+    short = pltpu.VMEM((8, W), F32)
+    flat = in_vmem((1, FLAT))
+
+    def stay(array):
+        return pltpu.with_memory_space_constraint(array, pltpu.HBM)
+
+    def exchanged(block, axis):
+        return lax.all_to_all(block, axis, 0, 0, tiled=True)
+
+    cross = lax.ppermute(start_block, "col", swap)
+    sent, x, d, high, low = call(
         first_kernel,
-        (f32(cols, 1, FLAT), in_vmem(whole, BF16), in_vmem(whole, BF16)),
-        (x, couplings),
+        (in_vmem((cols, 1, FLAT)), flat, flat, in_vmem(whole, BF16), in_vmem(whole, BF16)),
+        (stay(start_block), diag_terms.reshape(1, W), stay(couplings)),
         [
             pltpu.VMEM(whole, F32),
-            pltpu.VMEM((8, W), F32),
-            pltpu.VMEM((8, 2 * W), F32),
+            pltpu.VMEM((3, W), F32),
+            short,
+            tall,
             pltpu.SemaphoreType.DMA((2 * W // CHUNK,)),
+            pltpu.SemaphoreType.DMA,
         ],
-        [VMEM, pl.BlockSpec(memory_space=pl.ANY)],
+        [HBM, VMEM, HBM],
     )
-    got = lax.all_to_all(sent, "col", 0, 0, tiled=True)
-    got = collect(got, x, cross)
-    z = jnp.sum(got, axis=0) + d * x
-    cross = swapped(z)
-    sent = call(
-        forward_kernel,
-        f32(cols, 1, FLAT + 128),
-        (z, x, high, low),
-        [pltpu.VMEM((8, W), F32), pltpu.VMEM((8, 2 * W), F32)],
+    sent, cross = lax.optimization_barrier((sent, cross))
+    got = exchanged(sent, "col")
+    sent = call(backward_kernel, in_vmem((rows, 1, FLAT)), (got, x, cross, high, low), [tall])
+    got = exchanged(sent, "row")
+    z = call(collect_kernel, flat, (got, d, x))
+    cross = lax.ppermute(z, "col", swap)
+    sent = call(forward_kernel, in_vmem((cols, 1, FLAT + 128)), (z, x, high, low), [short, tall])
+    sent, cross = lax.optimization_barrier((sent, cross))
+    got = exchanged(sent, "col")
+    sent, coef = call(
+        second_backward_kernel,
+        (in_vmem((rows, 1, FLAT)), in_vmem((40, 128))),
+        (got, z, cross, high, low),
+        [tall],
     )
-    got = lax.all_to_all(sent, "col", 0, 0, tiled=True)
-    coef = call(algebra_kernel, f32(40, 128), (got,))
-    got = collect(got, z, cross)
-    sent, basis = call(residual_kernel, (f32(cols, 1, 128), f32(16, W)), (got, z, x, d, coef))
-    got = lax.all_to_all(sent, "col", 0, 0, tiled=True)
-    return call(last_kernel, (f32(2, 3, W), f32(2, 2, 3, 3)), (got, basis, coef))
+    got = exchanged(sent, "row")
+    sent, basis = call(residual_kernel, (in_vmem((cols, 1, 128)), in_vmem((16, W))), (got, z, x, d, coef))
+    got = exchanged(sent, "col")
+    f32 = lambda *shape: jax.ShapeDtypeStruct(shape, F32)
+    blocks, coeffs = call(last_kernel, (f32(3, 2, W), f32(2, 3, 2, 3)), (got, basis, coef))
+    return jnp.swapaxes(blocks, 0, 1), jnp.swapaxes(coeffs, 1, 2)
 
 
 def solution(mesh):

time: 110 us -> 104 us (0.945)
  blocking collectives: 12.2 us -> 85.3 us
  waiting for transfers between devices: 37.2 us -> 0.91 us
  starting transfers between devices: 38.3 us -> 5.93 us
  local copies, waits for them, and re-layouts: 10.7 us -> 0.69 us
    all_to_all x1 -> x5, blocking collectives: 12.2 us -> 85.3 us  [exchanged(): return lax.all_to_all(block, axis, 0, 0, tiled=True)]
    all_to_all x4 -> x0, waiting for transfers between devices: 34.1 us -> none  [the longest x2 18.5 us: collect(): return lax.all_to_all(sent, 'row', 0, 0, tiled=True)]
    all_to_all x4 -> x0, starting transfers between devices: 32 us -> none  [the longest x2 17.6 us: shards(): got = lax.all_to_all(sent, 'col', 0, 0, tiled=True)]
    unnamed x15 -> x0, local copies, waits for them, and re-layouts: 9.49 us -> none
    ppermute x2, waiting for transfers between devices: 3.11 us -> 0.91 us  [the longest x1 0.91 us: shards(): cross = lax.ppermute(z, 'col', swap)]
    pallas_call x2 -> x0, local copies, waits for them, and re-layouts: 1.21 us -> none  [call(): pl.pallas_call(kernel, out_shape=out, in_specs=specs or [VMEM] * len(inpu...]
  transfers between devices with their start and end apart: 6 -> 2, of which waited for: 6 -> 1; matrix products, arithmetic and copies ran while one was open for 0% -> 1% of each run, Pallas kernels for 0% -> 6%
where the time goes in v4:
time: 104 us; the launch traced here: 103 us
  blocking collectives  85.3 us (82%)
  Pallas kernels  9.72 us (9%)
  starting transfers between devices  5.93 us (6%)
    all_to_all x5, blocking collectives, exchanged(): return lax.all_to_all(block, axis, 0, 0, tiled=True)  85.3 us
    pallas_call x7, Pallas kernels, call(): pl.pallas_call(kernel, out_shape=out, in_specs=specs or [VMEM] * len(inpu...  9.72 us
    ppermute x1, starting transfers between devices, shards(): cross = lax.ppermute(start_block, 'col', swap)  3.94 us
  transfers between devices with their start and end apart: 2, of which 1 were waited for; matrix products, arithmetic and copies ran while one was open for 1% of the time, Pallas kernels for 6%

profile of v4, /device:TPU:1, one launch (start us, length us, event | category | flops | bytes accessed | tf_op | source)
XLA Modules:
  0.0 103.3 jit_solution(7399818448608587333)
XLA Ops:
  0.6 3.9 %collective-permute-start = (f32[3,768]{1,0:T(4,128)}, f32[3,768]{1,0:T(4,128)S(1)}, u32[]{:S(2)}, u32[]{:S(2)}) collective-permute-start(f32[3,768]{1,0:T(4,128)} %x_hbm.1), channel_id=1, source_target_pairs={{0,1},{1,0},{2,3},{3,2},{4,5},{5,4},{6,7},{7,6},{8,9},{9,8},{10,11... | collective-permute-start | bytes 27656 | tf_op jit(solution)/shard_map/ppermute | solution.py:308
  4.6 0.7 reshape.7.d_ref
  5.3 5.2 %first_kernel.1 = (f32[32,1,2304]{2,1,0:T(1,128)S(1)}, f32[1,2304]{1,0:T(1,128)S(1)}, f32[1,2304]{1,0:T(1,128)S(1)}, bf16[1536,768]{1,0:T(8,128)(2,1)S(1)}, bf16[1536,768]{1,0:T(8,128)(2,1)S(1)}) custom-call(f32[3,768]{1,0:T(4,128)} %x_hbm.1, f32[1,768]{1,0:T(1,128)S(1)} %reshape.7.d_ref, f32[1536,768]{1,0:T(8,128)} %a_ref.1), custom_call_target="tpu_custom_call" | custom-call | flops 2000000 | bytes 100000 | tf_op jit(solution)/shard_map/first_kernel/pallas_call | solution.py:281
  10.5 0.0 collective-permute-done.cross_ref
  10.5 24.2 %all_to_all.25.got_ref = f32[32,1,2304]{2,1,0:T(1,128)S(1)} all-to-all(f32[32,1,2304]{2,1,0:T(1,128)S(1)} %get-tuple-element.18), channel_id=1, replica_groups=mesh['row'=16,'col'=32] {'col'}, dimensions={0} | all-to-all | bytes 589824 | tf_op jit(solution)/shard_map/all_to_all | solution.py:306
  34.7 0.9 backward_kernel.1
  35.7 18.6 %all_to_all.26.got_ref = f32[16,1,2304]{2,1,0:T(1,128)S(1)} all-to-all(f32[16,1,2304]{2,1,0:T(1,128)S(1)} %backward_kernel.1), channel_id=1, replica_groups=mesh['row'=16,'col'=32] {'row'}, dimensions={0} | all-to-all | bytes 294912 | tf_op jit(solution)/shard_map/all_to_all | solution.py:306
  54.3 2.0 %collective-permute-start.1 = (f32[1,2304]{1,0:T(1,128)S(1)}, f32[1,2304]{1,0:T(1,128)S(1)}, u32[]{:S(2)}, u32[]{:S(2)}) collective-permute-start(f32[1,2304]{1,0:T(1,128)S(1)} %collect_kernel.1.z_ref.own_ref), channel_id=1, source_target_pairs={{0,1},{1,0},{2,3},{3,2},{4,5},{5,4},{6,7},{7,6},{8,9},{9,8},{10,11... | collective-permute-start | bytes 27656 | tf_op jit(solution)/shard_map/ppermute | solution.py:328
  56.3 1.5 %forward_kernel.1 = f32[32,1,2432]{2,1,0:T(1,128)S(1)} custom-call(f32[1,2304]{1,0:T(1,128)S(1)} %collect_kernel.1.z_ref.own_ref, f32[1,2304]{1,0:T(1,128)S(1)} %get-tuple-element.19.own_ref.x_ref, bf16[1536,768]{1,0:T(8,128)(2,1)S(1)} %get-tuple-element.21.high_ref, bf16[1536,768]{1,0:T(8,128)(2,1)S(1)} %get-tuple-element.22.low_ref), custom_call_target="tpu_custom_call" | custom-call | flops 2000000 | bytes 100000 | tf_op jit(solution)/shard_map/forward_kernel/pallas_call | solution.py:281
  57.8 0.9 collective-permute-done.1.cross_ref
  58.7 15.9 %all_to_all.27.got_ref = f32[32,1,2432]{2,1,0:T(1,128)S(1)} all-to-all(f32[32,1,2432]{2,1,0:T(1,128)S(1)} %forward_kernel.1), channel_id=1, replica_groups=mesh['row'=16,'col'=32] {'col'}, dimensions={0} | all-to-all | bytes 622592 | tf_op jit(solution)/shard_map/all_to_all | solution.py:306
  74.6 0.9 second_backward_kernel.1
  75.5 14.2 %all_to_all.28.got_ref = f32[16,1,2304]{2,1,0:T(1,128)S(1)} all-to-all(f32[16,1,2304]{2,1,0:T(1,128)S(1)} %get-tuple-element.26), channel_id=1, replica_groups=mesh['row'=16,'col'=32] {'row'}, dimensions={0} | all-to-all | bytes 294912 | tf_op jit(solution)/shard_map/all_to_all | solution.py:306
  89.7 0.3 residual_kernel.1
  90.0 12.4 %all_to_all.29.got_ref = f32[32,1,128]{2,1,0:T(1,128)S(1)} all-to-all(f32[32,1,128]{2,1,0:T(1,128)S(1)} %get-tuple-element.28), channel_id=1, replica_groups=mesh['row'=16,'col'=32] {'col'}, dimensions={0} | all-to-all | bytes 32768 | tf_op jit(solution)/shard_map/all_to_all | solution.py:306
  102.4 0.8 last_kernel.1
  (1 shorter events, 0.0 us)
Async XLA Ops:
  0.6 9.9 %collective-permute-start = (f32[3,768]{1,0:T(4,128)}, f32[3,768]{1,0:T(4,128)S(1)}, u32[]{:S(2)}, u32[]{:S(2)}) collective-permute-start(f32[3,768]{1,0:T(4,128)} %x_hbm.1), channel_id=1, source_target_pairs={{0,1},{1,0},{2,3},{3,2},{4,5},{5,4},{6,7},{7,6},{8,9},{9,8},{10,11... | collective-permute-start | bytes 27656 | tf_op jit(solution)/shard_map/ppermute | solution.py:308
  54.3 4.4 %collective-permute-start.1 = (f32[1,2304]{1,0:T(1,128)S(1)}, f32[1,2304]{1,0:T(1,128)S(1)}, u32[]{:S(2)}, u32[]{:S(2)}) collective-permute-start(f32[1,2304]{1,0:T(1,128)S(1)} %collect_kernel.1.z_ref.own_ref), channel_id=1, source_target_pairs={{0,1},{1,0},{2,3},{3,2},{4,5},{5,4},{6,7},{7,6},{8,9},{9,8},{10,11... | collective-permute-start | bytes 27656 | tf_op jit(solution)/shard_map/ppermute | solution.py:328

commit v5 on v4

--- a/solution.py
+++ b/solution.py
@@ -5,11 +5,13 @@
 from jax.experimental.pallas import tpu as pltpu
 from jax.sharding import PartitionSpec as P
 
+
 M = 24576
 SHIFT = 2.5
 W = 768
 FLAT = 3 * W
 CHUNK = 256
+DEEP = 3
 F32 = jnp.float32
 BF16 = jnp.bfloat16
 VMEM = pl.BlockSpec(memory_space=pltpu.VMEM)
@@ -53,6 +55,10 @@
     for at, value in enumerate(values):
         tile = jnp.where(lane == at, value, tile)
     return tile
+
+
+def products_of(rows):
+    return [sum(inner(a, b) for a, b in zip(rows[i], rows[j])) for i in range(6) for j in range(i, 6)]
 
 
 def unpacked(tile, count):
@@ -107,27 +113,32 @@
             sent_ref[2 * row_index + half, :, k * W : (k + 1) * W] = forward_ref[k : k + 1, half * W : (half + 1) * W]
 
 
-def first_kernel(x_hbm, d_ref, a_ref, sent_ref, flat_ref, diag_ref, high_ref, low_ref, whole, x_ref, x_rows, forward, sems, x_sem):
+def first_kernel(x_hbm, d_hbm, a_ref, sent_ref, flat_ref, diag_ref, high_ref, low_ref, whole, x_ref, d_ref, x_rows, forward, sems, x_sem, d_sem):
     row_index = lax.axis_index("row")
     pieces = [slice(i * CHUNK, (i + 1) * CHUNK) for i in range(2 * W // CHUNK)]
     copies = [pltpu.make_async_copy(a_ref.at[piece], whole.at[piece], sems.at[i]) for i, piece in enumerate(pieces)]
     first = pltpu.make_async_copy(x_hbm, x_ref, x_sem)
     first.start()
-    for copy in copies:
+    second = pltpu.make_async_copy(d_hbm, d_ref, d_sem)
+    second.start()
+    for copy in copies[:DEEP]:
         copy.start()
     x_rows[...] = jnp.zeros_like(x_rows)
     first.wait()
+    second.wait()
     x_rows[0:3, :] = x_ref[...]
     for k in range(3):
         lanes = slice(k * W, (k + 1) * W)
         flat_ref[:, lanes] = x_ref[k : k + 1, :]
-        diag_ref[:, lanes] = d_ref[...] - SHIFT
+        diag_ref[:, lanes] = d_ref[...].reshape(1, W) - SHIFT
     x = flat_ref[...]
     for p in range(sent_ref.shape[0]):
         sent_ref[p] = x
     parts = three_parts(x_rows[...])
-    for copy, piece in zip(copies, pieces):
-        copy.wait()
+    for i, piece in enumerate(pieces):
+        copies[i].wait()
+        if i + DEEP < len(copies):
+            copies[i + DEEP].start()
         block = whole[piece, :]
         high = block.astype(BF16)
         low = (block - high.astype(F32)).astype(BF16)
@@ -139,21 +150,33 @@
 
 def forward_kernel(z_ref, x_ref, high_ref, low_ref, sent_ref, z_rows, forward):
     row_index = lax.axis_index("row")
+    home = lax.axis_index("col") // 2 == row_index
     z = z_ref[...]
     z_rows[...] = jnp.zeros_like(z_rows)
     for k, row in enumerate(rows_of(z)):
         z_rows[k : k + 1, :] = row
     parts = three_parts(z_rows[...])
     six = rows_of(x_ref[...]) + rows_of(z)
-    tile = packed([inner(six[i], six[j]) for i in range(6) for j in range(i, 6)])
+    tile = packed(products_of([[row] for row in six]))
+    head = jnp.where(home, z[:, 0:128], tile)
     for p in range(sent_ref.shape[0]):
-        sent_ref[p, :, 0:FLAT] = z
-        sent_ref[p, :, FLAT:] = tile
+        sent_ref[p, :, 0:128] = head
+        sent_ref[p, :, 128:] = z[:, 128:]
     forward[...] = 0.5 * folded(over_rows(parts, high_ref[...]) + over_rows(parts, low_ref[...]))
     place(row_index, forward, sent_ref)
 
 
-def backward_kernel(got_ref, own_ref, cross_ref, high_ref, low_ref, sent_ref, v_rows):
+def first_backward_kernel(got_ref, own_ref, cross_ref, high_ref, low_ref, sent_ref, v_rows):
+    backward(got_ref, own_ref, cross_ref, high_ref, low_ref, sent_ref, v_rows)
+
+
+def second_backward_kernel(got_ref, own_ref, cross_ref, tile_ref, high_ref, low_ref, sent_ref, v_rows):
+    for p in range(sent_ref.shape[0]):
+        sent_ref[p, :, FLAT:] = tile_ref[...]
+    backward(got_ref, own_ref, cross_ref, high_ref, low_ref, sent_ref, v_rows)
+
+
+def backward(got_ref, own_ref, cross_ref, high_ref, low_ref, sent_ref, v_rows):
     row_index = lax.axis_index("row")
     col_index = lax.axis_index("col")
     home = col_index // 2 == row_index
@@ -161,14 +184,14 @@
     own = rows_of(own_ref[...])
     cross = rows_of(cross_ref[...]) if cross_ref.shape[0] == 1 else [cross_ref[k : k + 1, :] for k in range(3)]
     for half in range(2):
-        sent_here = rows_of(got_ref[2 * row_index + half, :, 0:FLAT])
+        sent_here = rows_of(got_ref[2 * row_index + half])
         for k in range(3):
             mine = jnp.where(col_index % 2 == half, own[k], cross[k])
             v_rows[k : k + 1, half * W : (half + 1) * W] = jnp.where(home, mine, sent_here[k])
     parts = three_parts(v_rows[...])
-    total = got_ref[0, :, 0:FLAT]
+    total = got_ref[0]
     for p in range(1, got_ref.shape[0]):
-        total = total + got_ref[p, :, 0:FLAT]
+        total = total + got_ref[p]
     total = rows_of(jnp.where(home, total, 0.0))
     wide = over_cols(parts, high_ref[...]) + over_cols(parts, low_ref[...])
     back = 0.5 * folded(wide)
@@ -178,15 +201,18 @@
             sent_ref[p, :, k * W : (k + 1) * W] = part
 
 
-def second_backward_kernel(got_ref, own_ref, cross_ref, high_ref, low_ref, sent_ref, coef_ref, v_rows):
-    algebra(got_ref, coef_ref)
-    backward_kernel(got_ref, own_ref, cross_ref, high_ref, low_ref, sent_ref, v_rows)
-
-
-def algebra(got_ref, coef_ref):
-    tile = got_ref[0, :, FLAT:]
-    for p in range(1, got_ref.shape[0]):
-        tile = tile + got_ref[p, :, FLAT:]
+def gram_kernel(got_ref, x_rows, tile_ref):
+    row_index = lax.axis_index("row")
+    tile = jnp.zeros((1, 128), F32)
+    for p in range(got_ref.shape[0]):
+        tile = tile + jnp.where(row_index == p // 2, 0.0, got_ref[p, :, 0:128])
+    z = [rows_of(got_ref[2 * row_index + half]) for half in range(2)]
+    rows = [[x_rows[k : k + 1, half * W : (half + 1) * W] for half in range(2)] for k in range(3)]
+    rows += [[z[half][k] for half in range(2)] for k in range(3)]
+    tile_ref[...] = tile + packed(products_of(rows))
+
+
+def algebra(tile, coef_ref):
     flat = iter(unpacked(tile, 21))
     gram = {(i, j): next(flat) for i in range(6) for j in range(i, 6)}
     g00 = symmetric([gram[i, j] for i in range(3) for j in range(i, 3)])
@@ -211,10 +237,12 @@
     return [[wide(row(9 * which + 3 * i + j)) for j in range(3)] for i in range(3)]
 
 
-def residual_kernel(got_ref, z_ref, x_ref, d_ref, coef_ref, sent_ref, basis_ref):
-    total = got_ref[0]
+def residual_kernel(got_ref, z_ref, x_ref, d_ref, sent_ref, basis_ref, coef_ref):
+    away = (lax.axis_index("col") // 2 + 1) % got_ref.shape[0]
+    algebra(got_ref[away, :, FLAT:], coef_ref)
+    total = got_ref[0, :, 0:FLAT]
     for p in range(1, got_ref.shape[0]):
-        total = total + got_ref[p]
+        total = total + got_ref[p, :, 0:FLAT]
     z = z_ref[...]
     y = rows_of(total + d_ref[...] * z)
     n0, n1, c0, l1 = (loaded(coef_ref, i, W) for i in range(4))
@@ -285,7 +313,6 @@
         out_specs=out_specs or jax.tree.map(lambda _: VMEM, out),
         scratch_shapes=list(scratch),
         cost_estimate=pl.CostEstimate(flops=flops, bytes_accessed=100_000, transcendentals=0),
-        name=kernel.__name__,
         compiler_params=pltpu.CompilerParams(vmem_limit_bytes=24 << 20),
     )(*inputs)
 
@@ -309,34 +336,41 @@
     sent, x, d, high, low = call(
         first_kernel,
         (in_vmem((cols, 1, FLAT)), flat, flat, in_vmem(whole, BF16), in_vmem(whole, BF16)),
-        (stay(start_block), diag_terms.reshape(1, W), stay(couplings)),
+        (stay(start_block), stay(diag_terms), stay(couplings)),
         [
             pltpu.VMEM(whole, F32),
             pltpu.VMEM((3, W), F32),
+            pltpu.VMEM((W,), F32),
             short,
             tall,
             pltpu.SemaphoreType.DMA((2 * W // CHUNK,)),
             pltpu.SemaphoreType.DMA,
+            pltpu.SemaphoreType.DMA,
         ],
-        [HBM, VMEM, HBM],
+        [HBM, HBM, HBM],
     )
     sent, cross = lax.optimization_barrier((sent, cross))
     got = exchanged(sent, "col")
-    sent = call(backward_kernel, in_vmem((rows, 1, FLAT)), (got, x, cross, high, low), [tall])
+    many = in_vmem((8, 2 * W))
+    sent, x_rows = call(first_backward_kernel, (in_vmem((rows, 1, FLAT)), many), (got, x, cross, high, low))
     got = exchanged(sent, "row")
     z = call(collect_kernel, flat, (got, d, x))
     cross = lax.ppermute(z, "col", swap)
-    sent = call(forward_kernel, in_vmem((cols, 1, FLAT + 128)), (z, x, high, low), [short, tall])
-    sent, cross = lax.optimization_barrier((sent, cross))
+    sent = call(forward_kernel, in_vmem((cols, 1, FLAT)), (z, x, high, low), [short, tall])
     got = exchanged(sent, "col")
-    sent, coef = call(
+    tile = call(gram_kernel, in_vmem((1, 128)), (got, x_rows))
+    sent = call(
         second_backward_kernel,
-        (in_vmem((rows, 1, FLAT)), in_vmem((40, 128))),
-        (got, z, cross, high, low),
+        in_vmem((rows, 1, FLAT + 128)),
+        (got, z, cross, tile, high, low),
         [tall],
     )
     got = exchanged(sent, "row")
-    sent, basis = call(residual_kernel, (in_vmem((cols, 1, 128)), in_vmem((16, W))), (got, z, x, d, coef))
+    sent, basis, coef = call(
+        residual_kernel,
+        (in_vmem((cols, 1, 128)), in_vmem((16, W)), in_vmem((40, 128))),
+        (got, z, x, d),
+    )
     got = exchanged(sent, "col")
     f32 = lambda *shape: jax.ShapeDtypeStruct(shape, F32)
     blocks, coeffs = call(last_kernel, (f32(3, 2, W), f32(2, 3, 2, 3)), (got, basis, coef))

time: 104 us -> 102 us (0.981)
  blocking collectives: 85.3 us -> 68.7 us
  waiting for transfers between devices: 0.91 us -> 9.61 us
  starting transfers between devices: 5.93 us -> 10.9 us
    all_to_all x5 -> x4, blocking collectives: 85.3 us -> 68.7 us  [exchanged(): return lax.all_to_all(block, axis, 0, 0, tiled=True)]
    all_to_all x0 -> x1, waiting for transfers between devices: none -> 9.61 us  [exchanged(): return lax.all_to_all(block, axis, 0, 0, tiled=True)]
    all_to_all x0 -> x1, starting transfers between devices: none -> 3.87 us  [exchanged(): return lax.all_to_all(block, axis, 0, 0, tiled=True)]
    unnamed x0 -> x4, local copies, waits for them, and re-layouts: none -> 1.66 us
    ppermute x1, starting transfers between devices: 1.99 us -> 3.13 us  [shards(): cross = lax.ppermute(z, 'col', swap)]
    pallas_call x7 -> x8, Pallas kernels: 9.72 us -> 10.1 us  [call(): pl.pallas_call(kernel, out_shape=out, in_specs=specs or [VMEM] * len(inpu...]
  transfers between devices with their start and end apart: 2 -> 3, of which waited for: 1 -> 1; matrix products, arithmetic and copies ran while one was open for 1% -> 0% of each run, Pallas kernels for 6% -> 5%
where the time goes in v5:
time: 102 us
  blocking collectives  68.7 us (67%)
  starting transfers between devices  10.9 us (11%)
  Pallas kernels  10.1 us (10%)
  waiting for transfers between devices  9.61 us (9%)
  local copies, waits for them, and re-layouts  1.66 us (2%)
    all_to_all x4, blocking collectives, exchanged(): return lax.all_to_all(block, axis, 0, 0, tiled=True)  68.7 us
    pallas_call x8, Pallas kernels, call(): pl.pallas_call(kernel, out_shape=out, in_specs=specs or [VMEM] * len(inpu...  10.1 us
    all_to_all x1, waiting for transfers between devices, exchanged(): return lax.all_to_all(block, axis, 0, 0, tiled=True)  9.61 us
    ppermute x1, starting transfers between devices, shards(): cross = lax.ppermute(start_block, 'col', swap)  3.94 us
    all_to_all x1, starting transfers between devices, exchanged(): return lax.all_to_all(block, axis, 0, 0, tiled=True)  3.87 us
    ppermute x1, starting transfers between devices, shards(): cross = lax.ppermute(z, 'col', swap)  3.13 us
  transfers between devices with their start and end apart: 3, of which 1 were waited for; matrix products, arithmetic and copies ran while one was open for 0% of the time, Pallas kernels for 5%

profile of v5, /device:TPU:1, one launch (start us, length us, event | category | flops | bytes accessed | tf_op | source)
XLA Modules:
  0.0 101.7 jit_solution(1007240430530725712)
XLA Ops:
  0.6 3.9 %collective-permute-start = (f32[3,768]{1,0:T(4,128)}, f32[3,768]{1,0:T(4,128)S(1)}, u32[]{:S(2)}, u32[]{:S(2)}) collective-permute-start(f32[3,768]{1,0:T(4,128)} %x_hbm.1), channel_id=1, source_target_pairs={{0,1},{1,0},{2,3},{3,2},{4,5},{5,4},{6,7},{7,6},{8,9},{9,8},{10,11... | collective-permute-start | bytes 27656 | tf_op jit(solution)/shard_map/ppermute | solution.py:335
  4.6 4.5 %shard_map.50 = (f32[32,1,2304]{2,1,0:T(1,128)S(1)}, f32[1,2304]{1,0:T(1,128)S(1)}, f32[1,2304]{1,0:T(1,128)S(1)}, bf16[1536,768]{1,0:T(8,128)(2,1)S(1)}, bf16[1536,768]{1,0:T(8,128)(2,1)S(1)}) custom-call(f32[3,768]{1,0:T(4,128)} %x_hbm.1, f32[768]{0:T(1024)} %d_hbm.1, f32[1536,768]{1,0:T(8,128)} %a_ref.1), custom_call_target="tpu_custom_call" | custom-call | flops 2000000 | bytes 100000 | tf_op jit(solution)/shard_map/pallas_call | solution.py:309
  9.1 0.0 copy-start
  9.1 0.0 collective-permute-done.cross_ref
  9.1 24.2 %all_to_all.25.got_ref = f32[32,1,2304]{2,1,0:T(1,128)S(1)} all-to-all(f32[32,1,2304]{2,1,0:T(1,128)S(1)} %get-tuple-element.17), channel_id=1, replica_groups=mesh['row'=16,'col'=32] {'col'}, dimensions={0} | all-to-all | bytes 589824 | tf_op jit(solution)/shard_map/all_to_all | solution.py:333
  33.3 0.9 shard_map.51
  34.3 18.6 %all_to_all.26.got_ref = f32[16,1,2304]{2,1,0:T(1,128)S(1)} all-to-all(f32[16,1,2304]{2,1,0:T(1,128)S(1)} %get-tuple-element.22), channel_id=1, replica_groups=mesh['row'=16,'col'=32] {'row'}, dimensions={0} | all-to-all | bytes 294912 | tf_op jit(solution)/shard_map/all_to_all | solution.py:333
  52.9 0.0 copy-done
  52.9 2.2 %shard_map.53 = f32[32,1,2304]{2,1,0:T(1,128)} custom-call(f32[1,2304]{1,0:T(1,128)S(1)} %shard_map.52.z_ref.own_ref, f32[1,2304]{1,0:T(1,128)S(1)} %get-tuple-element.18.own_ref.x_ref, bf16[1536,768]{1,0:T(8,128)(2,1)S(1)} %get-tuple-element.20.high_ref, bf16[1536,768]{1,0:T(8,128)(2,1)S(1)} %get-tuple-element.21.low_ref), custom_call_target="tpu_custom_call" | custom-call | flops 2000000 | bytes 100000 | tf_op jit(solution)/shard_map/pallas_call | solution.py:309
  55.1 3.9 %all-to-all-start.2 = ((f32[32,1,2304]{2,1,0:T(1,128)}), f32[32,1,2304]{2,1,0:T(1,128)S(1)}, u32[]{:S(2)}, u32[]{:S(2)}) async-start(f32[32,1,2304]{2,1,0:T(1,128)} %shard_map.53), calls=%async_computation.2 | async-start | bytes 589824 | tf_op jit(solution)/shard_map/all_to_all | solution.py:333
  59.0 3.1 %collective-permute-start.1 = (f32[1,2304]{1,0:T(1,128)S(1)}, f32[1,2304]{1,0:T(1,128)S(1)}, u32[]{:S(2)}, u32[]{:S(2)}) collective-permute-start(f32[1,2304]{1,0:T(1,128)S(1)} %shard_map.52.z_ref.own_ref), channel_id=1, source_target_pairs={{0,1},{1,0},{2,3},{3,2},{4,5},{5,4},{6,7},{7,6},{8,9},{9,8},{10,11... | collective-permute-start | bytes 27656 | tf_op jit(solution)/shard_map/ppermute | solution.py:358
  62.2 9.6 %all-to-all-done.2.got_ref = f32[32,1,2304]{2,1,0:T(1,128)S(1)} async-done(((f32[32,1,2304]{2,1,0:T(1,128)}), f32[32,1,2304]{2,1,0:T(1,128)S(1)}, u32[]{:S(2)}, u32[]{:S(2)}) %all-to-all-start.2) | async-done | bytes 294944 | tf_op jit(solution)/shard_map/all_to_all | solution.py:333
  71.8 0.2 shard_map.54.tile_ref
  72.0 0.0 collective-permute-done.1.cross_ref
  72.0 0.0 copy-start.1
  72.0 1.7 %copy-done.1 = bf16[1536,768]{1,0:T(8,128)(2,1)S(1)} copy-done((bf16[1536,768]{1,0:T(8,128)(2,1)S(1)}, bf16[1536,768]{1,0:T(8,128)(2,1)}, u32[]{:S(2)}) %copy-start.1) | copy-done | bytes 2359320
  73.6 0.9 shard_map.55
  74.6 13.8 %all_to_all.27.got_ref = f32[16,1,2432]{2,1,0:T(1,128)S(1)} all-to-all(f32[16,1,2432]{2,1,0:T(1,128)S(1)} %shard_map.55), channel_id=1, replica_groups=mesh['row'=16,'col'=32] {'row'}, dimensions={0} | all-to-all | bytes 311296 | tf_op jit(solution)/shard_map/all_to_all | solution.py:333
  88.4 0.4 shard_map.56
  88.8 12.1 %all_to_all.28.got_ref = f32[32,1,128]{2,1,0:T(1,128)S(1)} all-to-all(f32[32,1,128]{2,1,0:T(1,128)S(1)} %get-tuple-element.25), channel_id=1, replica_groups=mesh['row'=16,'col'=32] {'col'}, dimensions={0} | all-to-all | bytes 32768 | tf_op jit(solution)/shard_map/all_to_all | solution.py:333
  100.9 0.8 shard_map.57
  (1 shorter events, 0.0 us)
Async XLA Ops:
  0.6 8.5 %collective-permute-start = (f32[3,768]{1,0:T(4,128)}, f32[3,768]{1,0:T(4,128)S(1)}, u32[]{:S(2)}, u32[]{:S(2)}) collective-permute-start(f32[3,768]{1,0:T(4,128)} %x_hbm.1), channel_id=1, source_target_pairs={{0,1},{1,0},{2,3},{3,2},{4,5},{5,4},{6,7},{7,6},{8,9},{9,8},{10,11... | collective-permute-start | bytes 27656 | tf_op jit(solution)/shard_map/ppermute | solution.py:335
  9.1 43.8 %copy-start = (bf16[1536,768]{1,0:T(8,128)(2,1)}, bf16[1536,768]{1,0:T(8,128)(2,1)S(1)}, u32[]{:S(2)}) copy-start(bf16[1536,768]{1,0:T(8,128)(2,1)S(1)} %get-tuple-element.21.low_ref) | copy-start | bytes 7077892
  55.1 16.6 %all-to-all-start.2 = ((f32[32,1,2304]{2,1,0:T(1,128)}), f32[32,1,2304]{2,1,0:T(1,128)S(1)}, u32[]{:S(2)}, u32[]{:S(2)}) async-start(f32[32,1,2304]{2,1,0:T(1,128)} %shard_map.53), calls=%async_computation.2 | async-start | bytes 589824 | tf_op jit(solution)/shard_map/all_to_all | solution.py:333
  59.0 12.9 %collective-permute-start.1 = (f32[1,2304]{1,0:T(1,128)S(1)}, f32[1,2304]{1,0:T(1,128)S(1)}, u32[]{:S(2)}, u32[]{:S(2)}) collective-permute-start(f32[1,2304]{1,0:T(1,128)S(1)} %shard_map.52.z_ref.own_ref), channel_id=1, source_target_pairs={{0,1},{1,0},{2,3},{3,2},{4,5},{5,4},{6,7},{7,6},{8,9},{9,8},{10,11... | collective-permute-start | bytes 27656 | tf_op jit(solution)/shard_map/ppermute | solution.py:358
  72.0 1.7 %copy-start.1 = (bf16[1536,768]{1,0:T(8,128)(2,1)S(1)}, bf16[1536,768]{1,0:T(8,128)(2,1)}, u32[]{:S(2)}) copy-start(bf16[1536,768]{1,0:T(8,128)(2,1)} %copy-done) | copy-start | bytes 7077892

commit v6 on v5

--- a/solution.py
+++ b/solution.py
@@ -12,6 +12,7 @@
 FLAT = 3 * W
 CHUNK = 256
 DEEP = 3
+STRIP = 16
 F32 = jnp.float32
 BF16 = jnp.bfloat16
 VMEM = pl.BlockSpec(memory_space=pltpu.VMEM)
@@ -135,16 +136,22 @@
     for p in range(sent_ref.shape[0]):
         sent_ref[p] = x
     parts = three_parts(x_rows[...])
-    for i, piece in enumerate(pieces):
-        copies[i].wait()
-        if i + DEEP < len(copies):
-            copies[i + DEEP].start()
-        block = whole[piece, :]
-        high = block.astype(BF16)
-        low = (block - high.astype(F32)).astype(BF16)
-        high_ref[piece, :] = high
-        low_ref[piece, :] = low
-        forward[:, piece] = 0.5 * folded(over_rows(parts, high) + over_rows(parts, low))
+    for i in range(len(pieces) + 1):
+        if i < len(pieces):
+            piece = pieces[i]
+            copies[i].wait()
+            if i + DEEP < len(copies):
+                copies[i + DEEP].start()
+            for at in range(i * CHUNK, (i + 1) * CHUNK, STRIP):
+                strip = slice(at, at + STRIP)
+                block = whole[strip, :]
+                high = block.astype(BF16)
+                high_ref[strip, :] = high
+                low_ref[strip, :] = (block - high.astype(F32)).astype(BF16)
+        if i > 0:
+            piece = pieces[i - 1]
+            wide = over_rows(parts, high_ref[piece, :]) + over_rows(parts, low_ref[piece, :])
+            forward[:, piece] = 0.5 * folded(wide)
     place(row_index, forward, sent_ref)
 
 
@@ -166,33 +173,30 @@
     place(row_index, forward, sent_ref)
 
 
-def first_backward_kernel(got_ref, own_ref, cross_ref, high_ref, low_ref, sent_ref, v_rows):
-    backward(got_ref, own_ref, cross_ref, high_ref, low_ref, sent_ref, v_rows)
-
-
-def second_backward_kernel(got_ref, own_ref, cross_ref, tile_ref, high_ref, low_ref, sent_ref, v_rows):
+def first_backward_kernel(got_ref, own_ref, cross_ref, total_ref, high_ref, low_ref, sent_ref, v_rows):
+    backward(got_ref, own_ref, cross_ref, total_ref, high_ref, low_ref, sent_ref, v_rows)
+
+
+def second_backward_kernel(got_ref, own_ref, cross_ref, total_ref, tile_ref, high_ref, low_ref, sent_ref, v_rows):
     for p in range(sent_ref.shape[0]):
         sent_ref[p, :, FLAT:] = tile_ref[...]
-    backward(got_ref, own_ref, cross_ref, high_ref, low_ref, sent_ref, v_rows)
-
-
-def backward(got_ref, own_ref, cross_ref, high_ref, low_ref, sent_ref, v_rows):
+    backward(got_ref, own_ref, cross_ref, total_ref, high_ref, low_ref, sent_ref, v_rows)
+
+
+def backward(got_ref, own_ref, cross_ref, total_ref, high_ref, low_ref, sent_ref, v_rows):
     row_index = lax.axis_index("row")
     col_index = lax.axis_index("col")
     home = col_index // 2 == row_index
     v_rows[...] = jnp.zeros_like(v_rows)
     own = rows_of(own_ref[...])
-    cross = rows_of(cross_ref[...]) if cross_ref.shape[0] == 1 else [cross_ref[k : k + 1, :] for k in range(3)]
+    cross = rows_of(cross_ref[...])
     for half in range(2):
         sent_here = rows_of(got_ref[2 * row_index + half])
         for k in range(3):
             mine = jnp.where(col_index % 2 == half, own[k], cross[k])
             v_rows[k : k + 1, half * W : (half + 1) * W] = jnp.where(home, mine, sent_here[k])
     parts = three_parts(v_rows[...])
-    total = got_ref[0]
-    for p in range(1, got_ref.shape[0]):
-        total = total + got_ref[p]
-    total = rows_of(jnp.where(home, total, 0.0))
+    total = rows_of(total_ref[...])
     wide = over_cols(parts, high_ref[...]) + over_cols(parts, low_ref[...])
     back = 0.5 * folded(wide)
     for k in range(3):
@@ -201,7 +205,16 @@
             sent_ref[p, :, k * W : (k + 1) * W] = part
 
 
-def gram_kernel(got_ref, x_rows, tile_ref):
+def sum_kernel(got_ref, total_ref):
+    home = lax.axis_index("col") // 2 == lax.axis_index("row")
+    total = got_ref[0]
+    for p in range(1, got_ref.shape[0]):
+        total = total + got_ref[p]
+    total_ref[...] = jnp.where(home, total, 0.0)
+
+
+def gram_kernel(got_ref, x_rows, total_ref, tile_ref):
+    sum_kernel(got_ref, total_ref)
     row_index = lax.axis_index("row")
     tile = jnp.zeros((1, 128), F32)
     for p in range(got_ref.shape[0]):
@@ -332,7 +345,10 @@
     def exchanged(block, axis):
         return lax.all_to_all(block, axis, 0, 0, tiled=True)
 
-    cross = lax.ppermute(start_block, "col", swap)
+    def spread(sent, block):
+        cross = lax.ppermute(block, "col", swap)
+        return exchanged(sent, "col"), cross
+
     sent, x, d, high, low = call(
         first_kernel,
         (in_vmem((cols, 1, FLAT)), flat, flat, in_vmem(whole, BF16), in_vmem(whole, BF16)),
@@ -349,20 +365,21 @@
         ],
         [HBM, HBM, HBM],
     )
-    sent, cross = lax.optimization_barrier((sent, cross))
-    got = exchanged(sent, "col")
+    got, cross = spread(sent, x)
+    total = call(sum_kernel, flat, (got,))
     many = in_vmem((8, 2 * W))
-    sent, x_rows = call(first_backward_kernel, (in_vmem((rows, 1, FLAT)), many), (got, x, cross, high, low))
+    sent, x_rows = call(
+        first_backward_kernel, (in_vmem((rows, 1, FLAT)), many), (got, x, cross, total, high, low)
+    )
     got = exchanged(sent, "row")
     z = call(collect_kernel, flat, (got, d, x))
-    cross = lax.ppermute(z, "col", swap)
     sent = call(forward_kernel, in_vmem((cols, 1, FLAT)), (z, x, high, low), [short, tall])
-    got = exchanged(sent, "col")
-    tile = call(gram_kernel, in_vmem((1, 128)), (got, x_rows))
+    got, cross = spread(sent, z)
+    total, tile = call(gram_kernel, (flat, in_vmem((1, 128))), (got, x_rows))
     sent = call(
         second_backward_kernel,
         in_vmem((rows, 1, FLAT + 128)),
-        (got, z, cross, tile, high, low),
+        (got, z, cross, total, tile, high, low),
         [tall],
     )
     got = exchanged(sent, "row")

time: 102 us -> 103 us (level)
  blocking collectives: 68.7 us -> 44.3 us
  starting transfers between devices: 10.9 us -> 23.9 us
  waiting for transfers between devices: 9.61 us -> 18.5 us
  local copies, waits for them, and re-layouts: 1.66 us -> 4.74 us
    all_to_all x4 -> x3, blocking collectives: 68.7 us -> 44.3 us  [exchanged(): return lax.all_to_all(block, axis, 0, 0, tiled=True)]
    all_to_all x1 -> x2, starting transfers between devices: 3.87 us -> 17.6 us  [exchanged(): return lax.all_to_all(block, axis, 0, 0, tiled=True)]
    all_to_all x1 -> x2, waiting for transfers between devices: 9.61 us -> 18.5 us  [exchanged(): return lax.all_to_all(block, axis, 0, 0, tiled=True)]
    unnamed x4 -> x8, local copies, waits for them, and re-layouts: 1.66 us -> 4.74 us
    pallas_call x8 -> x9, Pallas kernels: 10.1 us -> 10.5 us  [call(): pl.pallas_call(kernel, out_shape=out, in_specs=specs or [VMEM] * len(inpu...]
  transfers between devices with their start and end apart: 3 -> 4, of which waited for: 1 -> 2; matrix products, arithmetic and copies ran while one was open for 0% -> 0% of each run, Pallas kernels for 5% -> 0%
where the time goes in v6:
time: 103 us
  blocking collectives  44.3 us (43%)
  starting transfers between devices  23.9 us (23%)
  waiting for transfers between devices  18.5 us (18%)
  Pallas kernels  10.5 us (10%)
  local copies, waits for them, and re-layouts  4.74 us (5%)
    all_to_all x3, blocking collectives, exchanged(): return lax.all_to_all(block, axis, 0, 0, tiled=True)  44.3 us
    all_to_all x2, waiting for transfers between devices, exchanged(): return lax.all_to_all(block, axis, 0, 0, tiled=True)  18.5 us
    all_to_all x2, starting transfers between devices, exchanged(): return lax.all_to_all(block, axis, 0, 0, tiled=True)  17.6 us
    pallas_call x9, Pallas kernels, call(): pl.pallas_call(kernel, out_shape=out, in_specs=specs or [VMEM] * len(inpu...  10.5 us
    ppermute x2, starting transfers between devices, spread(): cross = lax.ppermute(block, 'col', swap)  6.28 us
    unnamed x8, local copies, waits for them, and re-layouts  4.74 us
  transfers between devices with their start and end apart: 4, of which 2 were waited for; matrix products, arithmetic and copies ran while one was open for 0% of the time, Pallas kernels for 0%

profile of v6, /device:TPU:1, one launch (start us, length us, event | category | flops | bytes accessed | tf_op | source)
XLA Modules:
  0.0 102.7 jit_solution(15332275745318952447)
XLA Ops:
  0.6 5.0 %shard_map.50 = (f32[32,1,2304]{2,1,0:T(1,128)}, f32[1,2304]{1,0:T(1,128)S(1)}, f32[1,2304]{1,0:T(1,128)S(1)}, bf16[1536,768]{1,0:T(8,128)(2,1)S(1)}, bf16[1536,768]{1,0:T(8,128)(2,1)S(1)}) custom-call(f32[3,768]{1,0:T(4,128)} %x_hbm.1, f32[768]{0:T(1024)} %d_hbm.1, f32[1536,768]{1,0:T(8,128)} %a_ref.1), custom_call_target="tpu_custom_call" | custom-call | flops 2000000 | bytes 100000 | tf_op jit(solution)/shard_map/pallas_call | solution.py:322
  5.6 0.0 copy-start
  5.6 1.4 %copy-done = bf16[1536,768]{1,0:T(8,128)(2,1)} copy-done((bf16[1536,768]{1,0:T(8,128)(2,1)}, bf16[1536,768]{1,0:T(8,128)(2,1)S(1)}, u32[]{:S(2)}) %copy-start) | copy-done | bytes 2359320
  7.0 13.7 %all-to-all-start = ((f32[32,1,2304]{2,1,0:T(1,128)}), f32[32,1,2304]{2,1,0:T(1,128)S(1)}, u32[]{:S(2)}, u32[]{:S(2)}) async-start(f32[32,1,2304]{2,1,0:T(1,128)} %get-tuple-element.16), calls=%async_computation | async-start | bytes 589824 | tf_op jit(solution)/shard_map/all_to_all | solution.py:346
  20.7 3.1 %collective-permute-start = (f32[1,2304]{1,0:T(1,128)S(1)}, f32[1,2304]{1,0:T(1,128)S(1)}, u32[]{:S(2)}, u32[]{:S(2)}) collective-permute-start(f32[1,2304]{1,0:T(1,128)S(1)} %get-tuple-element.17.own_ref.x_ref), channel_id=1, source_target_pairs={{0,1},{1,0},{2,3},{3,2},{4,5},{5,4},{6,7},{7,6},{8,9},{9,8},{10,11... | collective-permute-start | bytes 27656 | tf_op jit(solution)/shard_map/ppermute | solution.py:349
  23.9 8.9 %all-to-all-done.got_ref = f32[32,1,2304]{2,1,0:T(1,128)S(1)} async-done(((f32[32,1,2304]{2,1,0:T(1,128)}), f32[32,1,2304]{2,1,0:T(1,128)S(1)}, u32[]{:S(2)}, u32[]{:S(2)}) %all-to-all-start) | async-done | bytes 294944 | tf_op jit(solution)/shard_map/all_to_all | solution.py:346
  32.8 0.0 collective-permute-done.cross_ref
  32.8 0.0 copy-start.1
  32.8 1.7 %copy-done.1 = bf16[1536,768]{1,0:T(8,128)(2,1)S(1)} copy-done((bf16[1536,768]{1,0:T(8,128)(2,1)S(1)}, bf16[1536,768]{1,0:T(8,128)(2,1)}, u32[]{:S(2)}) %copy-start.1) | copy-done | bytes 2359320
  34.5 0.0 copy-start.2
  34.5 0.9 shard_map.52
  35.4 18.4 %all_to_all.25.got_ref = f32[16,1,2304]{2,1,0:T(1,128)S(1)} all-to-all(f32[16,1,2304]{2,1,0:T(1,128)S(1)} %get-tuple-element.20), channel_id=1, replica_groups=mesh['row'=16,'col'=32] {'row'}, dimensions={0} | all-to-all | bytes 294912 | tf_op jit(solution)/shard_map/all_to_all | solution.py:346
  53.8 0.0 copy-done.2
  53.8 2.2 %shard_map.54 = f32[32,1,2304]{2,1,0:T(1,128)} custom-call(f32[1,2304]{1,0:T(1,128)S(1)} %shard_map.53.z_ref.own_ref, f32[1,2304]{1,0:T(1,128)S(1)} %get-tuple-element.17.own_ref.x_ref, bf16[1536,768]{1,0:T(8,128)(2,1)S(1)} %get-tuple-element.18.high_ref, bf16[1536,768]{1,0:T(8,128)(2,1)S(1)} %copy-done.2), custom_call_target="tpu_custom_call" | custom-call | flops 2000000 | bytes 100000 | tf_op jit(solution)/shard_map/pallas_call | solution.py:322
  56.0 3.9 %all-to-all-start.2 = ((f32[32,1,2304]{2,1,0:T(1,128)}), f32[32,1,2304]{2,1,0:T(1,128)S(1)}, u32[]{:S(2)}, u32[]{:S(2)}) async-start(f32[32,1,2304]{2,1,0:T(1,128)} %shard_map.54), calls=%async_computation.2 | async-start | bytes 589824 | tf_op jit(solution)/shard_map/all_to_all | solution.py:346
  60.0 3.1 %collective-permute-start.1 = (f32[1,2304]{1,0:T(1,128)S(1)}, f32[1,2304]{1,0:T(1,128)S(1)}, u32[]{:S(2)}, u32[]{:S(2)}) collective-permute-start(f32[1,2304]{1,0:T(1,128)S(1)} %shard_map.53.z_ref.own_ref), channel_id=1, source_target_pairs={{0,1},{1,0},{2,3},{3,2},{4,5},{5,4},{6,7},{7,6},{8,9},{9,8},{10,11... | collective-permute-start | bytes 27656 | tf_op jit(solution)/shard_map/ppermute | solution.py:349
  63.1 9.6 %all-to-all-done.2.got_ref = f32[32,1,2304]{2,1,0:T(1,128)S(1)} async-done(((f32[32,1,2304]{2,1,0:T(1,128)}), f32[32,1,2304]{2,1,0:T(1,128)S(1)}, u32[]{:S(2)}, u32[]{:S(2)}) %all-to-all-start.2) | async-done | bytes 294944 | tf_op jit(solution)/shard_map/all_to_all | solution.py:346
  72.7 0.2 shard_map.55
  72.9 0.0 collective-permute-done.1.cross_ref
  72.9 0.0 copy-start.3
  72.9 1.7 %copy-done.3 = bf16[1536,768]{1,0:T(8,128)(2,1)S(1)} copy-done((bf16[1536,768]{1,0:T(8,128)(2,1)S(1)}, bf16[1536,768]{1,0:T(8,128)(2,1)}, u32[]{:S(2)}) %copy-start.3) | copy-done | bytes 2359320
  74.6 0.9 shard_map.56
  75.5 13.8 %all_to_all.26.got_ref = f32[16,1,2432]{2,1,0:T(1,128)S(1)} all-to-all(f32[16,1,2432]{2,1,0:T(1,128)S(1)} %shard_map.56), channel_id=1, replica_groups=mesh['row'=16,'col'=32] {'row'}, dimensions={0} | all-to-all | bytes 311296 | tf_op jit(solution)/shard_map/all_to_all | solution.py:346
  89.3 0.4 shard_map.57
  89.8 12.1 %all_to_all.27.got_ref = f32[32,1,128]{2,1,0:T(1,128)S(1)} all-to-all(f32[32,1,128]{2,1,0:T(1,128)S(1)} %get-tuple-element.25), channel_id=1, replica_groups=mesh['row'=16,'col'=32] {'col'}, dimensions={0} | all-to-all | bytes 32768 | tf_op jit(solution)/shard_map/all_to_all | solution.py:346
  101.9 0.8 shard_map.58
  (2 shorter events, 0.1 us)
Async XLA Ops:
  5.6 1.4 %copy-start = (bf16[1536,768]{1,0:T(8,128)(2,1)}, bf16[1536,768]{1,0:T(8,128)(2,1)S(1)}, u32[]{:S(2)}) copy-start(bf16[1536,768]{1,0:T(8,128)(2,1)S(1)} %get-tuple-element.19.low_ref) | copy-start | bytes 7077892
  7.0 25.7 %all-to-all-start = ((f32[32,1,2304]{2,1,0:T(1,128)}), f32[32,1,2304]{2,1,0:T(1,128)S(1)}, u32[]{:S(2)}, u32[]{:S(2)}) async-start(f32[32,1,2304]{2,1,0:T(1,128)} %get-tuple-element.16), calls=%async_computation | async-start | bytes 589824 | tf_op jit(solution)/shard_map/all_to_all | solution.py:346
  20.7 12.1 %collective-permute-start = (f32[1,2304]{1,0:T(1,128)S(1)}, f32[1,2304]{1,0:T(1,128)S(1)}, u32[]{:S(2)}, u32[]{:S(2)}) collective-permute-start(f32[1,2304]{1,0:T(1,128)S(1)} %get-tuple-element.17.own_ref.x_ref), channel_id=1, source_target_pairs={{0,1},{1,0},{2,3},{3,2},{4,5},{5,4},{6,7},{7,6},{8,9},{9,8},{10,11... | collective-permute-start | bytes 27656 | tf_op jit(solution)/shard_map/ppermute | solution.py:349
  32.8 1.7 %copy-start.1 = (bf16[1536,768]{1,0:T(8,128)(2,1)S(1)}, bf16[1536,768]{1,0:T(8,128)(2,1)}, u32[]{:S(2)}) copy-start(bf16[1536,768]{1,0:T(8,128)(2,1)} %copy-done) | copy-start | bytes 7077892
  34.5 19.3 %copy-start.2 = (bf16[1536,768]{1,0:T(8,128)(2,1)S(1)}, bf16[1536,768]{1,0:T(8,128)(2,1)}, u32[]{:S(2)}) copy-start(bf16[1536,768]{1,0:T(8,128)(2,1)} %copy-done) | copy-start | bytes 7077892
  56.0 16.7 %all-to-all-start.2 = ((f32[32,1,2304]{2,1,0:T(1,128)}), f32[32,1,2304]{2,1,0:T(1,128)S(1)}, u32[]{:S(2)}, u32[]{:S(2)}) async-start(f32[32,1,2304]{2,1,0:T(1,128)} %shard_map.54), calls=%async_computation.2 | async-start | bytes 589824 | tf_op jit(solution)/shard_map/all_to_all | solution.py:346
  60.0 12.9 %collective-permute-start.1 = (f32[1,2304]{1,0:T(1,128)S(1)}, f32[1,2304]{1,0:T(1,128)S(1)}, u32[]{:S(2)}, u32[]{:S(2)}) collective-permute-start(f32[1,2304]{1,0:T(1,128)S(1)} %shard_map.53.z_ref.own_ref), channel_id=1, source_target_pairs={{0,1},{1,0},{2,3},{3,2},{4,5},{5,4},{6,7},{7,6},{8,9},{9,8},{10,11... | collective-permute-start | bytes 27656 | tf_op jit(solution)/shard_map/ppermute | solution.py:349
  72.9 1.7 %copy-start.3 = (bf16[1536,768]{1,0:T(8,128)(2,1)S(1)}, bf16[1536,768]{1,0:T(8,128)(2,1)}, u32[]{:S(2)}) copy-start(bf16[1536,768]{1,0:T(8,128)(2,1)} %copy-done) | copy-start | bytes 7077892

commit v7 on v6

--- a/solution.py
+++ b/solution.py
@@ -10,8 +10,7 @@
 SHIFT = 2.5
 W = 768
 FLAT = 3 * W
-CHUNK = 256
-DEEP = 3
+CHUNK = 512
 STRIP = 16
 F32 = jnp.float32
 BF16 = jnp.bfloat16
@@ -114,44 +113,37 @@
             sent_ref[2 * row_index + half, :, k * W : (k + 1) * W] = forward_ref[k : k + 1, half * W : (half + 1) * W]
 
 
-def first_kernel(x_hbm, d_hbm, a_ref, sent_ref, flat_ref, diag_ref, high_ref, low_ref, whole, x_ref, d_ref, x_rows, forward, sems, x_sem, d_sem):
-    row_index = lax.axis_index("row")
-    pieces = [slice(i * CHUNK, (i + 1) * CHUNK) for i in range(2 * W // CHUNK)]
-    copies = [pltpu.make_async_copy(a_ref.at[piece], whole.at[piece], sems.at[i]) for i, piece in enumerate(pieces)]
+def prepare_kernel(x_hbm, d_hbm, flat_ref, diag_ref, rows_ref, x_ref, d_ref, x_sem, d_sem):
     first = pltpu.make_async_copy(x_hbm, x_ref, x_sem)
+    second = pltpu.make_async_copy(d_hbm, d_ref, d_sem)
     first.start()
-    second = pltpu.make_async_copy(d_hbm, d_ref, d_sem)
     second.start()
-    for copy in copies[:DEEP]:
-        copy.start()
-    x_rows[...] = jnp.zeros_like(x_rows)
+    rows_ref[...] = jnp.zeros_like(rows_ref)
     first.wait()
     second.wait()
-    x_rows[0:3, :] = x_ref[...]
+    rows_ref[0:3, :] = x_ref[...]
     for k in range(3):
         lanes = slice(k * W, (k + 1) * W)
         flat_ref[:, lanes] = x_ref[k : k + 1, :]
         diag_ref[:, lanes] = d_ref[...].reshape(1, W) - SHIFT
-    x = flat_ref[...]
+
+
+def first_kernel(x_ref, rows_ref, a_ref, sent_ref, high_ref, low_ref, forward):
+    row_index = lax.axis_index("row")
+    x = x_ref[...]
     for p in range(sent_ref.shape[0]):
         sent_ref[p] = x
-    parts = three_parts(x_rows[...])
-    for i in range(len(pieces) + 1):
-        if i < len(pieces):
-            piece = pieces[i]
-            copies[i].wait()
-            if i + DEEP < len(copies):
-                copies[i + DEEP].start()
-            for at in range(i * CHUNK, (i + 1) * CHUNK, STRIP):
-                strip = slice(at, at + STRIP)
-                block = whole[strip, :]
-                high = block.astype(BF16)
-                high_ref[strip, :] = high
-                low_ref[strip, :] = (block - high.astype(F32)).astype(BF16)
-        if i > 0:
-            piece = pieces[i - 1]
-            wide = over_rows(parts, high_ref[piece, :]) + over_rows(parts, low_ref[piece, :])
-            forward[:, piece] = 0.5 * folded(wide)
+    parts = three_parts(rows_ref[...])
+    for start in range(0, 2 * W, CHUNK):
+        piece = slice(start, start + CHUNK)
+        for at in range(start, start + CHUNK, STRIP):
+            strip = slice(at, at + STRIP)
+            block = a_ref[strip, :]
+            high = block.astype(BF16)
+            high_ref[strip, :] = high
+            low_ref[strip, :] = (block - high.astype(F32)).astype(BF16)
+        wide = over_rows(parts, high_ref[piece, :]) + over_rows(parts, low_ref[piece, :])
+        forward[:, piece] = 0.5 * folded(wide)
     place(row_index, forward, sent_ref)
 
 
@@ -349,23 +341,22 @@
         cross = lax.ppermute(block, "col", swap)
         return exchanged(sent, "col"), cross
 
-    sent, x, d, high, low = call(
+    x, d, x_eight = call(
+        prepare_kernel,
+        (flat, flat, in_vmem((8, W))),
+        (stay(start_block), stay(diag_terms)),
+        [pltpu.VMEM((3, W), F32), pltpu.VMEM((W,), F32), pltpu.SemaphoreType.DMA, pltpu.SemaphoreType.DMA],
+        [HBM, HBM],
+        flops=5_000_000_000,
+    )
+    cross = lax.ppermute(x, "col", swap)
+    sent, high, low = call(
         first_kernel,
-        (in_vmem((cols, 1, FLAT)), flat, flat, in_vmem(whole, BF16), in_vmem(whole, BF16)),
-        (stay(start_block), stay(diag_terms), stay(couplings)),
-        [
-            pltpu.VMEM(whole, F32),
-            pltpu.VMEM((3, W), F32),
-            pltpu.VMEM((W,), F32),
-            short,
-            tall,
-            pltpu.SemaphoreType.DMA((2 * W // CHUNK,)),
-            pltpu.SemaphoreType.DMA,
-            pltpu.SemaphoreType.DMA,
-        ],
-        [HBM, HBM, HBM],
-    )
-    got, cross = spread(sent, x)
+        (in_vmem((cols, 1, FLAT)), in_vmem(whole, BF16), in_vmem(whole, BF16)),
+        (x, x_eight, couplings),
+        [tall],
+    )
+    got = exchanged(sent, "col")
     total = call(sum_kernel, flat, (got,))
     many = in_vmem((8, 2 * W))
     sent, x_rows = call(

time: 103 us -> 103 us (level)
  Pallas kernels: 10.5 us -> 8.87 us
  local copies, waits for them, and re-layouts: 4.74 us -> 6.23 us
    ppermute x2 -> x1, starting transfers between devices: 6.28 us -> 3.14 us  [spread(): cross = lax.ppermute(block, 'col', swap)]
    ppermute x0 -> x1, starting transfers between devices: none -> 3.14 us  [shards(): cross = lax.ppermute(x, 'col', swap)]
    pallas_call x9 -> x10, Pallas kernels: 10.5 us -> 8.87 us  [call(): pl.pallas_call(kernel, out_shape=out, in_specs=specs or [VMEM] * len(inpu...]
    unnamed x8 -> x10, local copies, waits for them, and re-layouts: 4.74 us -> 6.23 us
where the time goes in v7:
time: 103 us; the launch traced here: 102 us
  blocking collectives  44.3 us (43%)
  starting transfers between devices  23.9 us (23%)
  waiting for transfers between devices  18.5 us (18%)
  Pallas kernels  8.87 us (9%)
  local copies, waits for them, and re-layouts  6.23 us (6%)
    all_to_all x3, blocking collectives, exchanged(): return lax.all_to_all(block, axis, 0, 0, tiled=True)  44.3 us
    all_to_all x2, waiting for transfers between devices, exchanged(): return lax.all_to_all(block, axis, 0, 0, tiled=True)  18.5 us
    all_to_all x2, starting transfers between devices, exchanged(): return lax.all_to_all(block, axis, 0, 0, tiled=True)  17.6 us
    pallas_call x10, Pallas kernels, call(): pl.pallas_call(kernel, out_shape=out, in_specs=specs or [VMEM] * len(inpu...  8.87 us
    unnamed x10, local copies, waits for them, and re-layouts  6.23 us
    ppermute x1, starting transfers between devices, spread(): cross = lax.ppermute(block, 'col', swap)  3.14 us
    ppermute x1, starting transfers between devices, shards(): cross = lax.ppermute(x, 'col', swap)  3.14 us
  transfers between devices with their start and end apart: 4, of which 2 were waited for; matrix products, arithmetic and copies ran while one was open for 0% of the time, Pallas kernels for 0%

profile of v7, /device:TPU:1, one launch (start us, length us, event | category | flops | bytes accessed | tf_op | source)
XLA Modules:
  0.0 102.5 jit_solution(5565488363535108192)
XLA Ops:
  0.6 0.0 copy-start.4
  0.6 0.9 shard_map.50
  1.5 1.5 %copy-done.4 = f32[1536,768]{1,0:T(8,128)S(1)} copy-done((f32[1536,768]{1,0:T(8,128)S(1)}, f32[1536,768]{1,0:T(8,128)}, u32[]{:S(2)}) %copy-start.4) | copy-done | bytes 4718616
  3.0 2.4 %shard_map.51 = (f32[32,1,2304]{2,1,0:T(1,128)}, bf16[1536,768]{1,0:T(8,128)(2,1)S(1)}, bf16[1536,768]{1,0:T(8,128)(2,1)S(1)}) custom-call(f32[1,2304]{1,0:T(1,128)S(1)} %get-tuple-element.17.x_ref.own_ref, f32[8,768]{1,0:T(8,128)S(1)} %get-tuple-element.18.rows_ref, f32[1536,768]{1,0:T(8,128)S(1)} %copy-done.4), custom_call_target="tpu_custom_call" | custom-call | flops 2000000 | bytes 100000 | tf_op jit(solution)/shard_map/pallas_call | solution.py:314
  5.4 0.0 copy-start
  5.4 1.4 %copy-done = bf16[1536,768]{1,0:T(8,128)(2,1)} copy-done((bf16[1536,768]{1,0:T(8,128)(2,1)}, bf16[1536,768]{1,0:T(8,128)(2,1)S(1)}, u32[]{:S(2)}) %copy-start) | copy-done | bytes 2359320
  6.9 13.7 %all-to-all-start = ((f32[32,1,2304]{2,1,0:T(1,128)}), f32[32,1,2304]{2,1,0:T(1,128)S(1)}, u32[]{:S(2)}, u32[]{:S(2)}) async-start(f32[32,1,2304]{2,1,0:T(1,128)} %get-tuple-element.19), calls=%async_computation | async-start | bytes 589824 | tf_op jit(solution)/shard_map/all_to_all | solution.py:338
  20.6 3.1 %collective-permute-start = (f32[1,2304]{1,0:T(1,128)S(1)}, f32[1,2304]{1,0:T(1,128)S(1)}, u32[]{:S(2)}, u32[]{:S(2)}) collective-permute-start(f32[1,2304]{1,0:T(1,128)S(1)} %get-tuple-element.17.x_ref.own_ref), channel_id=1, source_target_pairs={{0,1},{1,0},{2,3},{3,2},{4,5},{5,4},{6,7},{7,6},{8,9},{9,8},{10,11... | collective-permute-start | bytes 27656 | tf_op jit(solution)/shard_map/ppermute | solution.py:352
  23.7 8.9 %all-to-all-done.got_ref = f32[32,1,2304]{2,1,0:T(1,128)S(1)} async-done(((f32[32,1,2304]{2,1,0:T(1,128)}), f32[32,1,2304]{2,1,0:T(1,128)S(1)}, u32[]{:S(2)}, u32[]{:S(2)}) %all-to-all-start) | async-done | bytes 294944 | tf_op jit(solution)/shard_map/all_to_all | solution.py:338
  32.6 0.0 collective-permute-done.cross_ref
  32.6 0.0 copy-start.1
  32.7 1.7 %copy-done.1 = bf16[1536,768]{1,0:T(8,128)(2,1)S(1)} copy-done((bf16[1536,768]{1,0:T(8,128)(2,1)S(1)}, bf16[1536,768]{1,0:T(8,128)(2,1)}, u32[]{:S(2)}) %copy-start.1) | copy-done | bytes 2359320
  34.3 0.0 copy-start.2
  34.3 0.9 shard_map.53
  35.3 18.4 %all_to_all.25.got_ref = f32[16,1,2304]{2,1,0:T(1,128)S(1)} all-to-all(f32[16,1,2304]{2,1,0:T(1,128)S(1)} %get-tuple-element.22), channel_id=1, replica_groups=mesh['row'=16,'col'=32] {'row'}, dimensions={0} | all-to-all | bytes 294912 | tf_op jit(solution)/shard_map/all_to_all | solution.py:338
  53.6 0.0 copy-done.2
  53.6 2.2 %shard_map.55 = f32[32,1,2304]{2,1,0:T(1,128)} custom-call(f32[1,2304]{1,0:T(1,128)S(1)} %shard_map.54.z_ref.own_ref, f32[1,2304]{1,0:T(1,128)S(1)} %get-tuple-element.17.x_ref.own_ref, bf16[1536,768]{1,0:T(8,128)(2,1)S(1)} %get-tuple-element.20.high_ref, bf16[1536,768]{1,0:T(8,128)(2,1)S(1)} %copy-done.2), custom_call_target="tpu_custom_call" | custom-call | flops 2000000 | bytes 100000 | tf_op jit(solution)/shard_map/pallas_call | solution.py:314
  55.9 3.9 %all-to-all-start.2 = ((f32[32,1,2304]{2,1,0:T(1,128)}), f32[32,1,2304]{2,1,0:T(1,128)S(1)}, u32[]{:S(2)}, u32[]{:S(2)}) async-start(f32[32,1,2304]{2,1,0:T(1,128)} %shard_map.55), calls=%async_computation.2 | async-start | bytes 589824 | tf_op jit(solution)/shard_map/all_to_all | solution.py:338
  59.8 3.1 %collective-permute-start.1 = (f32[1,2304]{1,0:T(1,128)S(1)}, f32[1,2304]{1,0:T(1,128)S(1)}, u32[]{:S(2)}, u32[]{:S(2)}) collective-permute-start(f32[1,2304]{1,0:T(1,128)S(1)} %shard_map.54.z_ref.own_ref), channel_id=1, source_target_pairs={{0,1},{1,0},{2,3},{3,2},{4,5},{5,4},{6,7},{7,6},{8,9},{9,8},{10,11... | collective-permute-start | bytes 27656 | tf_op jit(solution)/shard_map/ppermute | solution.py:341
  62.9 9.6 %all-to-all-done.2.got_ref = f32[32,1,2304]{2,1,0:T(1,128)S(1)} async-done(((f32[32,1,2304]{2,1,0:T(1,128)}), f32[32,1,2304]{2,1,0:T(1,128)S(1)}, u32[]{:S(2)}, u32[]{:S(2)}) %all-to-all-start.2) | async-done | bytes 294944 | tf_op jit(solution)/shard_map/all_to_all | solution.py:338
  72.5 0.2 shard_map.56
  72.7 0.0 collective-permute-done.1.cross_ref
  72.7 0.0 copy-start.3
  72.7 1.7 %copy-done.3 = bf16[1536,768]{1,0:T(8,128)(2,1)S(1)} copy-done((bf16[1536,768]{1,0:T(8,128)(2,1)S(1)}, bf16[1536,768]{1,0:T(8,128)(2,1)}, u32[]{:S(2)}) %copy-start.3) | copy-done | bytes 2359320
  74.4 0.9 shard_map.57
  75.3 13.8 %all_to_all.26.got_ref = f32[16,1,2432]{2,1,0:T(1,128)S(1)} all-to-all(f32[16,1,2432]{2,1,0:T(1,128)S(1)} %shard_map.57), channel_id=1, replica_groups=mesh['row'=16,'col'=32] {'row'}, dimensions={0} | all-to-all | bytes 311296 | tf_op jit(solution)/shard_map/all_to_all | solution.py:338
  89.2 0.4 shard_map.58
  89.6 12.1 %all_to_all.27.got_ref = f32[32,1,128]{2,1,0:T(1,128)S(1)} all-to-all(f32[32,1,128]{2,1,0:T(1,128)S(1)} %get-tuple-element.27), channel_id=1, replica_groups=mesh['row'=16,'col'=32] {'col'}, dimensions={0} | all-to-all | bytes 32768 | tf_op jit(solution)/shard_map/all_to_all | solution.py:338
  101.7 0.8 shard_map.59
  (2 shorter events, 0.1 us)
Async XLA Ops:
  0.6 2.4 %copy-start.4 = (f32[1536,768]{1,0:T(8,128)S(1)}, f32[1536,768]{1,0:T(8,128)}, u32[]{:S(2)}) copy-start(f32[1536,768]{1,0:T(8,128)} %a_ref.1) | copy-start | bytes 14155780
  5.4 1.4 %copy-start = (bf16[1536,768]{1,0:T(8,128)(2,1)}, bf16[1536,768]{1,0:T(8,128)(2,1)S(1)}, u32[]{:S(2)}) copy-start(bf16[1536,768]{1,0:T(8,128)(2,1)S(1)} %get-tuple-element.21.low_ref) | copy-start | bytes 7077892
  6.9 25.7 %all-to-all-start = ((f32[32,1,2304]{2,1,0:T(1,128)}), f32[32,1,2304]{2,1,0:T(1,128)S(1)}, u32[]{:S(2)}, u32[]{:S(2)}) async-start(f32[32,1,2304]{2,1,0:T(1,128)} %get-tuple-element.19), calls=%async_computation | async-start | bytes 589824 | tf_op jit(solution)/shard_map/all_to_all | solution.py:338
  20.6 12.1 %collective-permute-start = (f32[1,2304]{1,0:T(1,128)S(1)}, f32[1,2304]{1,0:T(1,128)S(1)}, u32[]{:S(2)}, u32[]{:S(2)}) collective-permute-start(f32[1,2304]{1,0:T(1,128)S(1)} %get-tuple-element.17.x_ref.own_ref), channel_id=1, source_target_pairs={{0,1},{1,0},{2,3},{3,2},{4,5},{5,4},{6,7},{7,6},{8,9},{9,8},{10,11... | collective-permute-start | bytes 27656 | tf_op jit(solution)/shard_map/ppermute | solution.py:352
  32.6 1.7 %copy-start.1 = (bf16[1536,768]{1,0:T(8,128)(2,1)S(1)}, bf16[1536,768]{1,0:T(8,128)(2,1)}, u32[]{:S(2)}) copy-start(bf16[1536,768]{1,0:T(8,128)(2,1)} %copy-done) | copy-start | bytes 7077892
  34.3 19.3 %copy-start.2 = (bf16[1536,768]{1,0:T(8,128)(2,1)S(1)}, bf16[1536,768]{1,0:T(8,128)(2,1)}, u32[]{:S(2)}) copy-start(bf16[1536,768]{1,0:T(8,128)(2,1)} %copy-done) | copy-start | bytes 7077892
  55.9 16.7 %all-to-all-start.2 = ((f32[32,1,2304]{2,1,0:T(1,128)}), f32[32,1,2304]{2,1,0:T(1,128)S(1)}, u32[]{:S(2)}, u32[]{:S(2)}) async-start(f32[32,1,2304]{2,1,0:T(1,128)} %shard_map.55), calls=%async_computation.2 | async-start | bytes 589824 | tf_op jit(solution)/shard_map/all_to_all | solution.py:338
  59.8 12.9 %collective-permute-start.1 = (f32[1,2304]{1,0:T(1,128)S(1)}, f32[1,2304]{1,0:T(1,128)S(1)}, u32[]{:S(2)}, u32[]{:S(2)}) collective-permute-start(f32[1,2304]{1,0:T(1,128)S(1)} %shard_map.54.z_ref.own_ref), channel_id=1, source_target_pairs={{0,1},{1,0},{2,3},{3,2},{4,5},{5,4},{6,7},{7,6},{8,9},{9,8},{10,11... | collective-permute-start | bytes 27656 | tf_op jit(solution)/shard_map/ppermute | solution.py:341
  72.7 1.7 %copy-start.3 = (bf16[1536,768]{1,0:T(8,128)(2,1)S(1)}, bf16[1536,768]{1,0:T(8,128)(2,1)}, u32[]{:S(2)}) copy-start(bf16[1536,768]{1,0:T(8,128)(2,1)} %copy-done) | copy-start | bytes 7077892

commit v8 on v7

--- a/solution.py
+++ b/solution.py
@@ -15,7 +15,6 @@
 F32 = jnp.float32
 BF16 = jnp.bfloat16
 VMEM = pl.BlockSpec(memory_space=pltpu.VMEM)
-HBM = pl.BlockSpec(memory_space=pltpu.HBM)
 
 
 def in_vmem(shape, dtype=F32):
@@ -113,27 +112,22 @@
             sent_ref[2 * row_index + half, :, k * W : (k + 1) * W] = forward_ref[k : k + 1, half * W : (half + 1) * W]
 
 
-def prepare_kernel(x_hbm, d_hbm, flat_ref, diag_ref, rows_ref, x_ref, d_ref, x_sem, d_sem):
-    first = pltpu.make_async_copy(x_hbm, x_ref, x_sem)
-    second = pltpu.make_async_copy(d_hbm, d_ref, d_sem)
-    first.start()
-    second.start()
-    rows_ref[...] = jnp.zeros_like(rows_ref)
-    first.wait()
-    second.wait()
-    rows_ref[0:3, :] = x_ref[...]
+def opening_kernel(mark_ref):
+    mark_ref[...] = jnp.zeros_like(mark_ref)
+
+
+def first_kernel(x_ref, d_ref, a_ref, mark_ref, sent_ref, flat_ref, diag_ref, high_ref, low_ref, x_rows, forward):
+    row_index = lax.axis_index("row")
+    x_rows[...] = jnp.zeros_like(x_rows)
+    x_rows[0:3, :] = x_ref[...]
     for k in range(3):
         lanes = slice(k * W, (k + 1) * W)
         flat_ref[:, lanes] = x_ref[k : k + 1, :]
         diag_ref[:, lanes] = d_ref[...].reshape(1, W) - SHIFT
-
-
-def first_kernel(x_ref, rows_ref, a_ref, sent_ref, high_ref, low_ref, forward):
-    row_index = lax.axis_index("row")
-    x = x_ref[...]
+    x = flat_ref[...]
     for p in range(sent_ref.shape[0]):
         sent_ref[p] = x
-    parts = three_parts(rows_ref[...])
+    parts = three_parts(x_rows[...])
     for start in range(0, 2 * W, CHUNK):
         piece = slice(start, start + CHUNK)
         for at in range(start, start + CHUNK, STRIP):
@@ -181,7 +175,7 @@
     home = col_index // 2 == row_index
     v_rows[...] = jnp.zeros_like(v_rows)
     own = rows_of(own_ref[...])
-    cross = rows_of(cross_ref[...])
+    cross = rows_of(cross_ref[...]) if cross_ref.shape[0] == 1 else [cross_ref[k : k + 1, :] for k in range(3)]
     for half in range(2):
         sent_here = rows_of(got_ref[2 * row_index + half])
         for k in range(3):
@@ -331,9 +325,6 @@
     short = pltpu.VMEM((8, W), F32)
     flat = in_vmem((1, FLAT))
 
-    def stay(array):
-        return pltpu.with_memory_space_constraint(array, pltpu.HBM)
-
     def exchanged(block, axis):
         return lax.all_to_all(block, axis, 0, 0, tiled=True)
 
@@ -341,20 +332,14 @@
         cross = lax.ppermute(block, "col", swap)
         return exchanged(sent, "col"), cross
 
-    x, d, x_eight = call(
-        prepare_kernel,
-        (flat, flat, in_vmem((8, W))),
-        (stay(start_block), stay(diag_terms)),
-        [pltpu.VMEM((3, W), F32), pltpu.VMEM((W,), F32), pltpu.SemaphoreType.DMA, pltpu.SemaphoreType.DMA],
-        [HBM, HBM],
-        flops=5_000_000_000,
-    )
-    cross = lax.ppermute(x, "col", swap)
-    sent, high, low = call(
+    mark = call(opening_kernel, in_vmem((8, 128)), (), flops=5_000_000_000)
+    held, mark = lax.optimization_barrier((start_block, mark))
+    cross = lax.ppermute(held, "col", swap)
+    sent, x, d, high, low = call(
         first_kernel,
-        (in_vmem((cols, 1, FLAT)), in_vmem(whole, BF16), in_vmem(whole, BF16)),
-        (x, x_eight, couplings),
-        [tall],
+        (in_vmem((cols, 1, FLAT)), flat, flat, in_vmem(whole, BF16), in_vmem(whole, BF16)),
+        (start_block, diag_terms, couplings, mark),
+        [short, tall],
     )
     got = exchanged(sent, "col")
     total = call(sum_kernel, flat, (got,))

time: 103 us -> 103 us (level)
    unnamed x10 -> x14, local copies, waits for them, and re-layouts: 6.23 us -> 7.08 us
where the time goes in v8:
time: 103 us; the launch traced here: 102 us
  blocking collectives  44.3 us (43%)
  starting transfers between devices  23.9 us (23%)
  waiting for transfers between devices  18.5 us (18%)
  Pallas kernels  7.96 us (8%)
  local copies, waits for them, and re-layouts  7.08 us (7%)
    all_to_all x3, blocking collectives, exchanged(): return lax.all_to_all(block, axis, 0, 0, tiled=True)  44.3 us
    all_to_all x2, waiting for transfers between devices, exchanged(): return lax.all_to_all(block, axis, 0, 0, tiled=True)  18.5 us
    all_to_all x2, starting transfers between devices, exchanged(): return lax.all_to_all(block, axis, 0, 0, tiled=True)  17.6 us
    pallas_call x10, Pallas kernels, call(): pl.pallas_call(kernel, out_shape=out, in_specs=specs or [VMEM] * len(inpu...  7.96 us
    unnamed x14, local copies, waits for them, and re-layouts  7.08 us
    ppermute x1, starting transfers between devices, shards(): cross = lax.ppermute(held, 'col', swap)  3.14 us
    ppermute x1, starting transfers between devices, spread(): cross = lax.ppermute(block, 'col', swap)  3.14 us
  transfers between devices with their start and end apart: 4, of which 2 were waited for; matrix products, arithmetic and copies ran while one was open for 0% of the time, Pallas kernels for 0%

profile of v8, /device:TPU:1, one launch (start us, length us, event | category | flops | bytes accessed | tf_op | source)
XLA Modules:
  0.0 102.5 jit_solution(10032113131487430195)
XLA Ops:
  0.6 0.0 copy-start.5
  0.6 0.0 copy-start.4
  0.6 0.0 copy-start.6
  0.7 0.7 copy-done.5
  1.3 1.6 %copy-done.4 = f32[1536,768]{1,0:T(8,128)S(1)} copy-done((f32[1536,768]{1,0:T(8,128)S(1)}, f32[1536,768]{1,0:T(8,128)}, u32[]{:S(2)}) %copy-start.4) | copy-done | bytes 4718616
  3.0 0.0 copy-done.6
  3.0 2.4 %shard_map.51 = (f32[32,1,2304]{2,1,0:T(1,128)}, f32[1,2304]{1,0:T(1,128)S(1)}, f32[1,2304]{1,0:T(1,128)S(1)}, bf16[1536,768]{1,0:T(8,128)(2,1)S(1)}, bf16[1536,768]{1,0:T(8,128)(2,1)S(1)}) custom-call(f32[3,768]{1,0:T(4,128)S(1)} %copy-done.5, f32[768]{0:T(1024)S(1)} %copy-done.6, f32[1536,768]{1,0:T(8,128)S(1)} %copy-done.4, f32[8,128]{1,0:T(8,128)S(1)} %shard_map.50.mark_ref), custom_call_target="tpu_custom_call" | custom-call | flops 2000000 | bytes 100000 | tf_op jit(solution)/shard_map/pallas_call | solution.py:308
  5.4 0.0 copy-start
  5.4 1.4 %copy-done = bf16[1536,768]{1,0:T(8,128)(2,1)} copy-done((bf16[1536,768]{1,0:T(8,128)(2,1)}, bf16[1536,768]{1,0:T(8,128)(2,1)S(1)}, u32[]{:S(2)}) %copy-start) | copy-done | bytes 2359320
  6.8 13.7 %all-to-all-start = ((f32[32,1,2304]{2,1,0:T(1,128)}), f32[32,1,2304]{2,1,0:T(1,128)S(1)}, u32[]{:S(2)}, u32[]{:S(2)}) async-start(f32[32,1,2304]{2,1,0:T(1,128)} %get-tuple-element.19), calls=%async_computation | async-start | bytes 589824 | tf_op jit(solution)/shard_map/all_to_all | solution.py:329
  20.5 3.1 %collective-permute-start = (f32[3,768]{1,0:T(4,128)S(1)}, f32[3,768]{1,0:T(4,128)S(1)}, u32[]{:S(2)}, u32[]{:S(2)}) collective-permute-start(f32[3,768]{1,0:T(4,128)S(1)} %copy-done.5), channel_id=1, source_target_pairs={{0,1},{1,0},{2,3},{3,2},{4,5},{5,4},{6,7},{7,6},{8,9},{9,8},{10,11... | collective-permute-start | bytes 27656 | tf_op jit(solution)/shard_map/ppermute | solution.py:337
  23.7 8.9 %all-to-all-done.got_ref = f32[32,1,2304]{2,1,0:T(1,128)S(1)} async-done(((f32[32,1,2304]{2,1,0:T(1,128)}), f32[32,1,2304]{2,1,0:T(1,128)S(1)}, u32[]{:S(2)}, u32[]{:S(2)}) %all-to-all-start) | async-done | bytes 294944 | tf_op jit(solution)/shard_map/all_to_all | solution.py:329
  32.6 0.0 collective-permute-done.cross_ref
  32.6 0.0 copy-start.1
  32.6 1.7 %copy-done.1 = bf16[1536,768]{1,0:T(8,128)(2,1)S(1)} copy-done((bf16[1536,768]{1,0:T(8,128)(2,1)S(1)}, bf16[1536,768]{1,0:T(8,128)(2,1)}, u32[]{:S(2)}) %copy-start.1) | copy-done | bytes 2359320
  34.3 0.0 copy-start.2
  34.3 0.9 shard_map.53
  35.2 18.4 %all_to_all.25.got_ref = f32[16,1,2304]{2,1,0:T(1,128)S(1)} all-to-all(f32[16,1,2304]{2,1,0:T(1,128)S(1)} %get-tuple-element.24), channel_id=1, replica_groups=mesh['row'=16,'col'=32] {'row'}, dimensions={0} | all-to-all | bytes 294912 | tf_op jit(solution)/shard_map/all_to_all | solution.py:329
  53.6 0.0 copy-done.2
  53.6 2.2 %shard_map.55 = f32[32,1,2304]{2,1,0:T(1,128)} custom-call(f32[1,2304]{1,0:T(1,128)S(1)} %shard_map.54.z_ref.own_ref, f32[1,2304]{1,0:T(1,128)S(1)} %get-tuple-element.20.own_ref.x_ref, bf16[1536,768]{1,0:T(8,128)(2,1)S(1)} %get-tuple-element.22.high_ref, bf16[1536,768]{1,0:T(8,128)(2,1)S(1)} %copy-done.2), custom_call_target="tpu_custom_call" | custom-call | flops 2000000 | bytes 100000 | tf_op jit(solution)/shard_map/pallas_call | solution.py:308
  55.8 3.9 %all-to-all-start.2 = ((f32[32,1,2304]{2,1,0:T(1,128)}), f32[32,1,2304]{2,1,0:T(1,128)S(1)}, u32[]{:S(2)}, u32[]{:S(2)}) async-start(f32[32,1,2304]{2,1,0:T(1,128)} %shard_map.55), calls=%async_computation.2 | async-start | bytes 589824 | tf_op jit(solution)/shard_map/all_to_all | solution.py:329
  59.7 3.1 %collective-permute-start.1 = (f32[1,2304]{1,0:T(1,128)S(1)}, f32[1,2304]{1,0:T(1,128)S(1)}, u32[]{:S(2)}, u32[]{:S(2)}) collective-permute-start(f32[1,2304]{1,0:T(1,128)S(1)} %shard_map.54.z_ref.own_ref), channel_id=1, source_target_pairs={{0,1},{1,0},{2,3},{3,2},{4,5},{5,4},{6,7},{7,6},{8,9},{9,8},{10,11... | collective-permute-start | bytes 27656 | tf_op jit(solution)/shard_map/ppermute | solution.py:332
  62.9 9.6 %all-to-all-done.2.got_ref = f32[32,1,2304]{2,1,0:T(1,128)S(1)} async-done(((f32[32,1,2304]{2,1,0:T(1,128)}), f32[32,1,2304]{2,1,0:T(1,128)S(1)}, u32[]{:S(2)}, u32[]{:S(2)}) %all-to-all-start.2) | async-done | bytes 294944 | tf_op jit(solution)/shard_map/all_to_all | solution.py:329
  72.5 0.2 shard_map.56
  72.7 0.0 collective-permute-done.1.cross_ref
  72.7 0.0 copy-start.3
  72.7 1.7 %copy-done.3 = bf16[1536,768]{1,0:T(8,128)(2,1)S(1)} copy-done((bf16[1536,768]{1,0:T(8,128)(2,1)S(1)}, bf16[1536,768]{1,0:T(8,128)(2,1)}, u32[]{:S(2)}) %copy-start.3) | copy-done | bytes 2359320
  74.3 0.9 shard_map.57
  75.3 13.8 %all_to_all.26.got_ref = f32[16,1,2432]{2,1,0:T(1,128)S(1)} all-to-all(f32[16,1,2432]{2,1,0:T(1,128)S(1)} %shard_map.57), channel_id=1, replica_groups=mesh['row'=16,'col'=32] {'row'}, dimensions={0} | all-to-all | bytes 311296 | tf_op jit(solution)/shard_map/all_to_all | solution.py:329
  89.1 0.4 shard_map.58
  89.5 12.1 %all_to_all.27.got_ref = f32[32,1,128]{2,1,0:T(1,128)S(1)} all-to-all(f32[32,1,128]{2,1,0:T(1,128)S(1)} %get-tuple-element.29), channel_id=1, replica_groups=mesh['row'=16,'col'=32] {'col'}, dimensions={0} | all-to-all | bytes 32768 | tf_op jit(solution)/shard_map/all_to_all | solution.py:329
  101.6 0.8 shard_map.59
  (3 shorter events, 0.1 us)
Async XLA Ops:
  0.6 0.7 copy-start.5
  0.6 2.3 %copy-start.4 = (f32[1536,768]{1,0:T(8,128)S(1)}, f32[1536,768]{1,0:T(8,128)}, u32[]{:S(2)}) copy-start(f32[1536,768]{1,0:T(8,128)} %a_ref.1) | copy-start | bytes 14155780
  0.6 2.3 %copy-start.6 = (f32[768]{0:T(1024)S(1)}, f32[768]{0:T(1024)}, u32[]{:S(2)}) copy-start(f32[768]{0:T(1024)} %d_ref.1) | copy-start | bytes 9220
  5.4 1.4 %copy-start = (bf16[1536,768]{1,0:T(8,128)(2,1)}, bf16[1536,768]{1,0:T(8,128)(2,1)S(1)}, u32[]{:S(2)}) copy-start(bf16[1536,768]{1,0:T(8,128)(2,1)S(1)} %get-tuple-element.23.low_ref) | copy-start | bytes 7077892
  6.8 25.7 %all-to-all-start = ((f32[32,1,2304]{2,1,0:T(1,128)}), f32[32,1,2304]{2,1,0:T(1,128)S(1)}, u32[]{:S(2)}, u32[]{:S(2)}) async-start(f32[32,1,2304]{2,1,0:T(1,128)} %get-tuple-element.19), calls=%async_computation | async-start | bytes 589824 | tf_op jit(solution)/shard_map/all_to_all | solution.py:329
  20.5 12.1 %collective-permute-start = (f32[3,768]{1,0:T(4,128)S(1)}, f32[3,768]{1,0:T(4,128)S(1)}, u32[]{:S(2)}, u32[]{:S(2)}) collective-permute-start(f32[3,768]{1,0:T(4,128)S(1)} %copy-done.5), channel_id=1, source_target_pairs={{0,1},{1,0},{2,3},{3,2},{4,5},{5,4},{6,7},{7,6},{8,9},{9,8},{10,11... | collective-permute-start | bytes 27656 | tf_op jit(solution)/shard_map/ppermute | solution.py:337
  32.6 1.7 %copy-start.1 = (bf16[1536,768]{1,0:T(8,128)(2,1)S(1)}, bf16[1536,768]{1,0:T(8,128)(2,1)}, u32[]{:S(2)}) copy-start(bf16[1536,768]{1,0:T(8,128)(2,1)} %copy-done) | copy-start | bytes 7077892
  34.3 19.3 %copy-start.2 = (bf16[1536,768]{1,0:T(8,128)(2,1)S(1)}, bf16[1536,768]{1,0:T(8,128)(2,1)}, u32[]{:S(2)}) copy-start(bf16[1536,768]{1,0:T(8,128)(2,1)} %copy-done) | copy-start | bytes 7077892
  55.8 16.7 %all-to-all-start.2 = ((f32[32,1,2304]{2,1,0:T(1,128)}), f32[32,1,2304]{2,1,0:T(1,128)S(1)}, u32[]{:S(2)}, u32[]{:S(2)}) async-start(f32[32,1,2304]{2,1,0:T(1,128)} %shard_map.55), calls=%async_computation.2 | async-start | bytes 589824 | tf_op jit(solution)/shard_map/all_to_all | solution.py:329
  59.7 12.9 %collective-permute-start.1 = (f32[1,2304]{1,0:T(1,128)S(1)}, f32[1,2304]{1,0:T(1,128)S(1)}, u32[]{:S(2)}, u32[]{:S(2)}) collective-permute-start(f32[1,2304]{1,0:T(1,128)S(1)} %shard_map.54.z_ref.own_ref), channel_id=1, source_target_pairs={{0,1},{1,0},{2,3},{3,2},{4,5},{5,4},{6,7},{7,6},{8,9},{9,8},{10,11... | collective-permute-start | bytes 27656 | tf_op jit(solution)/shard_map/ppermute | solution.py:332
  72.7 1.7 %copy-start.3 = (bf16[1536,768]{1,0:T(8,128)(2,1)S(1)}, bf16[1536,768]{1,0:T(8,128)(2,1)}, u32[]{:S(2)}) copy-start(bf16[1536,768]{1,0:T(8,128)(2,1)} %copy-done) | copy-start | bytes 7077892

commit v9 on v8

--- a/solution.py
+++ b/solution.py
@@ -15,6 +15,7 @@
 F32 = jnp.float32
 BF16 = jnp.bfloat16
 VMEM = pl.BlockSpec(memory_space=pltpu.VMEM)
+HBM = pl.BlockSpec(memory_space=pltpu.HBM)
 
 
 def in_vmem(shape, dtype=F32):
@@ -163,13 +164,42 @@
     backward(got_ref, own_ref, cross_ref, total_ref, high_ref, low_ref, sent_ref, v_rows)
 
 
-def second_backward_kernel(got_ref, own_ref, cross_ref, total_ref, tile_ref, high_ref, low_ref, sent_ref, v_rows):
+def second_backward_kernel(
+    got_ref, own_ref, cross_ref, x_rows, high_ref, low_hbm, sent_ref, low, v_rows, total_ref, tile_ref, wide_ref, sems
+):
+    pieces = [slice(start, start + CHUNK) for start in range(0, 2 * W, CHUNK)]
+    copies = [pltpu.make_async_copy(low_hbm.at[piece], low.at[piece], sems.at[i]) for i, piece in enumerate(pieces)]
+    for copy in copies:
+        copy.start()
+    assemble(got_ref, own_ref, cross_ref, v_rows)
+    parts = three_parts(v_rows[...])
+    wide_ref[...] = over_cols(parts, high_ref[...])
+    gram_kernel(got_ref, x_rows, total_ref, tile_ref)
     for p in range(sent_ref.shape[0]):
         sent_ref[p, :, FLAT:] = tile_ref[...]
-    backward(got_ref, own_ref, cross_ref, total_ref, high_ref, low_ref, sent_ref, v_rows)
+    total = rows_of(total_ref[...])
+    wide = wide_ref[...]
+    for copy, piece in zip(copies, pieces):
+        copy.wait()
+        wide = wide + over_cols(parts[:, piece], low[piece, :])
+    deliver(0.5 * folded(wide), total, sent_ref)
 
 
 def backward(got_ref, own_ref, cross_ref, total_ref, high_ref, low_ref, sent_ref, v_rows):
+    assemble(got_ref, own_ref, cross_ref, v_rows)
+    parts = three_parts(v_rows[...])
+    wide = over_cols(parts, high_ref[...]) + over_cols(parts, low_ref[...])
+    deliver(0.5 * folded(wide), rows_of(total_ref[...]), sent_ref)
+
+
+def deliver(back, total, sent_ref):
+    for k in range(3):
+        part = back[k : k + 1] + total[k]
+        for p in range(sent_ref.shape[0]):
+            sent_ref[p, :, k * W : (k + 1) * W] = part
+
+
+def assemble(got_ref, own_ref, cross_ref, v_rows):
     row_index = lax.axis_index("row")
     col_index = lax.axis_index("col")
     home = col_index // 2 == row_index
@@ -181,14 +211,6 @@
         for k in range(3):
             mine = jnp.where(col_index % 2 == half, own[k], cross[k])
             v_rows[k : k + 1, half * W : (half + 1) * W] = jnp.where(home, mine, sent_here[k])
-    parts = three_parts(v_rows[...])
-    total = rows_of(total_ref[...])
-    wide = over_cols(parts, high_ref[...]) + over_cols(parts, low_ref[...])
-    back = 0.5 * folded(wide)
-    for k in range(3):
-        part = back[k : k + 1] + total[k]
-        for p in range(sent_ref.shape[0]):
-            sent_ref[p, :, k * W : (k + 1) * W] = part
 
 
 def sum_kernel(got_ref, total_ref):
@@ -328,10 +350,6 @@
     def exchanged(block, axis):
         return lax.all_to_all(block, axis, 0, 0, tiled=True)
 
-    def spread(sent, block):
-        cross = lax.ppermute(block, "col", swap)
-        return exchanged(sent, "col"), cross
-
     mark = call(opening_kernel, in_vmem((8, 128)), (), flops=5_000_000_000)
     held, mark = lax.optimization_barrier((start_block, mark))
     cross = lax.ppermute(held, "col", swap)
@@ -349,14 +367,23 @@
     )
     got = exchanged(sent, "row")
     z = call(collect_kernel, flat, (got, d, x))
-    sent = call(forward_kernel, in_vmem((cols, 1, FLAT)), (z, x, high, low), [short, tall])
-    got, cross = spread(sent, z)
-    total, tile = call(gram_kernel, (flat, in_vmem((1, 128))), (got, x_rows))
+    slots = jax.ShapeDtypeStruct((cols, 1, FLAT), F32)
+    sent = call(forward_kernel, slots, (z, x, high, low), [short, tall])
+    cross = lax.ppermute(z, "col", swap)
+    got = exchanged(sent, "col")
     sent = call(
         second_backward_kernel,
         in_vmem((rows, 1, FLAT + 128)),
-        (got, z, cross, total, tile, high, low),
-        [tall],
+        (got, z, cross, x_rows, high, pltpu.with_memory_space_constraint(low, pltpu.HBM)),
+        [
+            pltpu.VMEM(whole, BF16),
+            tall,
+            pltpu.VMEM((1, FLAT), F32),
+            pltpu.VMEM((1, 128), F32),
+            pltpu.VMEM((24, W), F32),
+            pltpu.SemaphoreType.DMA((2 * W // CHUNK,)),
+        ],
+        [VMEM] * 5 + [HBM],
     )
     got = exchanged(sent, "row")
     sent, basis, coef = call(

time: 103 us -> 103 us (level)
  local copies, waits for them, and re-layouts: 7.08 us -> 5.41 us
  Pallas kernels: 7.96 us -> 9.34 us
    unnamed x14 -> x12, local copies, waits for them, and re-layouts: 7.08 us -> 5.41 us
    all_to_all x2, waiting for transfers between devices: 18.5 us -> 16.9 us  [exchanged(): return lax.all_to_all(block, axis, 0, 0, tiled=True)]
    ppermute x1, waiting for transfers between devices: 0.01 us -> 1.56 us  [shards(): cross = lax.ppermute(z, 'col', swap)]
    pallas_call x10 -> x9, Pallas kernels: 7.96 us -> 9.34 us  [call(): pl.pallas_call(kernel, out_shape=out, in_specs=specs or [VMEM] * len(inpu...]
  transfers between devices with their start and end apart: 4 -> 4, of which waited for: 2 -> 3; matrix products, arithmetic and copies ran while one was open for 0% -> 0% of each run, Pallas kernels for 0% -> 0%
where the time goes in v9:
time: 103 us; the launch traced here: 102 us
  blocking collectives  44.3 us (43%)
  starting transfers between devices  23.9 us (23%)
  waiting for transfers between devices  18.5 us (18%)
  Pallas kernels  9.34 us (9%)
  local copies, waits for them, and re-layouts  5.41 us (5%)
    all_to_all x3, blocking collectives, exchanged(): return lax.all_to_all(block, axis, 0, 0, tiled=True)  44.3 us
    all_to_all x2, starting transfers between devices, exchanged(): return lax.all_to_all(block, axis, 0, 0, tiled=True)  17.6 us
    all_to_all x2, waiting for transfers between devices, exchanged(): return lax.all_to_all(block, axis, 0, 0, tiled=True)  16.9 us
    pallas_call x9, Pallas kernels, call(): pl.pallas_call(kernel, out_shape=out, in_specs=specs or [VMEM] * len(inpu...  9.34 us
    unnamed x12, local copies, waits for them, and re-layouts  5.41 us
    ppermute x1, starting transfers between devices, shards(): cross = lax.ppermute(held, 'col', swap)  3.14 us
    ppermute x1, starting transfers between devices, shards(): cross = lax.ppermute(z, 'col', swap)  3.14 us
  transfers between devices with their start and end apart: 4, of which 3 were waited for; matrix products, arithmetic and copies ran while one was open for 0% of the time, Pallas kernels for 0%

profile of v9, /device:TPU:1, one launch (start us, length us, event | category | flops | bytes accessed | tf_op | source)
XLA Modules:
  0.0 102.1 jit_solution(14517193255724934727)
XLA Ops:
  0.6 0.0 copy-start.4
  0.6 0.0 copy-start.3
  0.6 0.0 copy-start.5
  0.7 0.7 copy-done.4
  1.3 1.6 %copy-done.3 = f32[1536,768]{1,0:T(8,128)S(1)} copy-done((f32[1536,768]{1,0:T(8,128)S(1)}, f32[1536,768]{1,0:T(8,128)}, u32[]{:S(2)}) %copy-start.3) | copy-done | bytes 4718616
  3.0 0.0 copy-done.5
  3.0 2.4 %shard_map.51 = (f32[32,1,2304]{2,1,0:T(1,128)}, f32[1,2304]{1,0:T(1,128)S(1)}, f32[1,2304]{1,0:T(1,128)S(1)}, bf16[1536,768]{1,0:T(8,128)(2,1)S(1)}, bf16[1536,768]{1,0:T(8,128)(2,1)S(1)}) custom-call(f32[3,768]{1,0:T(4,128)S(1)} %copy-done.4, f32[768]{0:T(1024)S(1)} %copy-done.5, f32[1536,768]{1,0:T(8,128)S(1)} %copy-done.3, f32[8,128]{1,0:T(8,128)S(1)} %shard_map.50.mark_ref), custom_call_target="tpu_custom_call" | custom-call | flops 2000000 | bytes 100000 | tf_op jit(solution)/shard_map/pallas_call | solution.py:330
  5.4 0.0 copy-start
  5.4 1.4 %copy-done = bf16[1536,768]{1,0:T(8,128)(2,1)} copy-done((bf16[1536,768]{1,0:T(8,128)(2,1)}, bf16[1536,768]{1,0:T(8,128)(2,1)S(1)}, u32[]{:S(2)}) %copy-start) | copy-done | bytes 2359320
  6.8 13.7 %all-to-all-start = ((f32[32,1,2304]{2,1,0:T(1,128)}), f32[32,1,2304]{2,1,0:T(1,128)S(1)}, u32[]{:S(2)}, u32[]{:S(2)}) async-start(f32[32,1,2304]{2,1,0:T(1,128)} %get-tuple-element.17), calls=%async_computation | async-start | bytes 589824 | tf_op jit(solution)/shard_map/all_to_all | solution.py:351
  20.5 3.1 %collective-permute-start = (f32[3,768]{1,0:T(4,128)S(1)}, f32[3,768]{1,0:T(4,128)S(1)}, u32[]{:S(2)}, u32[]{:S(2)}) collective-permute-start(f32[3,768]{1,0:T(4,128)S(1)} %copy-done.4), channel_id=1, source_target_pairs={{0,1},{1,0},{2,3},{3,2},{4,5},{5,4},{6,7},{7,6},{8,9},{9,8},{10,11... | collective-permute-start | bytes 27656 | tf_op jit(solution)/shard_map/ppermute | solution.py:355
  23.7 8.9 %all-to-all-done.got_ref = f32[32,1,2304]{2,1,0:T(1,128)S(1)} async-done(((f32[32,1,2304]{2,1,0:T(1,128)}), f32[32,1,2304]{2,1,0:T(1,128)S(1)}, u32[]{:S(2)}, u32[]{:S(2)}) %all-to-all-start) | async-done | bytes 294944 | tf_op jit(solution)/shard_map/all_to_all | solution.py:351
  32.6 0.0 collective-permute-done.cross_ref
  32.6 0.0 copy-start.1
  32.6 1.7 %copy-done.1 = bf16[1536,768]{1,0:T(8,128)(2,1)S(1)} copy-done((bf16[1536,768]{1,0:T(8,128)(2,1)S(1)}, bf16[1536,768]{1,0:T(8,128)(2,1)}, u32[]{:S(2)}) %copy-start.1) | copy-done | bytes 2359320
  34.3 0.0 copy-start.2
  34.3 0.9 shard_map.53
  35.2 18.4 %all_to_all.25.got_ref = f32[16,1,2304]{2,1,0:T(1,128)S(1)} all-to-all(f32[16,1,2304]{2,1,0:T(1,128)S(1)} %get-tuple-element.22), channel_id=1, replica_groups=mesh['row'=16,'col'=32] {'row'}, dimensions={0} | all-to-all | bytes 294912 | tf_op jit(solution)/shard_map/all_to_all | solution.py:351
  53.6 0.0 copy-done.2
  53.6 2.2 %shard_map.55 = f32[32,1,2304]{2,1,0:T(1,128)} custom-call(f32[1,2304]{1,0:T(1,128)S(1)} %shard_map.54.z_ref.own_ref, f32[1,2304]{1,0:T(1,128)S(1)} %get-tuple-element.18.own_ref.x_ref, bf16[1536,768]{1,0:T(8,128)(2,1)S(1)} %get-tuple-element.20.high_ref, bf16[1536,768]{1,0:T(8,128)(2,1)S(1)} %copy-done.2), custom_call_target="tpu_custom_call" | custom-call | flops 2000000 | bytes 100000 | tf_op jit(solution)/shard_map/pallas_call | solution.py:330
  55.8 3.9 %all-to-all-start.2 = ((f32[32,1,2304]{2,1,0:T(1,128)}), f32[32,1,2304]{2,1,0:T(1,128)S(1)}, u32[]{:S(2)}, u32[]{:S(2)}) async-start(f32[32,1,2304]{2,1,0:T(1,128)} %shard_map.55), calls=%async_computation.2 | async-start | bytes 589824 | tf_op jit(solution)/shard_map/all_to_all | solution.py:351
  59.7 3.1 %collective-permute-start.1 = (f32[1,2304]{1,0:T(1,128)S(1)}, f32[1,2304]{1,0:T(1,128)S(1)}, u32[]{:S(2)}, u32[]{:S(2)}) collective-permute-start(f32[1,2304]{1,0:T(1,128)S(1)} %shard_map.54.z_ref.own_ref), channel_id=1, source_target_pairs={{0,1},{1,0},{2,3},{3,2},{4,5},{5,4},{6,7},{7,6},{8,9},{9,8},{10,11... | collective-permute-start | bytes 27656 | tf_op jit(solution)/shard_map/ppermute | solution.py:372
  62.9 1.6 %collective-permute-done.1.cross_ref = f32[1,2304]{1,0:T(1,128)S(1)} collective-permute-done((f32[1,2304]{1,0:T(1,128)S(1)}, f32[1,2304]{1,0:T(1,128)S(1)}, u32[]{:S(2)}, u32[]{:S(2)}) %collective-permute-start.1) | collective-permute-done | bytes 9248 | tf_op jit(solution)/shard_map/ppermute | solution.py:372
  64.4 8.0 %all-to-all-done.2.got_ref = f32[32,1,2304]{2,1,0:T(1,128)S(1)} async-done(((f32[32,1,2304]{2,1,0:T(1,128)}), f32[32,1,2304]{2,1,0:T(1,128)S(1)}, u32[]{:S(2)}, u32[]{:S(2)}) %all-to-all-start.2) | async-done | bytes 294944 | tf_op jit(solution)/shard_map/all_to_all | solution.py:351
  72.5 2.5 %shard_map.56 = f32[16,1,2432]{2,1,0:T(1,128)S(1)} custom-call(f32[32,1,2304]{2,1,0:T(1,128)S(1)} %all-to-all-done.2.got_ref, f32[1,2304]{1,0:T(1,128)S(1)} %shard_map.54.z_ref.own_ref, f32[1,2304]{1,0:T(1,128)S(1)} %collective-permute-done.1.cross_ref, f32[8,1536]{1,0:T(8,128)S(1)} %get-tuple-element.24.x_rows, ...), custom_call_target="tpu_custom_call" | custom-call | flops 2000000 | bytes 100000 | tf_op jit(solution)/shard_map/pallas_call | solution.py:330
  75.0 13.8 %all_to_all.26.got_ref = f32[16,1,2432]{2,1,0:T(1,128)S(1)} all-to-all(f32[16,1,2432]{2,1,0:T(1,128)S(1)} %shard_map.56), channel_id=1, replica_groups=mesh['row'=16,'col'=32] {'row'}, dimensions={0} | all-to-all | bytes 311296 | tf_op jit(solution)/shard_map/all_to_all | solution.py:351
  88.8 0.4 shard_map.57
  89.2 12.1 %all_to_all.27.got_ref = f32[32,1,128]{2,1,0:T(1,128)S(1)} all-to-all(f32[32,1,128]{2,1,0:T(1,128)S(1)} %get-tuple-element.25), channel_id=1, replica_groups=mesh['row'=16,'col'=32] {'col'}, dimensions={0} | all-to-all | bytes 32768 | tf_op jit(solution)/shard_map/all_to_all | solution.py:351
  101.3 0.8 shard_map.58
  (3 shorter events, 0.1 us)
Async XLA Ops:
  0.6 0.7 copy-start.4
  0.6 2.3 %copy-start.3 = (f32[1536,768]{1,0:T(8,128)S(1)}, f32[1536,768]{1,0:T(8,128)}, u32[]{:S(2)}) copy-start(f32[1536,768]{1,0:T(8,128)} %a_ref.1) | copy-start | bytes 14155780
  0.6 2.3 %copy-start.5 = (f32[768]{0:T(1024)S(1)}, f32[768]{0:T(1024)}, u32[]{:S(2)}) copy-start(f32[768]{0:T(1024)} %d_ref.1) | copy-start | bytes 9220
  5.4 1.4 %copy-start = (bf16[1536,768]{1,0:T(8,128)(2,1)}, bf16[1536,768]{1,0:T(8,128)(2,1)S(1)}, u32[]{:S(2)}) copy-start(bf16[1536,768]{1,0:T(8,128)(2,1)S(1)} %get-tuple-element.21.low_ref.low_hbm) | copy-start | bytes 7077892
  6.8 25.7 %all-to-all-start = ((f32[32,1,2304]{2,1,0:T(1,128)}), f32[32,1,2304]{2,1,0:T(1,128)S(1)}, u32[]{:S(2)}, u32[]{:S(2)}) async-start(f32[32,1,2304]{2,1,0:T(1,128)} %get-tuple-element.17), calls=%async_computation | async-start | bytes 589824 | tf_op jit(solution)/shard_map/all_to_all | solution.py:351
  20.5 12.1 %collective-permute-start = (f32[3,768]{1,0:T(4,128)S(1)}, f32[3,768]{1,0:T(4,128)S(1)}, u32[]{:S(2)}, u32[]{:S(2)}) collective-permute-start(f32[3,768]{1,0:T(4,128)S(1)} %copy-done.4), channel_id=1, source_target_pairs={{0,1},{1,0},{2,3},{3,2},{4,5},{5,4},{6,7},{7,6},{8,9},{9,8},{10,11... | collective-permute-start | bytes 27656 | tf_op jit(solution)/shard_map/ppermute | solution.py:355
  32.6 1.7 %copy-start.1 = (bf16[1536,768]{1,0:T(8,128)(2,1)S(1)}, bf16[1536,768]{1,0:T(8,128)(2,1)}, u32[]{:S(2)}) copy-start(bf16[1536,768]{1,0:T(8,128)(2,1)} %copy-done) | copy-start | bytes 7077892
  34.3 19.3 %copy-start.2 = (bf16[1536,768]{1,0:T(8,128)(2,1)S(1)}, bf16[1536,768]{1,0:T(8,128)(2,1)}, u32[]{:S(2)}) copy-start(bf16[1536,768]{1,0:T(8,128)(2,1)} %copy-done) | copy-start | bytes 7077892
  55.8 16.7 %all-to-all-start.2 = ((f32[32,1,2304]{2,1,0:T(1,128)}), f32[32,1,2304]{2,1,0:T(1,128)S(1)}, u32[]{:S(2)}, u32[]{:S(2)}) async-start(f32[32,1,2304]{2,1,0:T(1,128)} %shard_map.55), calls=%async_computation.2 | async-start | bytes 589824 | tf_op jit(solution)/shard_map/all_to_all | solution.py:351
  59.7 4.7 %collective-permute-start.1 = (f32[1,2304]{1,0:T(1,128)S(1)}, f32[1,2304]{1,0:T(1,128)S(1)}, u32[]{:S(2)}, u32[]{:S(2)}) collective-permute-start(f32[1,2304]{1,0:T(1,128)S(1)} %shard_map.54.z_ref.own_ref), channel_id=1, source_target_pairs={{0,1},{1,0},{2,3},{3,2},{4,5},{5,4},{6,7},{7,6},{8,9},{9,8},{10,11... | collective-permute-start | bytes 27656 | tf_op jit(solution)/shard_map/ppermute | solution.py:372

commit v10 on v9

--- a/solution.py
+++ b/solution.py
@@ -117,7 +117,7 @@
     mark_ref[...] = jnp.zeros_like(mark_ref)
 
 
-def first_kernel(x_ref, d_ref, a_ref, mark_ref, sent_ref, flat_ref, diag_ref, high_ref, low_ref, x_rows, forward):
+def first_kernel(x_ref, d_ref, a_ref, mark_ref, sent_ref, flat_ref, diag_ref, high_ref, near_ref, far_ref, x_rows, forward):
     row_index = lax.axis_index("row")
     x_rows[...] = jnp.zeros_like(x_rows)
     x_rows[0:3, :] = x_ref[...]
@@ -131,18 +131,19 @@
     parts = three_parts(x_rows[...])
     for start in range(0, 2 * W, CHUNK):
         piece = slice(start, start + CHUNK)
+        low_ref, base = (near_ref, 0) if start == 0 else (far_ref, CHUNK)
         for at in range(start, start + CHUNK, STRIP):
-            strip = slice(at, at + STRIP)
-            block = a_ref[strip, :]
+            block = a_ref[at : at + STRIP, :]
             high = block.astype(BF16)
-            high_ref[strip, :] = high
-            low_ref[strip, :] = (block - high.astype(F32)).astype(BF16)
-        wide = over_rows(parts, high_ref[piece, :]) + over_rows(parts, low_ref[piece, :])
+            high_ref[at : at + STRIP, :] = high
+            low_ref[at - base : at - base + STRIP, :] = (block - high.astype(F32)).astype(BF16)
+        low = low_ref[start - base : start - base + CHUNK, :]
+        wide = over_rows(parts, high_ref[piece, :]) + over_rows(parts, low)
         forward[:, piece] = 0.5 * folded(wide)
     place(row_index, forward, sent_ref)
 
 
-def forward_kernel(z_ref, x_ref, high_ref, low_ref, sent_ref, z_rows, forward):
+def forward_kernel(z_ref, x_ref, high_ref, near_ref, far_ref, sent_hbm, sent_ref, pair_ref, z_rows, forward, sems):
     row_index = lax.axis_index("row")
     home = lax.axis_index("col") // 2 == row_index
     z = z_ref[...]
@@ -156,24 +157,36 @@
     for p in range(sent_ref.shape[0]):
         sent_ref[p, :, 0:128] = head
         sent_ref[p, :, 128:] = z[:, 128:]
-    forward[...] = 0.5 * folded(over_rows(parts, high_ref[...]) + over_rows(parts, low_ref[...]))
-    place(row_index, forward, sent_ref)
-
-
-def first_backward_kernel(got_ref, own_ref, cross_ref, total_ref, high_ref, low_ref, sent_ref, v_rows):
-    backward(got_ref, own_ref, cross_ref, total_ref, high_ref, low_ref, sent_ref, v_rows)
+    filled = pltpu.make_async_copy(sent_ref, sent_hbm, sems.at[0])
+    filled.start()
+    for piece, low_ref in ((slice(0, CHUNK), near_ref), (slice(CHUNK, 2 * W), far_ref)):
+        wide = over_rows(parts, high_ref[piece, :]) + over_rows(parts, low_ref[...])
+        forward[:, piece] = 0.5 * folded(wide)
+    place(0, forward, pair_ref)
+    aimed = pltpu.make_async_copy(pair_ref, sent_hbm.at[pl.ds(2 * row_index, 2)], sems.at[1])
+    filled.wait()
+    aimed.start()
+    aimed.wait()
+
+
+def first_backward_kernel(got_ref, own_ref, cross_ref, total_ref, high_ref, near_ref, far_ref, sent_ref, v_rows):
+    assemble(got_ref, own_ref, cross_ref, v_rows)
+    parts = three_parts(v_rows[...])
+    wide = over_cols(parts, high_ref[...]) + over_cols(parts[:, :CHUNK], near_ref[...])
+    wide = wide + over_cols(parts[:, CHUNK:], far_ref[...])
+    deliver(0.5 * folded(wide), rows_of(total_ref[...]), sent_ref)
 
 
 def second_backward_kernel(
-    got_ref, own_ref, cross_ref, x_rows, high_ref, low_hbm, sent_ref, low, v_rows, total_ref, tile_ref, wide_ref, sems
+    got_ref, own_ref, cross_ref, x_rows, high_ref, near_ref, far_hbm, sent_ref, far, v_rows, total_ref, tile_ref, wide_ref, sems
 ):
-    pieces = [slice(start, start + CHUNK) for start in range(0, 2 * W, CHUNK)]
-    copies = [pltpu.make_async_copy(low_hbm.at[piece], low.at[piece], sems.at[i]) for i, piece in enumerate(pieces)]
+    pieces = [slice(start, start + CHUNK) for start in range(0, far.shape[0], CHUNK)]
+    copies = [pltpu.make_async_copy(far_hbm.at[piece], far.at[piece], sems.at[i]) for i, piece in enumerate(pieces)]
     for copy in copies:
         copy.start()
     assemble(got_ref, own_ref, cross_ref, v_rows)
     parts = three_parts(v_rows[...])
-    wide_ref[...] = over_cols(parts, high_ref[...])
+    wide_ref[...] = over_cols(parts, high_ref[...]) + over_cols(parts[:, :CHUNK], near_ref[...])
     gram_kernel(got_ref, x_rows, total_ref, tile_ref)
     for p in range(sent_ref.shape[0]):
         sent_ref[p, :, FLAT:] = tile_ref[...]
@@ -181,15 +194,8 @@
     wide = wide_ref[...]
     for copy, piece in zip(copies, pieces):
         copy.wait()
-        wide = wide + over_cols(parts[:, piece], low[piece, :])
+        wide = wide + over_cols(parts[:, CHUNK + piece.start : CHUNK + piece.stop], far[piece, :])
     deliver(0.5 * folded(wide), total, sent_ref)
-
-
-def backward(got_ref, own_ref, cross_ref, total_ref, high_ref, low_ref, sent_ref, v_rows):
-    assemble(got_ref, own_ref, cross_ref, v_rows)
-    parts = three_parts(v_rows[...])
-    wide = over_cols(parts, high_ref[...]) + over_cols(parts, low_ref[...])
-    deliver(0.5 * folded(wide), rows_of(total_ref[...]), sent_ref)
 
 
 def deliver(back, total, sent_ref):
@@ -342,7 +348,7 @@
     cols = lax.axis_size("col")
     rows = lax.axis_size("row")
     swap = [(i, i ^ 1) for i in range(cols)]
-    whole = (2 * W, W)
+    whole, part, rest = (2 * W, W), (CHUNK, W), (2 * W - CHUNK, W)
     tall = pltpu.VMEM((8, 2 * W), F32)
     short = pltpu.VMEM((8, W), F32)
     flat = in_vmem((1, FLAT))
@@ -353,9 +359,9 @@
     mark = call(opening_kernel, in_vmem((8, 128)), (), flops=5_000_000_000)
     held, mark = lax.optimization_barrier((start_block, mark))
     cross = lax.ppermute(held, "col", swap)
-    sent, x, d, high, low = call(
+    sent, x, d, high, near, far = call(
         first_kernel,
-        (in_vmem((cols, 1, FLAT)), flat, flat, in_vmem(whole, BF16), in_vmem(whole, BF16)),
+        (in_vmem((cols, 1, FLAT)), flat, flat, in_vmem(whole, BF16), in_vmem(part, BF16), in_vmem(rest, BF16)),
         (start_block, diag_terms, couplings, mark),
         [short, tall],
     )
@@ -363,27 +369,32 @@
     total = call(sum_kernel, flat, (got,))
     many = in_vmem((8, 2 * W))
     sent, x_rows = call(
-        first_backward_kernel, (in_vmem((rows, 1, FLAT)), many), (got, x, cross, total, high, low)
+        first_backward_kernel, (in_vmem((rows, 1, FLAT)), many), (got, x, cross, total, high, near, far)
     )
     got = exchanged(sent, "row")
     z = call(collect_kernel, flat, (got, d, x))
-    slots = jax.ShapeDtypeStruct((cols, 1, FLAT), F32)
-    sent = call(forward_kernel, slots, (z, x, high, low), [short, tall])
+    sent = call(
+        forward_kernel,
+        pltpu.HBM((cols, 1, FLAT), F32),
+        (z, x, high, near, far),
+        [pltpu.VMEM((cols, 1, FLAT), F32), pltpu.VMEM((2, 1, FLAT), F32), short, tall, pltpu.SemaphoreType.DMA((2,))],
+        out_specs=HBM,
+    )
     cross = lax.ppermute(z, "col", swap)
     got = exchanged(sent, "col")
     sent = call(
         second_backward_kernel,
         in_vmem((rows, 1, FLAT + 128)),
-        (got, z, cross, x_rows, high, pltpu.with_memory_space_constraint(low, pltpu.HBM)),
+        (got, z, cross, x_rows, high, near, pltpu.with_memory_space_constraint(far, pltpu.HBM)),
         [
-            pltpu.VMEM(whole, BF16),
+            pltpu.VMEM(rest, BF16),
             tall,
             pltpu.VMEM((1, FLAT), F32),
             pltpu.VMEM((1, 128), F32),
             pltpu.VMEM((24, W), F32),
-            pltpu.SemaphoreType.DMA((2 * W // CHUNK,)),
+            pltpu.SemaphoreType.DMA((2 * W // CHUNK - 1,)),
         ],
-        [VMEM] * 5 + [HBM],
+        [VMEM] * 6 + [HBM],
     )
     got = exchanged(sent, "row")
     sent, basis, coef = call(

time: 103 us -> 103 us (level)
  no operation moved by 1% of the time
where the time goes in v10:
time: 103 us; the launch traced here: 102 us
  blocking collectives  44.3 us (43%)
  starting transfers between devices  23.9 us (23%)
  waiting for transfers between devices  18.5 us (18%)
  Pallas kernels  8.99 us (9%)
  local copies, waits for them, and re-layouts  5.59 us (5%)
    all_to_all x3, blocking collectives, exchanged(): return lax.all_to_all(block, axis, 0, 0, tiled=True)  44.3 us
    all_to_all x2, starting transfers between devices, exchanged(): return lax.all_to_all(block, axis, 0, 0, tiled=True)  17.6 us
    all_to_all x2, waiting for transfers between devices, exchanged(): return lax.all_to_all(block, axis, 0, 0, tiled=True)  16.9 us
    pallas_call x9, Pallas kernels, call(): pl.pallas_call(kernel, out_shape=out, in_specs=specs or [VMEM] * len(inpu...  8.99 us
    unnamed x12, local copies, waits for them, and re-layouts  5.59 us
    ppermute x1, starting transfers between devices, shards(): cross = lax.ppermute(z, 'col', swap)  3.14 us
    ppermute x1, starting transfers between devices, shards(): cross = lax.ppermute(held, 'col', swap)  3.14 us
  transfers between devices with their start and end apart: 4, of which 3 were waited for; matrix products, arithmetic and copies ran while one was open for 0% of the time, Pallas kernels for 0%

profile of v10, /device:TPU:1, one launch (start us, length us, event | category | flops | bytes accessed | tf_op | source)
XLA Modules:
  0.0 102.0 jit_solution(10115659394396795423)
XLA Ops:
  0.6 0.0 copy-start.4
  0.6 0.0 copy-start.2
  0.6 0.0 copy-start.5
  0.7 0.7 copy-done.4
  1.3 1.6 %copy-done.2 = f32[1536,768]{1,0:T(8,128)S(1)} copy-done((f32[1536,768]{1,0:T(8,128)S(1)}, f32[1536,768]{1,0:T(8,128)}, u32[]{:S(2)}) %copy-start.2) | copy-done | bytes 4718616
  3.0 0.0 copy-done.5
  3.0 1.7 %shard_map.51 = (f32[32,1,2304]{2,1,0:T(1,128)S(1)}, f32[1,2304]{1,0:T(1,128)S(1)}, f32[1,2304]{1,0:T(1,128)S(1)}, bf16[1536,768]{1,0:T(8,128)(2,1)S(1)}, bf16[5...) custom-call(f32[3,768]{1,0:T(4,128)S(1)} %copy-done.4, f32[768]{0:T(1024)S(1)} %copy-done.5, ...), custom_call_target="tpu_custom_call" | custom-call | flops 2000000 | bytes 100000 | tf_op jit(solution)/shard_map/pallas_call | solution.py:336
  4.7 0.0 copy-start
  4.7 1.2 %copy-done = bf16[1024,768]{1,0:T(8,128)(2,1)} copy-done((bf16[1024,768]{1,0:T(8,128)(2,1)}, bf16[1024,768]{1,0:T(8,128)(2,1)S(1)}, u32[]{:S(2)}) %copy-start) | copy-done | bytes 1572888
  5.8 0.0 copy-start.3
  5.8 0.7 copy-done.3
  6.5 13.7 %all-to-all-start = ((f32[32,1,2304]{2,1,0:T(1,128)}), f32[32,1,2304]{2,1,0:T(1,128)S(1)}, u32[]{:S(2)}, u32[]{:S(2)}) async-start(f32[32,1,2304]{2,1,0:T(1,128)} %copy-done.3), calls=%async_computation | async-start | bytes 589824 | tf_op jit(solution)/shard_map/all_to_all | solution.py:357
  20.3 3.1 %collective-permute-start = (f32[3,768]{1,0:T(4,128)S(1)}, f32[3,768]{1,0:T(4,128)S(1)}, u32[]{:S(2)}, u32[]{:S(2)}) collective-permute-start(f32[3,768]{1,0:T(4,128)S(1)} %copy-done.4), channel_id=1, source_target_pairs={{0,1},{1,0},{2,3},{3,2},{4,5},{5,4},{6,7},{7,6},{8,9},{9,8},{10,11... | collective-permute-start | bytes 27656 | tf_op jit(solution)/shard_map/ppermute | solution.py:361
  23.4 8.9 %all-to-all-done.got_ref = f32[32,1,2304]{2,1,0:T(1,128)S(1)} async-done(((f32[32,1,2304]{2,1,0:T(1,128)}), f32[32,1,2304]{2,1,0:T(1,128)S(1)}, u32[]{:S(2)}, u32[]{:S(2)}) %all-to-all-start) | async-done | bytes 294944 | tf_op jit(solution)/shard_map/all_to_all | solution.py:357
  32.3 0.0 collective-permute-done.cross_ref
  32.3 0.0 copy-start.1
  32.3 1.4 %copy-done.1 = bf16[1024,768]{1,0:T(8,128)(2,1)S(1)} copy-done((bf16[1024,768]{1,0:T(8,128)(2,1)S(1)}, bf16[1024,768]{1,0:T(8,128)(2,1)}, u32[]{:S(2)}) %copy-start.1) | copy-done | bytes 1572888
  33.7 0.9 shard_map.53
  34.7 18.4 %all_to_all.25.got_ref = f32[16,1,2304]{2,1,0:T(1,128)S(1)} all-to-all(f32[16,1,2304]{2,1,0:T(1,128)S(1)} %get-tuple-element.24), channel_id=1, replica_groups=mesh['row'=16,'col'=32] {'row'}, dimensions={0} | all-to-all | bytes 294912 | tf_op jit(solution)/shard_map/all_to_all | solution.py:357
  53.1 2.8 %shard_map.55 = f32[32,1,2304]{2,1,0:T(1,128)} custom-call(f32[1,2304]{1,0:T(1,128)S(1)} %shard_map.54.z_ref.own_ref, f32[1,2304]{1,0:T(1,128)S(1)} %get-tuple-element.19.own_ref.x_ref, bf16[1536,768]{1,0:T(8,128)(2,1)S(1)} %get-tuple-element.21.high_ref, bf16[512,768]{1,0:T(8,128)(2,1)S(1)} %get-tuple-element.22.near_ref, bf16[1024,768]{1,0:T(8,128)(2,1)S(1)} %copy-done.1), custom_call_target="tpu_custom_call" | custom-call | flops 2000000 | bytes 100000 | tf_op jit(solution)/shard_map/pallas_call | solution.py:336
  55.8 3.9 %all-to-all-start.2 = ((f32[32,1,2304]{2,1,0:T(1,128)}), f32[32,1,2304]{2,1,0:T(1,128)S(1)}, u32[]{:S(2)}, u32[]{:S(2)}) async-start(f32[32,1,2304]{2,1,0:T(1,128)} %shard_map.55), calls=%async_computation.2 | async-start | bytes 589824 | tf_op jit(solution)/shard_map/all_to_all | solution.py:357
  59.8 3.1 %collective-permute-start.1 = (f32[1,2304]{1,0:T(1,128)S(1)}, f32[1,2304]{1,0:T(1,128)S(1)}, u32[]{:S(2)}, u32[]{:S(2)}) collective-permute-start(f32[1,2304]{1,0:T(1,128)S(1)} %shard_map.54.z_ref.own_ref), channel_id=1, source_target_pairs={{0,1},{1,0},{2,3},{3,2},{4,5},{5,4},{6,7},{7,6},{8,9},{9,8},{10,11... | collective-permute-start | bytes 27656 | tf_op jit(solution)/shard_map/ppermute | solution.py:383
  62.9 1.6 %collective-permute-done.1.cross_ref = f32[1,2304]{1,0:T(1,128)S(1)} collective-permute-done((f32[1,2304]{1,0:T(1,128)S(1)}, f32[1,2304]{1,0:T(1,128)S(1)}, u32[]{:S(2)}, u32[]{:S(2)}) %collective-permute-start.1) | collective-permute-done | bytes 9248 | tf_op jit(solution)/shard_map/ppermute | solution.py:383
  64.5 8.1 %all-to-all-done.2.got_ref = f32[32,1,2304]{2,1,0:T(1,128)S(1)} async-done(((f32[32,1,2304]{2,1,0:T(1,128)}), f32[32,1,2304]{2,1,0:T(1,128)S(1)}, u32[]{:S(2)}, u32[]{:S(2)}) %all-to-all-start.2) | async-done | bytes 294944 | tf_op jit(solution)/shard_map/all_to_all | solution.py:357
  72.5 2.3 %shard_map.56 = f32[16,1,2432]{2,1,0:T(1,128)S(1)} custom-call(f32[32,1,2304]{2,1,0:T(1,128)S(1)} %all-to-all-done.2.got_ref, f32[1,2304]{1,0:T(1,128)S(1)} %shard_map.54.z_ref.own_ref, f32[1,2304]{1,0:T(1,128)S(1)} %collective-permute-done.1.cross_ref, f32[8,1536]{1,0:T(8,128)S(1)} %get-tuple-element.26.x_rows, ...), custom_call_target="tpu_custom_call" | custom-call | flops 2000000 | bytes 100000 | tf_op jit(solution)/shard_map/pallas_call | solution.py:336
  74.9 13.8 %all_to_all.26.got_ref = f32[16,1,2432]{2,1,0:T(1,128)S(1)} all-to-all(f32[16,1,2432]{2,1,0:T(1,128)S(1)} %shard_map.56), channel_id=1, replica_groups=mesh['row'=16,'col'=32] {'row'}, dimensions={0} | all-to-all | bytes 311296 | tf_op jit(solution)/shard_map/all_to_all | solution.py:357
  88.7 0.4 shard_map.57
  89.1 12.1 %all_to_all.27.got_ref = f32[32,1,128]{2,1,0:T(1,128)S(1)} all-to-all(f32[32,1,128]{2,1,0:T(1,128)S(1)} %get-tuple-element.27), channel_id=1, replica_groups=mesh['row'=16,'col'=32] {'col'}, dimensions={0} | all-to-all | bytes 32768 | tf_op jit(solution)/shard_map/all_to_all | solution.py:357
  101.2 0.8 shard_map.58
  (3 shorter events, 0.1 us)
Async XLA Ops:
  0.6 0.7 copy-start.4
  0.6 2.3 %copy-start.2 = (f32[1536,768]{1,0:T(8,128)S(1)}, f32[1536,768]{1,0:T(8,128)}, u32[]{:S(2)}) copy-start(f32[1536,768]{1,0:T(8,128)} %a_ref.1) | copy-start | bytes 14155780
  0.6 2.3 %copy-start.5 = (f32[768]{0:T(1024)S(1)}, f32[768]{0:T(1024)}, u32[]{:S(2)}) copy-start(f32[768]{0:T(1024)} %d_ref.1) | copy-start | bytes 9220
  4.7 1.2 %copy-start = (bf16[1024,768]{1,0:T(8,128)(2,1)}, bf16[1024,768]{1,0:T(8,128)(2,1)S(1)}, u32[]{:S(2)}) copy-start(bf16[1024,768]{1,0:T(8,128)(2,1)S(1)} %get-tuple-element.23.far_ref.far_hbm) | copy-start | bytes 4718596
  5.8 0.7 copy-start.3
  6.5 25.7 %all-to-all-start = ((f32[32,1,2304]{2,1,0:T(1,128)}), f32[32,1,2304]{2,1,0:T(1,128)S(1)}, u32[]{:S(2)}, u32[]{:S(2)}) async-start(f32[32,1,2304]{2,1,0:T(1,128)} %copy-done.3), calls=%async_computation | async-start | bytes 589824 | tf_op jit(solution)/shard_map/all_to_all | solution.py:357
  20.3 12.1 %collective-permute-start = (f32[3,768]{1,0:T(4,128)S(1)}, f32[3,768]{1,0:T(4,128)S(1)}, u32[]{:S(2)}, u32[]{:S(2)}) collective-permute-start(f32[3,768]{1,0:T(4,128)S(1)} %copy-done.4), channel_id=1, source_target_pairs={{0,1},{1,0},{2,3},{3,2},{4,5},{5,4},{6,7},{7,6},{8,9},{9,8},{10,11... | collective-permute-start | bytes 27656 | tf_op jit(solution)/shard_map/ppermute | solution.py:361
  32.3 1.4 %copy-start.1 = (bf16[1024,768]{1,0:T(8,128)(2,1)S(1)}, bf16[1024,768]{1,0:T(8,128)(2,1)}, u32[]{:S(2)}) copy-start(bf16[1024,768]{1,0:T(8,128)(2,1)} %copy-done) | copy-start | bytes 4718596
  55.8 16.7 %all-to-all-start.2 = ((f32[32,1,2304]{2,1,0:T(1,128)}), f32[32,1,2304]{2,1,0:T(1,128)S(1)}, u32[]{:S(2)}, u32[]{:S(2)}) async-start(f32[32,1,2304]{2,1,0:T(1,128)} %shard_map.55), calls=%async_computation.2 | async-start | bytes 589824 | tf_op jit(solution)/shard_map/all_to_all | solution.py:357
  59.8 4.7 %collective-permute-start.1 = (f32[1,2304]{1,0:T(1,128)S(1)}, f32[1,2304]{1,0:T(1,128)S(1)}, u32[]{:S(2)}, u32[]{:S(2)}) collective-permute-start(f32[1,2304]{1,0:T(1,128)S(1)} %shard_map.54.z_ref.own_ref), channel_id=1, source_target_pairs={{0,1},{1,0},{2,3},{3,2},{4,5},{5,4},{6,7},{7,6},{8,9},{9,8},{10,11... | collective-permute-start | bytes 27656 | tf_op jit(solution)/shard_map/ppermute | solution.py:383

commit v11 on v10

--- a/solution.py
+++ b/solution.py
@@ -143,7 +143,7 @@
     place(row_index, forward, sent_ref)
 
 
-def forward_kernel(z_ref, x_ref, high_ref, near_ref, far_ref, sent_hbm, sent_ref, pair_ref, z_rows, forward, sems):
+def forward_kernel(z_ref, x_ref, high_ref, near_ref, far_ref, sent_ref, z_rows, forward):
     row_index = lax.axis_index("row")
     home = lax.axis_index("col") // 2 == row_index
     z = z_ref[...]
@@ -157,16 +157,9 @@
     for p in range(sent_ref.shape[0]):
         sent_ref[p, :, 0:128] = head
         sent_ref[p, :, 128:] = z[:, 128:]
-    filled = pltpu.make_async_copy(sent_ref, sent_hbm, sems.at[0])
-    filled.start()
-    for piece, low_ref in ((slice(0, CHUNK), near_ref), (slice(CHUNK, 2 * W), far_ref)):
-        wide = over_rows(parts, high_ref[piece, :]) + over_rows(parts, low_ref[...])
-        forward[:, piece] = 0.5 * folded(wide)
-    place(0, forward, pair_ref)
-    aimed = pltpu.make_async_copy(pair_ref, sent_hbm.at[pl.ds(2 * row_index, 2)], sems.at[1])
-    filled.wait()
-    aimed.start()
-    aimed.wait()
+    low = jnp.concatenate([over_rows(parts, near_ref[...]), over_rows(parts, far_ref[...])], 1)
+    forward[...] = 0.5 * folded(over_rows(parts, high_ref[...]) + low)
+    place(row_index, forward, sent_ref)
 
 
 def first_backward_kernel(got_ref, own_ref, cross_ref, total_ref, high_ref, near_ref, far_ref, sent_ref, v_rows):
@@ -373,13 +366,8 @@
     )
     got = exchanged(sent, "row")
     z = call(collect_kernel, flat, (got, d, x))
-    sent = call(
-        forward_kernel,
-        pltpu.HBM((cols, 1, FLAT), F32),
-        (z, x, high, near, far),
-        [pltpu.VMEM((cols, 1, FLAT), F32), pltpu.VMEM((2, 1, FLAT), F32), short, tall, pltpu.SemaphoreType.DMA((2,))],
-        out_specs=HBM,
-    )
+    slots = pltpu.HBM((cols, 1, FLAT), F32)
+    sent = call(forward_kernel, slots, (z, x, high, near, far), [short, tall], out_specs=pl.BlockSpec())
     cross = lax.ppermute(z, "col", swap)
     got = exchanged(sent, "col")
     sent = call(

time: 103 us -> 102 us (level)
  no operation moved by 1% of the time
where the time goes in v11:
time: 102 us; the launch traced here: 101 us
  blocking collectives  44.3 us (43%)
  starting transfers between devices  23.9 us (23%)
  waiting for transfers between devices  18.5 us (18%)
  Pallas kernels  8.43 us (8%)
  local copies, waits for them, and re-layouts  5.59 us (5%)
    all_to_all x3, blocking collectives, exchanged(): return lax.all_to_all(block, axis, 0, 0, tiled=True)  44.3 us
    all_to_all x2, starting transfers between devices, exchanged(): return lax.all_to_all(block, axis, 0, 0, tiled=True)  17.6 us
    all_to_all x2, waiting for transfers between devices, exchanged(): return lax.all_to_all(block, axis, 0, 0, tiled=True)  16.9 us
    pallas_call x9, Pallas kernels, call(): pl.pallas_call(kernel, out_shape=out, in_specs=specs or [VMEM] * len(inpu...  8.43 us
    unnamed x12, local copies, waits for them, and re-layouts  5.59 us
    ppermute x1, starting transfers between devices, shards(): cross = lax.ppermute(held, 'col', swap)  3.14 us
    ppermute x1, starting transfers between devices, shards(): cross = lax.ppermute(z, 'col', swap)  3.14 us
  transfers between devices with their start and end apart: 4, of which 3 were waited for; matrix products, arithmetic and copies ran while one was open for 0% of the time, Pallas kernels for 0%

profile of v11, /device:TPU:1, one launch (start us, length us, event | category | flops | bytes accessed | tf_op | source)
XLA Modules:
  0.0 101.4 jit_solution(15845448244319443707)
XLA Ops:
  0.6 0.0 copy-start.4
  0.6 0.0 copy-start.2
  0.6 0.0 copy-start.5
  0.7 0.7 copy-done.4
  1.3 1.6 %copy-done.2 = f32[1536,768]{1,0:T(8,128)S(1)} copy-done((f32[1536,768]{1,0:T(8,128)S(1)}, f32[1536,768]{1,0:T(8,128)}, u32[]{:S(2)}) %copy-start.2) | copy-done | bytes 4718616
  3.0 0.0 copy-done.5
  3.0 1.7 %shard_map.51 = (f32[32,1,2304]{2,1,0:T(1,128)S(1)}, f32[1,2304]{1,0:T(1,128)S(1)}, f32[1,2304]{1,0:T(1,128)S(1)}, bf16[1536,768]{1,0:T(8,128)(2,1)S(1)}, bf16[5...) custom-call(f32[3,768]{1,0:T(4,128)S(1)} %copy-done.4, f32[768]{0:T(1024)S(1)} %copy-done.5, ...), custom_call_target="tpu_custom_call" | custom-call | flops 2000000 | bytes 100000 | tf_op jit(solution)/shard_map/pallas_call | solution.py:329
  4.7 0.0 copy-start
  4.7 1.2 %copy-done = bf16[1024,768]{1,0:T(8,128)(2,1)} copy-done((bf16[1024,768]{1,0:T(8,128)(2,1)}, bf16[1024,768]{1,0:T(8,128)(2,1)S(1)}, u32[]{:S(2)}) %copy-start) | copy-done | bytes 1572888
  5.8 0.0 copy-start.3
  5.8 0.7 copy-done.3
  6.5 13.7 %all-to-all-start = ((f32[32,1,2304]{2,1,0:T(1,128)}), f32[32,1,2304]{2,1,0:T(1,128)S(1)}, u32[]{:S(2)}, u32[]{:S(2)}) async-start(f32[32,1,2304]{2,1,0:T(1,128)} %copy-done.3), calls=%async_computation | async-start | bytes 589824 | tf_op jit(solution)/shard_map/all_to_all | solution.py:350
  20.3 3.1 %collective-permute-start = (f32[3,768]{1,0:T(4,128)S(1)}, f32[3,768]{1,0:T(4,128)S(1)}, u32[]{:S(2)}, u32[]{:S(2)}) collective-permute-start(f32[3,768]{1,0:T(4,128)S(1)} %copy-done.4), channel_id=1, source_target_pairs={{0,1},{1,0},{2,3},{3,2},{4,5},{5,4},{6,7},{7,6},{8,9},{9,8},{10,11... | collective-permute-start | bytes 27656 | tf_op jit(solution)/shard_map/ppermute | solution.py:354
  23.4 8.9 %all-to-all-done.got_ref = f32[32,1,2304]{2,1,0:T(1,128)S(1)} async-done(((f32[32,1,2304]{2,1,0:T(1,128)}), f32[32,1,2304]{2,1,0:T(1,128)S(1)}, u32[]{:S(2)}, u32[]{:S(2)}) %all-to-all-start) | async-done | bytes 294944 | tf_op jit(solution)/shard_map/all_to_all | solution.py:350
  32.3 0.0 collective-permute-done.cross_ref
  32.3 0.0 copy-start.1
  32.3 1.4 %copy-done.1 = bf16[1024,768]{1,0:T(8,128)(2,1)S(1)} copy-done((bf16[1024,768]{1,0:T(8,128)(2,1)S(1)}, bf16[1024,768]{1,0:T(8,128)(2,1)}, u32[]{:S(2)}) %copy-start.1) | copy-done | bytes 1572888
  33.7 0.9 shard_map.53
  34.7 18.4 %all_to_all.25.got_ref = f32[16,1,2304]{2,1,0:T(1,128)S(1)} all-to-all(f32[16,1,2304]{2,1,0:T(1,128)S(1)} %get-tuple-element.24), channel_id=1, replica_groups=mesh['row'=16,'col'=32] {'row'}, dimensions={0} | all-to-all | bytes 294912 | tf_op jit(solution)/shard_map/all_to_all | solution.py:350
  53.1 2.2 %shard_map.55 = f32[32,1,2304]{2,1,0:T(1,128)} custom-call(f32[1,2304]{1,0:T(1,128)S(1)} %shard_map.54.z_ref.own_ref, f32[1,2304]{1,0:T(1,128)S(1)} %get-tuple-element.19.own_ref.x_ref, bf16[1536,768]{1,0:T(8,128)(2,1)S(1)} %get-tuple-element.21.high_ref, bf16[512,768]{1,0:T(8,128)(2,1)S(1)} %get-tuple-element.22.near_ref, bf16[1024,768]{1,0:T(8,128)(2,1)S(1)} %copy-done.1), custom_call_target="tpu_custom_call" | custom-call | flops 2000000 | bytes 100000 | tf_op jit(solution)/shard_map/pallas_call | solution.py:329
  55.3 3.9 %all-to-all-start.2 = ((f32[32,1,2304]{2,1,0:T(1,128)}), f32[32,1,2304]{2,1,0:T(1,128)S(1)}, u32[]{:S(2)}, u32[]{:S(2)}) async-start(f32[32,1,2304]{2,1,0:T(1,128)} %shard_map.55), calls=%async_computation.2 | async-start | bytes 589824 | tf_op jit(solution)/shard_map/all_to_all | solution.py:350
  59.2 3.1 %collective-permute-start.1 = (f32[1,2304]{1,0:T(1,128)S(1)}, f32[1,2304]{1,0:T(1,128)S(1)}, u32[]{:S(2)}, u32[]{:S(2)}) collective-permute-start(f32[1,2304]{1,0:T(1,128)S(1)} %shard_map.54.z_ref.own_ref), channel_id=1, source_target_pairs={{0,1},{1,0},{2,3},{3,2},{4,5},{5,4},{6,7},{7,6},{8,9},{9,8},{10,11... | collective-permute-start | bytes 27656 | tf_op jit(solution)/shard_map/ppermute | solution.py:371
  62.3 1.6 %collective-permute-done.1.cross_ref = f32[1,2304]{1,0:T(1,128)S(1)} collective-permute-done((f32[1,2304]{1,0:T(1,128)S(1)}, f32[1,2304]{1,0:T(1,128)S(1)}, u32[]{:S(2)}, u32[]{:S(2)}) %collective-permute-start.1) | collective-permute-done | bytes 9248 | tf_op jit(solution)/shard_map/ppermute | solution.py:371
  63.9 8.0 %all-to-all-done.2.got_ref = f32[32,1,2304]{2,1,0:T(1,128)S(1)} async-done(((f32[32,1,2304]{2,1,0:T(1,128)}), f32[32,1,2304]{2,1,0:T(1,128)S(1)}, u32[]{:S(2)}, u32[]{:S(2)}) %all-to-all-start.2) | async-done | bytes 294944 | tf_op jit(solution)/shard_map/all_to_all | solution.py:350
  71.9 2.3 %shard_map.56 = f32[16,1,2432]{2,1,0:T(1,128)S(1)} custom-call(f32[32,1,2304]{2,1,0:T(1,128)S(1)} %all-to-all-done.2.got_ref, f32[1,2304]{1,0:T(1,128)S(1)} %shard_map.54.z_ref.own_ref, f32[1,2304]{1,0:T(1,128)S(1)} %collective-permute-done.1.cross_ref, f32[8,1536]{1,0:T(8,128)S(1)} %get-tuple-element.26.x_rows, ...), custom_call_target="tpu_custom_call" | custom-call | flops 2000000 | bytes 100000 | tf_op jit(solution)/shard_map/pallas_call | solution.py:329
  74.2 13.8 %all_to_all.26.got_ref = f32[16,1,2432]{2,1,0:T(1,128)S(1)} all-to-all(f32[16,1,2432]{2,1,0:T(1,128)S(1)} %shard_map.56), channel_id=1, replica_groups=mesh['row'=16,'col'=32] {'row'}, dimensions={0} | all-to-all | bytes 311296 | tf_op jit(solution)/shard_map/all_to_all | solution.py:350
  88.1 0.4 shard_map.57
  88.5 12.1 %all_to_all.27.got_ref = f32[32,1,128]{2,1,0:T(1,128)S(1)} all-to-all(f32[32,1,128]{2,1,0:T(1,128)S(1)} %get-tuple-element.27), channel_id=1, replica_groups=mesh['row'=16,'col'=32] {'col'}, dimensions={0} | all-to-all | bytes 32768 | tf_op jit(solution)/shard_map/all_to_all | solution.py:350
  100.6 0.8 shard_map.58
  (3 shorter events, 0.1 us)
Async XLA Ops:
  0.6 0.7 copy-start.4
  0.6 2.3 %copy-start.2 = (f32[1536,768]{1,0:T(8,128)S(1)}, f32[1536,768]{1,0:T(8,128)}, u32[]{:S(2)}) copy-start(f32[1536,768]{1,0:T(8,128)} %a_ref.1) | copy-start | bytes 14155780
  0.6 2.3 %copy-start.5 = (f32[768]{0:T(1024)S(1)}, f32[768]{0:T(1024)}, u32[]{:S(2)}) copy-start(f32[768]{0:T(1024)} %d_ref.1) | copy-start | bytes 9220
  4.7 1.2 %copy-start = (bf16[1024,768]{1,0:T(8,128)(2,1)}, bf16[1024,768]{1,0:T(8,128)(2,1)S(1)}, u32[]{:S(2)}) copy-start(bf16[1024,768]{1,0:T(8,128)(2,1)S(1)} %get-tuple-element.23.far_ref.far_hbm) | copy-start | bytes 4718596
  5.8 0.7 copy-start.3
  6.5 25.7 %all-to-all-start = ((f32[32,1,2304]{2,1,0:T(1,128)}), f32[32,1,2304]{2,1,0:T(1,128)S(1)}, u32[]{:S(2)}, u32[]{:S(2)}) async-start(f32[32,1,2304]{2,1,0:T(1,128)} %copy-done.3), calls=%async_computation | async-start | bytes 589824 | tf_op jit(solution)/shard_map/all_to_all | solution.py:350
  20.3 12.1 %collective-permute-start = (f32[3,768]{1,0:T(4,128)S(1)}, f32[3,768]{1,0:T(4,128)S(1)}, u32[]{:S(2)}, u32[]{:S(2)}) collective-permute-start(f32[3,768]{1,0:T(4,128)S(1)} %copy-done.4), channel_id=1, source_target_pairs={{0,1},{1,0},{2,3},{3,2},{4,5},{5,4},{6,7},{7,6},{8,9},{9,8},{10,11... | collective-permute-start | bytes 27656 | tf_op jit(solution)/shard_map/ppermute | solution.py:354
  32.3 1.4 %copy-start.1 = (bf16[1024,768]{1,0:T(8,128)(2,1)S(1)}, bf16[1024,768]{1,0:T(8,128)(2,1)}, u32[]{:S(2)}) copy-start(bf16[1024,768]{1,0:T(8,128)(2,1)} %copy-done) | copy-start | bytes 4718596
  55.3 16.7 %all-to-all-start.2 = ((f32[32,1,2304]{2,1,0:T(1,128)}), f32[32,1,2304]{2,1,0:T(1,128)S(1)}, u32[]{:S(2)}, u32[]{:S(2)}) async-start(f32[32,1,2304]{2,1,0:T(1,128)} %shard_map.55), calls=%async_computation.2 | async-start | bytes 589824 | tf_op jit(solution)/shard_map/all_to_all | solution.py:350
  59.2 4.7 %collective-permute-start.1 = (f32[1,2304]{1,0:T(1,128)S(1)}, f32[1,2304]{1,0:T(1,128)S(1)}, u32[]{:S(2)}, u32[]{:S(2)}) collective-permute-start(f32[1,2304]{1,0:T(1,128)S(1)} %shard_map.54.z_ref.own_ref), channel_id=1, source_target_pairs={{0,1},{1,0},{2,3},{3,2},{4,5},{5,4},{6,7},{7,6},{8,9},{9,8},{10,11... | collective-permute-start | bytes 27656 | tf_op jit(solution)/shard_map/ppermute | solution.py:371

commit v12 on v9

--- a/solution.py
+++ b/solution.py
@@ -156,7 +156,11 @@
     for p in range(sent_ref.shape[0]):
         sent_ref[p, :, 0:128] = head
         sent_ref[p, :, 128:] = z[:, 128:]
-    forward[...] = 0.5 * folded(over_rows(parts, high_ref[...]) + over_rows(parts, low_ref[...]))
+    cut = 4 * W // 3
+    tall = over_rows(high_ref[cut:, :], parts) + over_rows(low_ref[cut:, :], parts)
+    wide = over_rows(parts, high_ref[0:cut, :]) + over_rows(parts, low_ref[0:cut, :])
+    forward[:, 0:cut] = 0.5 * folded(wide)
+    forward[:, cut:] = 0.5 * folded(tall.T)
     place(row_index, forward, sent_ref)
 
 

time: 103 us -> 103 us (level)
  no operation moved by 1% of the time
where the time goes in v12:
time: 103 us; the launch traced here: 102 us
  blocking collectives  44.3 us (43%)
  starting transfers between devices  23.9 us (23%)
  waiting for transfers between devices  18.5 us (18%)
  Pallas kernels  9.21 us (9%)
  local copies, waits for them, and re-layouts  5.41 us (5%)
    all_to_all x3, blocking collectives, exchanged(): return lax.all_to_all(block, axis, 0, 0, tiled=True)  44.3 us
    all_to_all x2, starting transfers between devices, exchanged(): return lax.all_to_all(block, axis, 0, 0, tiled=True)  17.6 us
    all_to_all x2, waiting for transfers between devices, exchanged(): return lax.all_to_all(block, axis, 0, 0, tiled=True)  16.9 us
    pallas_call x9, Pallas kernels, call(): pl.pallas_call(kernel, out_shape=out, in_specs=specs or [VMEM] * len(inpu...  9.21 us
    unnamed x12, local copies, waits for them, and re-layouts  5.41 us
    ppermute x1, starting transfers between devices, shards(): cross = lax.ppermute(held, 'col', swap)  3.14 us
    ppermute x1, starting transfers between devices, shards(): cross = lax.ppermute(z, 'col', swap)  3.14 us
  transfers between devices with their start and end apart: 4, of which 3 were waited for; matrix products, arithmetic and copies ran while one was open for 0% of the time, Pallas kernels for 0%

profile of v12, /device:TPU:1, one launch (start us, length us, event | category | flops | bytes accessed | tf_op | source)
XLA Modules:
  0.0 102.0 jit_solution(1107591251772088085)
XLA Ops:
  0.6 0.0 copy-start.4
  0.6 0.0 copy-start.3
  0.6 0.0 copy-start.5
  0.7 0.7 copy-done.4
  1.3 1.6 %copy-done.3 = f32[1536,768]{1,0:T(8,128)S(1)} copy-done((f32[1536,768]{1,0:T(8,128)S(1)}, f32[1536,768]{1,0:T(8,128)}, u32[]{:S(2)}) %copy-start.3) | copy-done | bytes 4718616
  3.0 0.0 copy-done.5
  3.0 2.4 %shard_map.51 = (f32[32,1,2304]{2,1,0:T(1,128)}, f32[1,2304]{1,0:T(1,128)S(1)}, f32[1,2304]{1,0:T(1,128)S(1)}, bf16[1536,768]{1,0:T(8,128)(2,1)S(1)}, bf16[1536,768]{1,0:T(8,128)(2,1)S(1)}) custom-call(f32[3,768]{1,0:T(4,128)S(1)} %copy-done.4, f32[768]{0:T(1024)S(1)} %copy-done.5, f32[1536,768]{1,0:T(8,128)S(1)} %copy-done.3, f32[8,128]{1,0:T(8,128)S(1)} %shard_map.50.mark_ref), custom_call_target="tpu_custom_call" | custom-call | flops 2000000 | bytes 100000 | tf_op jit(solution)/shard_map/pallas_call | solution.py:334
  5.4 0.0 copy-start
  5.4 1.4 %copy-done = bf16[1536,768]{1,0:T(8,128)(2,1)} copy-done((bf16[1536,768]{1,0:T(8,128)(2,1)}, bf16[1536,768]{1,0:T(8,128)(2,1)S(1)}, u32[]{:S(2)}) %copy-start) | copy-done | bytes 2359320
  6.8 13.7 %all-to-all-start = ((f32[32,1,2304]{2,1,0:T(1,128)}), f32[32,1,2304]{2,1,0:T(1,128)S(1)}, u32[]{:S(2)}, u32[]{:S(2)}) async-start(f32[32,1,2304]{2,1,0:T(1,128)} %get-tuple-element.17), calls=%async_computation | async-start | bytes 589824 | tf_op jit(solution)/shard_map/all_to_all | solution.py:355
  20.5 3.1 %collective-permute-start = (f32[3,768]{1,0:T(4,128)S(1)}, f32[3,768]{1,0:T(4,128)S(1)}, u32[]{:S(2)}, u32[]{:S(2)}) collective-permute-start(f32[3,768]{1,0:T(4,128)S(1)} %copy-done.4), channel_id=1, source_target_pairs={{0,1},{1,0},{2,3},{3,2},{4,5},{5,4},{6,7},{7,6},{8,9},{9,8},{10,11... | collective-permute-start | bytes 27656 | tf_op jit(solution)/shard_map/ppermute | solution.py:359
  23.7 8.9 %all-to-all-done.got_ref = f32[32,1,2304]{2,1,0:T(1,128)S(1)} async-done(((f32[32,1,2304]{2,1,0:T(1,128)}), f32[32,1,2304]{2,1,0:T(1,128)S(1)}, u32[]{:S(2)}, u32[]{:S(2)}) %all-to-all-start) | async-done | bytes 294944 | tf_op jit(solution)/shard_map/all_to_all | solution.py:355
  32.6 0.0 collective-permute-done.cross_ref
  32.6 0.0 copy-start.1
  32.6 1.7 %copy-done.1 = bf16[1536,768]{1,0:T(8,128)(2,1)S(1)} copy-done((bf16[1536,768]{1,0:T(8,128)(2,1)S(1)}, bf16[1536,768]{1,0:T(8,128)(2,1)}, u32[]{:S(2)}) %copy-start.1) | copy-done | bytes 2359320
  34.3 0.0 copy-start.2
  34.3 0.9 shard_map.53
  35.2 18.4 %all_to_all.25.got_ref = f32[16,1,2304]{2,1,0:T(1,128)S(1)} all-to-all(f32[16,1,2304]{2,1,0:T(1,128)S(1)} %get-tuple-element.22), channel_id=1, replica_groups=mesh['row'=16,'col'=32] {'row'}, dimensions={0} | all-to-all | bytes 294912 | tf_op jit(solution)/shard_map/all_to_all | solution.py:355
  53.6 0.0 copy-done.2
  53.6 2.1 %shard_map.55 = f32[32,1,2304]{2,1,0:T(1,128)} custom-call(f32[1,2304]{1,0:T(1,128)S(1)} %shard_map.54.z_ref.own_ref, f32[1,2304]{1,0:T(1,128)S(1)} %get-tuple-element.18.own_ref.x_ref, bf16[1536,768]{1,0:T(8,128)(2,1)S(1)} %get-tuple-element.20.high_ref, bf16[1536,768]{1,0:T(8,128)(2,1)S(1)} %copy-done.2), custom_call_target="tpu_custom_call" | custom-call | flops 2000000 | bytes 100000 | tf_op jit(solution)/shard_map/pallas_call | solution.py:334
  55.7 3.9 %all-to-all-start.2 = ((f32[32,1,2304]{2,1,0:T(1,128)}), f32[32,1,2304]{2,1,0:T(1,128)S(1)}, u32[]{:S(2)}, u32[]{:S(2)}) async-start(f32[32,1,2304]{2,1,0:T(1,128)} %shard_map.55), calls=%async_computation.2 | async-start | bytes 589824 | tf_op jit(solution)/shard_map/all_to_all | solution.py:355
  59.6 3.1 %collective-permute-start.1 = (f32[1,2304]{1,0:T(1,128)S(1)}, f32[1,2304]{1,0:T(1,128)S(1)}, u32[]{:S(2)}, u32[]{:S(2)}) collective-permute-start(f32[1,2304]{1,0:T(1,128)S(1)} %shard_map.54.z_ref.own_ref), channel_id=1, source_target_pairs={{0,1},{1,0},{2,3},{3,2},{4,5},{5,4},{6,7},{7,6},{8,9},{9,8},{10,11... | collective-permute-start | bytes 27656 | tf_op jit(solution)/shard_map/ppermute | solution.py:376
  62.8 1.6 %collective-permute-done.1.cross_ref = f32[1,2304]{1,0:T(1,128)S(1)} collective-permute-done((f32[1,2304]{1,0:T(1,128)S(1)}, f32[1,2304]{1,0:T(1,128)S(1)}, u32[]{:S(2)}, u32[]{:S(2)}) %collective-permute-start.1) | collective-permute-done | bytes 9248 | tf_op jit(solution)/shard_map/ppermute | solution.py:376
  64.3 8.0 %all-to-all-done.2.got_ref = f32[32,1,2304]{2,1,0:T(1,128)S(1)} async-done(((f32[32,1,2304]{2,1,0:T(1,128)}), f32[32,1,2304]{2,1,0:T(1,128)S(1)}, u32[]{:S(2)}, u32[]{:S(2)}) %all-to-all-start.2) | async-done | bytes 294944 | tf_op jit(solution)/shard_map/all_to_all | solution.py:355
  72.4 2.5 %shard_map.56 = f32[16,1,2432]{2,1,0:T(1,128)S(1)} custom-call(f32[32,1,2304]{2,1,0:T(1,128)S(1)} %all-to-all-done.2.got_ref, f32[1,2304]{1,0:T(1,128)S(1)} %shard_map.54.z_ref.own_ref, f32[1,2304]{1,0:T(1,128)S(1)} %collective-permute-done.1.cross_ref, f32[8,1536]{1,0:T(8,128)S(1)} %get-tuple-element.24.x_rows, ...), custom_call_target="tpu_custom_call" | custom-call | flops 2000000 | bytes 100000 | tf_op jit(solution)/shard_map/pallas_call | solution.py:334
  74.8 13.8 %all_to_all.26.got_ref = f32[16,1,2432]{2,1,0:T(1,128)S(1)} all-to-all(f32[16,1,2432]{2,1,0:T(1,128)S(1)} %shard_map.56), channel_id=1, replica_groups=mesh['row'=16,'col'=32] {'row'}, dimensions={0} | all-to-all | bytes 311296 | tf_op jit(solution)/shard_map/all_to_all | solution.py:355
  88.7 0.4 shard_map.57
  89.1 12.1 %all_to_all.27.got_ref = f32[32,1,128]{2,1,0:T(1,128)S(1)} all-to-all(f32[32,1,128]{2,1,0:T(1,128)S(1)} %get-tuple-element.25), channel_id=1, replica_groups=mesh['row'=16,'col'=32] {'col'}, dimensions={0} | all-to-all | bytes 32768 | tf_op jit(solution)/shard_map/all_to_all | solution.py:355
  101.2 0.8 shard_map.58
  (3 shorter events, 0.1 us)
Async XLA Ops:
  0.6 0.7 copy-start.4
  0.6 2.3 %copy-start.3 = (f32[1536,768]{1,0:T(8,128)S(1)}, f32[1536,768]{1,0:T(8,128)}, u32[]{:S(2)}) copy-start(f32[1536,768]{1,0:T(8,128)} %a_ref.1) | copy-start | bytes 14155780
  0.6 2.3 %copy-start.5 = (f32[768]{0:T(1024)S(1)}, f32[768]{0:T(1024)}, u32[]{:S(2)}) copy-start(f32[768]{0:T(1024)} %d_ref.1) | copy-start | bytes 9220
  5.4 1.4 %copy-start = (bf16[1536,768]{1,0:T(8,128)(2,1)}, bf16[1536,768]{1,0:T(8,128)(2,1)S(1)}, u32[]{:S(2)}) copy-start(bf16[1536,768]{1,0:T(8,128)(2,1)S(1)} %get-tuple-element.21.low_ref.low_hbm) | copy-start | bytes 7077892
  6.8 25.7 %all-to-all-start = ((f32[32,1,2304]{2,1,0:T(1,128)}), f32[32,1,2304]{2,1,0:T(1,128)S(1)}, u32[]{:S(2)}, u32[]{:S(2)}) async-start(f32[32,1,2304]{2,1,0:T(1,128)} %get-tuple-element.17), calls=%async_computation | async-start | bytes 589824 | tf_op jit(solution)/shard_map/all_to_all | solution.py:355
  20.5 12.1 %collective-permute-start = (f32[3,768]{1,0:T(4,128)S(1)}, f32[3,768]{1,0:T(4,128)S(1)}, u32[]{:S(2)}, u32[]{:S(2)}) collective-permute-start(f32[3,768]{1,0:T(4,128)S(1)} %copy-done.4), channel_id=1, source_target_pairs={{0,1},{1,0},{2,3},{3,2},{4,5},{5,4},{6,7},{7,6},{8,9},{9,8},{10,11... | collective-permute-start | bytes 27656 | tf_op jit(solution)/shard_map/ppermute | solution.py:359
  32.6 1.7 %copy-start.1 = (bf16[1536,768]{1,0:T(8,128)(2,1)S(1)}, bf16[1536,768]{1,0:T(8,128)(2,1)}, u32[]{:S(2)}) copy-start(bf16[1536,768]{1,0:T(8,128)(2,1)} %copy-done) | copy-start | bytes 7077892
  34.3 19.3 %copy-start.2 = (bf16[1536,768]{1,0:T(8,128)(2,1)S(1)}, bf16[1536,768]{1,0:T(8,128)(2,1)}, u32[]{:S(2)}) copy-start(bf16[1536,768]{1,0:T(8,128)(2,1)} %copy-done) | copy-start | bytes 7077892
  55.7 16.7 %all-to-all-start.2 = ((f32[32,1,2304]{2,1,0:T(1,128)}), f32[32,1,2304]{2,1,0:T(1,128)S(1)}, u32[]{:S(2)}, u32[]{:S(2)}) async-start(f32[32,1,2304]{2,1,0:T(1,128)} %shard_map.55), calls=%async_computation.2 | async-start | bytes 589824 | tf_op jit(solution)/shard_map/all_to_all | solution.py:355
  59.6 4.7 %collective-permute-start.1 = (f32[1,2304]{1,0:T(1,128)S(1)}, f32[1,2304]{1,0:T(1,128)S(1)}, u32[]{:S(2)}, u32[]{:S(2)}) collective-permute-start(f32[1,2304]{1,0:T(1,128)S(1)} %shard_map.54.z_ref.own_ref), channel_id=1, source_target_pairs={{0,1},{1,0},{2,3},{3,2},{4,5},{5,4},{6,7},{7,6},{8,9},{9,8},{10,11... | collective-permute-start | bytes 27656 | tf_op jit(solution)/shard_map/ppermute | solution.py:376
